TPU v7x, 32 devices: a whole 2x2x4 slice. The times are simulated.
32 devices in a mesh: dp: 2 (over core), ctx: 16 (over z, y, x).
Axes of the slice: x: 2, y: 2, z: 4, core: 2. Of those that a mesh axis runs over, the one named last changes fastest.
Arguments:
- tokens: bfloat16 [4, 1024, 2048], P('dp', 'ctx'), may hold values from -6 to 6
- segment_ids: int32 [4, 1024], P('dp'), may hold values from 0 to 7, never falling along the last dimension, each value on 1 to 512 neighbouring positions
- routes: int32 [4, 1024, 8], P('dp', 'ctx'), may hold values from 0 to 15, all different within a row
- cotangent: bfloat16 [4, 1024, 2048], P('dp', 'ctx'), may hold values from -6 to 6
- q_weight: bfloat16 [2048, 4096], P(('dp', 'ctx')), may hold values from -0.125 to 0.125
- k_weight: bfloat16 [2048, 512], P(('dp', 'ctx')), may hold values from -0.125 to 0.125
- v_weight: bfloat16 [2048, 512], P(('dp', 'ctx')), may hold values from -0.125 to 0.125
- o_weight: bfloat16 [4096, 2048], P(('dp', 'ctx')), may hold values from -0.375 to 0.375
- router_weight: bfloat16 [2048, 16], P(('dp', 'ctx')), may hold values from -0.0625 to 0.0625
- norm_gains: bfloat16 [4352], P(('dp', 'ctx')), may hold values from 0.25 to 1.75
- gate_up_weight: bfloat16 [16, 2048, 1536], P('ctx', 'dp'), may hold values from -0.125 to 0.125
- down_weight: bfloat16 [16, 768, 2048], P('ctx', None, 'dp'), may hold values from -0.875 to 0.875
Outputs:
- output: bfloat16 [4, 1024, 2048], P('dp', 'ctx')
- input_grad: bfloat16 [4, 1024, 2048], P('dp', 'ctx')
- q_weight_grad: float32 [2048, 4096], P(('dp', 'ctx'))
- k_weight_grad: float32 [2048, 512], P(('dp', 'ctx'))
- v_weight_grad: float32 [2048, 512], P(('dp', 'ctx'))
- o_weight_grad: float32 [4096, 2048], P(('dp', 'ctx'))
- router_weight_grad: float32 [2048, 16], P(('dp', 'ctx'))
- norm_gains_grad: float32 [4352], P(('dp', 'ctx'))
- gate_up_weight_grad: float32 [16, 2048, 1536], P('ctx', 'dp')
- down_weight_grad: float32 [16, 768, 2048], P('ctx', None, 'dp')
Inputs may be any that keep to these rules, and one draw needn't show every extreme that they name: `segment_ids`: Non-decreasing along each sequence; every document holds at most 512 positions, and one holds exactly that many. `routes`: each token names 8 different experts; every expert is named by some token.
All inputs are finite; a program needn't handle non-finite values.
Results may differ from a plain program's by a relative error of at most 0.019.
Values may be sent and summed in bfloat16 or wider, within the bound.
No kernel may reach another device: no remote copies, remote signals or barrier semaphores. Data moves between devices by JAX's collectives and lax.ppermute only.
A program may use at most 320 MiB of HBM per device.

v0:
```python
import jax
import jax.numpy as jnp
from jax import lax
from jax.sharding import PartitionSpec as P

H = 32
KV = 4
HD = 128
TOPK = 8


eps_norm = 1e-06
rope_base = 1000000.0
neg_big = -1e30


def rms_scale(operand):
    return lax.rsqrt(jnp.mean(operand * operand, axis=-1, keepdims=True) + eps_norm)


def norm_back(operand, scale_rows, gain_vec, upstream):
    weighted = gain_vec * upstream
    inner_mean = jnp.mean(operand * weighted, axis=-1, keepdims=True)
    return scale_rows * weighted - operand * scale_rows * scale_rows * scale_rows * inner_mean


def rope_tables(positions, head_size):
    frequency = rope_base ** (-(jnp.arange(head_size // 2, dtype=jnp.float32) * 2.0 / head_size))
    angles = positions.astype(jnp.float32)[:, None] * frequency[None, :]
    angles = jnp.concatenate([angles, angles], axis=-1)
    return (jnp.cos(angles), jnp.sin(angles))


def rotate(operand, cosine, sine_table):
    half_width = operand.shape[-1] // 2
    turned = jnp.concatenate([-operand[..., half_width:], operand[..., :half_width]], axis=-1)
    return operand * cosine + turned * sine_table


def rotate_back(upstream, cosine, sine_table):
    shifted = upstream * sine_table
    half_width = upstream.shape[-1] // 2
    return upstream * cosine + jnp.concatenate(
        [shifted[..., half_width:], -shifted[..., :half_width]], axis=-1
    )


def split_gains(gains_full, model_width):
    gains_wide = gains_full.astype(jnp.float32)
    return (
        gains_wide[:model_width],
        gains_wide[model_width : 2 * model_width],
        gains_wide[2 * model_width : 2 * model_width + HD],
        gains_wide[2 * model_width + HD :],
    )


def masked_scores(query_groups, key_all, allowed, score_scale):
    scores = (
        jnp.einsum("ckgd,lkd->kcgl", query_groups, key_all, preferred_element_type=jnp.float32)
        * score_scale
    )
    return jnp.where(allowed, scores, neg_big)


def attention_weights(q_weight, k_weight, v_weight, o_weight, router_weight, norm_gains):
    return (
        lax.all_gather(q_weight, ("dp", "ctx"), axis=0, tiled=True),
        lax.all_gather(k_weight, ("dp", "ctx"), axis=0, tiled=True),
        lax.all_gather(v_weight, ("dp", "ctx"), axis=0, tiled=True),
        lax.all_gather(o_weight, ("dp", "ctx"), axis=0, tiled=True),
        lax.all_gather(router_weight, ("dp", "ctx"), axis=0, tiled=True),
        lax.all_gather(norm_gains, ("dp", "ctx"), axis=0, tiled=True),
    )


def expert_weights(gate_up_weight, down_weight):
    return (
        lax.all_gather(gate_up_weight, "dp", axis=1, tiled=True),
        lax.all_gather(down_weight, "dp", axis=2, tiled=True),
    )


def gather_keys(k_local, v_local):
    return (
        lax.all_gather(k_local, "ctx", axis=0, tiled=True),
        lax.all_gather(v_local, "ctx", axis=0, tiled=True),
    )


def to_experts(slot_rows):
    return lax.all_to_all(slot_rows, "ctx", split_axis=0, concat_axis=1, tiled=True)


def from_experts(slot_rows):
    return lax.all_to_all(slot_rows, "ctx", split_axis=1, concat_axis=0, tiled=True)


def on_device(
    tokens,
    segment_ids,
    routes,
    cotangent,
    q_weight,
    k_weight,
    v_weight,
    o_weight,
    router_weight,
    norm_gains,
    gate_up_weight,
    down_weight,
):
    micro_count = tokens.shape[0]
    block_len = tokens.shape[1]
    model_width = tokens.shape[2]
    ctx_ranks = lax.axis_size("ctx")
    length = block_len * ctx_ranks
    local_experts = gate_up_weight.shape[0]
    experts = local_experts * ctx_ranks
    capacity = max(2, (5 * block_len * TOPK + 4 * experts - 1) // (4 * experts))
    hidden_units = down_weight.shape[1]
    groups = H // KV
    score_scale = HD ** (-0.5)
    pair_count = block_len * TOPK
    block_start = lax.axis_index("ctx") * block_len
    query_pos = block_start + jnp.arange(block_len, dtype=jnp.int32)
    causal = jnp.arange(length, dtype=jnp.int32)[None, :] <= query_pos[:, None]
    cosine, sine_table = rope_tables(query_pos, HD)
    cosine = cosine[:, None, :]
    sine_table = sine_table[:, None, :]
    expert_ids = jnp.arange(experts, dtype=jnp.int32)
    pair_ids = jnp.arange(pair_count, dtype=jnp.int32)
    zero_row = jnp.zeros((1, model_width), jnp.bfloat16)
    q_grad_sum = jnp.zeros((model_width, H * HD), jnp.float32)
    k_grad_sum = jnp.zeros((model_width, KV * HD), jnp.float32)
    v_grad_sum = jnp.zeros((model_width, KV * HD), jnp.float32)
    o_grad_sum = jnp.zeros((H * HD, model_width), jnp.float32)
    router_sum = jnp.zeros((model_width, experts), jnp.float32)
    attn_gain_sum = jnp.zeros((model_width,), jnp.float32)
    ffn_gain_sum = jnp.zeros((model_width,), jnp.float32)
    q_gain_sum = jnp.zeros((HD,), jnp.float32)
    k_gain_sum = jnp.zeros((HD,), jnp.float32)
    gate_up_sum = jnp.zeros((local_experts, model_width, 2 * hidden_units), jnp.float32)
    down_sum = jnp.zeros((local_experts, hidden_units, model_width), jnp.float32)
    outputs = []
    input_grads = []
    for micro_index in range(micro_count):
        attn_set = attention_weights(
            q_weight, k_weight, v_weight, o_weight, router_weight, norm_gains
        )
        expert_set = expert_weights(gate_up_weight, down_weight)
        q_full, k_full, v_full, o_full, router_full, gains_full = attn_set
        gate_up_full, down_full = expert_set
        attn_gain, ffn_gain, q_gain, k_gain = split_gains(gains_full, model_width)
        inputs = tokens[micro_index].astype(jnp.float32)
        first_scale = rms_scale(inputs)
        normed = (inputs * first_scale * attn_gain).astype(jnp.bfloat16)
        q_proj = jnp.dot(normed, q_full, preferred_element_type=jnp.float32).reshape(
            block_len, H, HD
        )
        k_proj = jnp.dot(normed, k_full, preferred_element_type=jnp.float32).reshape(
            block_len, KV, HD
        )
        v_local = jnp.dot(normed, v_full, preferred_element_type=jnp.float32).astype(jnp.bfloat16)
        q_scale = rms_scale(q_proj)
        k_scale = rms_scale(k_proj)
        query_groups = (
            rotate(q_proj * q_scale * q_gain, cosine, sine_table)
            .astype(jnp.bfloat16)
            .reshape(block_len, KV, groups, HD)
        )
        k_local = (
            rotate(k_proj * k_scale * k_gain, cosine, sine_table)
            .astype(jnp.bfloat16)
            .reshape(block_len, KV * HD)
        )
        key_all, value_all = gather_keys(k_local, v_local)
        key_all = key_all.reshape(length, KV, HD)
        value_all = value_all.reshape(length, KV, HD)
        segments = segment_ids[micro_index]
        query_seg = lax.dynamic_slice_in_dim(segments, block_start, block_len)
        allowed = (causal & (segments[None, :] == query_seg[:, None]))[None, :, None, :]
        scores = masked_scores(query_groups, key_all, allowed, score_scale)
        row_top = jnp.max(scores, axis=-1, keepdims=True)
        exp_terms = jnp.exp(scores - row_top)
        row_total = jnp.sum(exp_terms, axis=-1, keepdims=True)
        log_total = row_top + jnp.log(row_total)
        prob_low = (exp_terms / row_total).astype(jnp.bfloat16)
        attended = jnp.einsum(
            "kcgl,lkd->ckgd", prob_low, value_all, preferred_element_type=jnp.float32
        )
        attended = attended.reshape(block_len, H * HD).astype(jnp.bfloat16)
        middle = inputs + jnp.dot(attended, o_full, preferred_element_type=jnp.float32)
        second_scale = rms_scale(middle)
        hidden = (middle * second_scale * ffn_gain).astype(jnp.bfloat16)
        logits = jnp.dot(hidden, router_full, preferred_element_type=jnp.float32)
        token_routes = routes[micro_index]
        route_hit = token_routes[:, :, None] == expert_ids[None, None, :]
        chosen = jnp.sum(jnp.where(route_hit, logits[:, None, :], 0.0), axis=-1)
        gate_weights = jax.nn.softmax(chosen, axis=-1)
        pair_hit = route_hit.reshape(pair_count, experts).astype(jnp.int32)
        earlier = jnp.cumsum(pair_hit, axis=0) - pair_hit
        slot_index = jnp.sum(earlier * pair_hit, axis=-1)
        kept_pair = slot_index < capacity
        target_row = jnp.where(
            kept_pair, token_routes.reshape(-1) * capacity + slot_index, experts * capacity
        )
        slot_pair = (
            jnp.full((experts * capacity,), pair_count, jnp.int32)
            .at[target_row]
            .set(pair_ids, mode="drop")
        )
        source_row = jnp.where(slot_pair < pair_count, slot_pair // TOPK, block_len)
        padded_hidden = jnp.concatenate([hidden, zero_row], axis=0)
        send_rows = padded_hidden[source_row].reshape(experts, capacity, model_width)
        received = to_experts(send_rows)
        gate_up = jnp.einsum(
            "erd,edf->erf", received, gate_up_full, preferred_element_type=jnp.float32
        )
        gate_part = gate_up[..., :hidden_units]
        up_part = gate_up[..., hidden_units:]
        activated = (jax.nn.silu(gate_part) * up_part).astype(jnp.bfloat16)
        expert_out = jnp.einsum(
            "erf,efd->erd", activated, down_full, preferred_element_type=jnp.float32
        ).astype(jnp.bfloat16)
        returned = from_experts(expert_out).reshape(experts * capacity, model_width)
        padded_out = jnp.concatenate([returned, zero_row], axis=0)
        pair_out = padded_out[target_row].reshape(block_len, TOPK, model_width).astype(jnp.float32)
        kept_weight = kept_pair.reshape(block_len, TOPK).astype(jnp.float32)
        pair_weight = gate_weights * kept_weight
        result = middle + jnp.sum(pair_weight[:, :, None] * pair_out, axis=1)
        outputs.append(result.astype(jnp.bfloat16))
        q_full, k_full, v_full, o_full, router_full, gains_full = attention_weights(
            q_weight, k_weight, v_weight, o_weight, router_weight, norm_gains
        )
        gate_up_full, down_full = expert_weights(gate_up_weight, down_weight)
        attn_gain, ffn_gain, q_gain, k_gain = split_gains(gains_full, model_width)
        upstream = cotangent[micro_index].astype(jnp.float32)
        pair_grad = (pair_weight[:, :, None] * upstream[:, None, :]).reshape(
            pair_count, model_width
        )
        padded_grad = jnp.concatenate([pair_grad, jnp.zeros((1, model_width), jnp.float32)], axis=0)
        slot_grad = (
            padded_grad[slot_pair].astype(jnp.bfloat16).reshape(experts, capacity, model_width)
        )
        gate_grad = jnp.sum(upstream[:, None, :] * pair_out, axis=-1) * kept_weight
        chosen_grad = gate_weights * (
            gate_grad - jnp.sum(gate_weights * gate_grad, axis=-1, keepdims=True)
        )
        logit_grad = jnp.sum(jnp.where(route_hit, chosen_grad[:, :, None], 0.0), axis=1).astype(
            jnp.bfloat16
        )
        out_grad = to_experts(slot_grad)
        act_grad = jnp.einsum(
            "erd,efd->erf", out_grad, down_full, preferred_element_type=jnp.float32
        )
        down_sum = down_sum + jnp.einsum(
            "erf,erd->efd", activated, out_grad, preferred_element_type=jnp.float32
        )
        sigmoid_gate = jax.nn.sigmoid(gate_part)
        gate_back = act_grad * up_part * sigmoid_gate * (1.0 + gate_part * (1.0 - sigmoid_gate))
        up_back = act_grad * gate_part * sigmoid_gate
        gu_grad = jnp.concatenate([gate_back, up_back], axis=-1).astype(jnp.bfloat16)
        gate_up_sum = gate_up_sum + jnp.einsum(
            "erd,erf->edf", received, gu_grad, preferred_element_type=jnp.float32
        )
        row_grad = jnp.einsum(
            "erf,edf->erd", gu_grad, gate_up_full, preferred_element_type=jnp.float32
        ).astype(jnp.bfloat16)
        back_rows = from_experts(row_grad).reshape(experts * capacity, model_width)
        padded_back = jnp.concatenate([back_rows, zero_row], axis=0)
        hidden_grad = jnp.sum(
            padded_back[target_row].reshape(block_len, TOPK, model_width).astype(jnp.float32),
            axis=1,
        )
        hidden_grad = hidden_grad + jnp.dot(
            logit_grad, router_full.T, preferred_element_type=jnp.float32
        )
        router_sum = router_sum + jnp.dot(hidden.T, logit_grad, preferred_element_type=jnp.float32)
        ffn_gain_sum = ffn_gain_sum + jnp.sum(hidden_grad * middle * second_scale, axis=0)
        middle_grad = upstream + norm_back(middle, second_scale, ffn_gain, hidden_grad)
        middle_low = middle_grad.astype(jnp.bfloat16)
        o_grad_sum = o_grad_sum + jnp.dot(
            attended.T, middle_low, preferred_element_type=jnp.float32
        )
        attended_grad = jnp.dot(middle_low, o_full.T, preferred_element_type=jnp.float32).astype(
            jnp.bfloat16
        )
        attended_grad = attended_grad.reshape(block_len, KV, groups, HD)
        prob_full = jnp.exp(masked_scores(query_groups, key_all, allowed, score_scale) - log_total)
        prob_grad = jnp.einsum(
            "ckgd,lkd->kcgl", attended_grad, value_all, preferred_element_type=jnp.float32
        )
        inner_sum = jnp.sum(prob_full * prob_grad, axis=-1, keepdims=True)
        score_grad = (prob_full * (prob_grad - inner_sum)).astype(jnp.bfloat16)
        value_part = jnp.einsum(
            "kcgl,ckgd->lkd",
            prob_full.astype(jnp.bfloat16),
            attended_grad,
            preferred_element_type=jnp.float32,
        )
        key_part = (
            jnp.einsum(
                "kcgl,ckgd->lkd", score_grad, query_groups, preferred_element_type=jnp.float32
            )
            * score_scale
        )
        query_grad = (
            jnp.einsum("kcgl,lkd->ckgd", score_grad, key_all, preferred_element_type=jnp.float32)
            * score_scale
        )
        key_sum, value_sum = (
            lax.psum_scatter(
                key_part.reshape(length, KV * HD).astype(jnp.bfloat16),
                "ctx",
                scatter_dimension=0,
                tiled=True,
            ).astype(jnp.float32),
            lax.psum_scatter(
                value_part.reshape(length, KV * HD).astype(jnp.bfloat16),
                "ctx",
                scatter_dimension=0,
                tiled=True,
            ).astype(jnp.float32),
        )
        key_rot_grad = rotate_back(key_sum.reshape(block_len, KV, HD), cosine, sine_table)
        k_gain_sum = k_gain_sum + jnp.sum(key_rot_grad * k_proj * k_scale, axis=(0, 1))
        k_low = (
            norm_back(k_proj, k_scale, k_gain, key_rot_grad)
            .reshape(block_len, KV * HD)
            .astype(jnp.bfloat16)
        )
        query_rot_grad = rotate_back(query_grad.reshape(block_len, H, HD), cosine, sine_table)
        q_gain_sum = q_gain_sum + jnp.sum(query_rot_grad * q_proj * q_scale, axis=(0, 1))
        q_low = (
            norm_back(q_proj, q_scale, q_gain, query_rot_grad)
            .reshape(block_len, H * HD)
            .astype(jnp.bfloat16)
        )
        v_low = value_sum.astype(jnp.bfloat16)
        q_grad_sum = q_grad_sum + jnp.dot(normed.T, q_low, preferred_element_type=jnp.float32)
        k_grad_sum = k_grad_sum + jnp.dot(normed.T, k_low, preferred_element_type=jnp.float32)
        v_grad_sum = v_grad_sum + jnp.dot(normed.T, v_low, preferred_element_type=jnp.float32)
        normed_grad = jnp.dot(q_low, q_full.T, preferred_element_type=jnp.float32)
        normed_grad = normed_grad + jnp.dot(k_low, k_full.T, preferred_element_type=jnp.float32)
        normed_grad = normed_grad + jnp.dot(v_low, v_full.T, preferred_element_type=jnp.float32)
        attn_gain_sum = attn_gain_sum + jnp.sum(normed_grad * inputs * first_scale, axis=0)
        input_grad = middle_grad + norm_back(inputs, first_scale, attn_gain, normed_grad)
        input_grads.append(input_grad.astype(jnp.bfloat16))
    gains_sum = jnp.concatenate([attn_gain_sum, ffn_gain_sum, q_gain_sum, k_gain_sum])
    q_share, k_share, v_share, o_share, router_share, gains_share = (
        lax.psum_scatter(q_grad_sum, ("dp", "ctx"), scatter_dimension=0, tiled=True),
        lax.psum_scatter(k_grad_sum, ("dp", "ctx"), scatter_dimension=0, tiled=True),
        lax.psum_scatter(v_grad_sum, ("dp", "ctx"), scatter_dimension=0, tiled=True),
        lax.psum_scatter(o_grad_sum, ("dp", "ctx"), scatter_dimension=0, tiled=True),
        lax.psum_scatter(router_sum, ("dp", "ctx"), scatter_dimension=0, tiled=True),
        lax.psum_scatter(gains_sum, ("dp", "ctx"), scatter_dimension=0, tiled=True),
    )
    gate_up_share, down_share = (
        lax.psum_scatter(
            gate_up_sum.astype(jnp.bfloat16), "dp", scatter_dimension=1, tiled=True
        ).astype(jnp.float32),
        lax.psum_scatter(
            down_sum.astype(jnp.bfloat16), "dp", scatter_dimension=2, tiled=True
        ).astype(jnp.float32),
    )
    return (
        jnp.stack(outputs),
        jnp.stack(input_grads),
        q_share,
        k_share,
        v_share,
        o_share,
        router_share,
        gains_share,
        gate_up_share,
        down_share,
    )


def solution(mesh):
    placed = (
        P("dp", "ctx", None),
        P("dp", None),
        P("dp", "ctx", None),
        P("dp", "ctx", None),
        P(("dp", "ctx"), None),
        P(("dp", "ctx"), None),
        P(("dp", "ctx"), None),
        P(("dp", "ctx"), None),
        P(("dp", "ctx"), None),
        P(("dp", "ctx")),
        P("ctx", "dp", None),
        P("ctx", None, "dp"),
    )
    return jax.shard_map(
        on_device,
        mesh=mesh,
        in_specs=placed,
        out_specs=(
            P("dp", "ctx", None),
            P("dp", "ctx", None),
            P(("dp", "ctx"), None),
            P(("dp", "ctx"), None),
            P(("dp", "ctx"), None),
            P(("dp", "ctx"), None),
            P(("dp", "ctx"), None),
            P(("dp", "ctx")),
            P("ctx", "dp", None),
            P("ctx", None, "dp"),
        ),
        check_vma=False,
    )
```

profile of v0, /device:TPU:1, one launch (start us, length us, event | category | flops | bytes accessed | tf_op | source)
XLA Modules:
  0.0 3535.6 jit_solution(3470368454868702518)
XLA Ops:
  10.4 41.2 %all-reduce.8 = bf16[4352]{0:T(1024)(128)(2,1)S(1)} all-reduce(bf16[4352]{0:T(1024)(128)(2,1)S(1)} %dynamic-update-slice), channel_id=1, replica_groups=mesh['dp'=2,'ctx'=16] {'dp','ctx'}, use_global_device_ids=true, to_apply=%add.8 | all-reduce | flops 4352 | bytes 17408
  53.3 17.2 all-gather.18.cloned.1.call-done
  77.3 51.0 %all-gather.12.cloned.1.call-done = bf16[2048,512]{1,0:T(8,128)(2,1)} async-done(((bf16[64,512]{1,0:T(8,128)(2,1)}), bf16[2048,512]{1,0:T(8,128)(2,1)}) %all-gather.12.cloned.1.call-update) | async-done | bytes 2097168 | tf_op jit(solution)/shard_map/all_gather | solution.py:70
  138.2 45.1 %all-gather.20.cloned.1.call-done = bf16[1024,512]{1,0:T(8,128)(2,1)} async-done(((bf16[64,512]{1,0:T(8,128)(2,1)}), bf16[1024,512]{1,0:T(8,128)(2,1)}) %all-gather.20.cloned.1.call-update) | async-done | bytes 1048592 | tf_op jit(solution)/shard_map/all_gather | solution.py:86
  185.6 54.9 %all-gather.14.cloned.1.call-done = bf16[1024,512]{1,0:T(8,128)(2,1)} async-done(((bf16[64,512]{1,0:T(8,128)(2,1)}), bf16[1024,512]{1,0:T(8,128)(2,1)}) %all-gather.14.cloned.1.call-update) | async-done | bytes 1048592 | tf_op jit(solution)/shard_map/all_gather | solution.py:87
  242.6 116.3 %all-gather.16.cloned.1.call-done = bf16[2048,4096]{1,0:T(8,128)(2,1)} async-done(((bf16[64,4096]{1,0:T(8,128)(2,1)}), bf16[2048,4096]{1,0:T(8,128)(2,1)}) %all-gather.16.cloned.1.call-update) | async-done | bytes 16777232 | tf_op jit(solution)/shard_map/all_gather | solution.py:68
  358.9 22.5 copy.268
  417.3 57.0 %all-gather.22.cloned.1.call-done = bf16[4096,2048]{1,0:T(8,128)(2,1)} async-done(((bf16[128,2048]{1,0:T(8,128)(2,1)}), bf16[4096,2048]{1,0:T(8,128)(2,1)}) %all-gather.22.cloned.1.call-update) | async-done | bytes 16777232 | tf_op jit(solution)/shard_map/all_gather | solution.py:71
  492.7 111.4 %all-gather = bf16[32,64,16]{1,2,0:T(8,128)(2,1)S(1)} all-gather(bf16[1,64,16]{1,2,0:T(8,128)(2,1)S(1)} %bitcast.607), channel_id=1, replica_groups=mesh['dp'=2,'ctx'=16] {'dp','ctx'}, dimensions={0}, use_global_device_ids=true | all-gather | bytes 67584 | tf_op jit(solution)/shard_map/all_gather | solution.py:72
  631.3 34.5 all-to-all-done.4
  689.0 17.5 reduce.12
  747.6 17.5 reduce.13
  780.3 14.3 all-to-all-start.1
  794.6 21.5 all-gather.30.cloned.1.call-done
  817.6 65.3 %all-gather.28.cloned.1.call-done = bf16[1024,512]{1,0:T(8,128)(2,1)} async-done(((bf16[64,512]{1,0:T(8,128)(2,1)}), bf16[1024,512]{1,0:T(8,128)(2,1)}) %all-gather.28.cloned.1.call-update) | async-done | bytes 1048592 | tf_op jit(solution)/shard_map/all_gather | solution.py:87
  972.3 45.5 %all-to-all-done.2 = bf16[16,40,2048]{2,1,0:T(8,128)(2,1)} async-done(((bf16[16,40,2048]{2,1,0:T(8,128)(2,1)}), bf16[16,40,2048]{2,1,0:T(8,128)(2,1)}, u32[]{:S(2)}, u32[]{:S(2)}) %all-to-all-start.2) | async-done | bytes 2621472 | tf_op jit(solution)/shard_map/all_to_all | solution.py:92
  1040.5 40.9 %all-to-all-done.6 = bf16[16,40,2048]{2,1,0:T(8,128)(2,1)S(1)} async-done(((bf16[16,40,2048]{2,1,0:T(8,128)(2,1)}), bf16[16,40,2048]{2,1,0:T(8,128)(2,1)S(1)}, u32[]{:S(2)}, u32[]{:S(2)}) %all-to-all-start.6) | async-done | bytes 2621472 | tf_op jit(solution)/shard_map/all_to_all | solution.py:92
  1104.3 16.2 reduce.14
  1148.5 16.0 reduce.15
  1168.9 19.6 all-to-all-done.7
  1225.4 26.7 all-to-all-done.3
  1404.9 67.6 %reduce-scatter.18.cloned.1.call-done = bf16[64,512]{1,0:T(8,128)(2,1)} async-done(((bf16[1024,512]{1,0:T(8,128)(2,1)}), bf16[64,512]{1,0:T(8,128)(2,1)}) %reduce-scatter.18.cloned.1.call-update) | async-done | bytes 65552 | tf_op jit(solution)/shard_map/reduce_scatter | solution.py:313
  1478.9 70.9 %reduce-scatter.34.cloned.1.call-done = bf16[64,512]{1,0:T(8,128)(2,1)} async-done(((bf16[1024,512]{1,0:T(8,128)(2,1)}), bf16[64,512]{1,0:T(8,128)(2,1)}) %reduce-scatter.34.cloned.1.call-update) | async-done | bytes 65552
  1553.4 73.5 %reduce-scatter.36.cloned.1.call-done = bf16[64,512]{1,0:T(8,128)(2,1)} async-done(((bf16[1024,512]{1,0:T(8,128)(2,1)}), bf16[64,512]{1,0:T(8,128)(2,1)}) %reduce-scatter.36.cloned.1.call-update) | async-done | bytes 65552
  1662.9 24.9 convolution_add_fusion
  1702.0 24.9 convolution_add_fusion.1
  1752.5 24.4 reduce-scatter.38.cloned.1.call-done
  1795.0 40.5 %all-reduce.9 = f32[4352]{0:T(1024)S(1)} all-reduce(f32[4352]{0:T(1024)S(1)} %pad_maximum_fusion.9), channel_id=11, replica_groups=mesh['dp'=2,'ctx'=16] {'dp','ctx'}, use_global_device_ids=true, to_apply=%region_63.64.clone | all-reduce | flops 4352 | bytes 34816
  1844.2 114.4 %reduce-scatter.24.cloned.1.call-done = f32[64,512]{1,0:T(8,128)} async-done(((f32[2048,512]{1,0:T(8,128)}), f32[64,512]{1,0:T(8,128)}) %reduce-scatter.24.cloned.1.call-update) | async-done | bytes 131088 | tf_op jit(solution)/shard_map/reduce_scatter | solution.py:353
  1958.6 150.2 %reduce-scatter.26.cloned.1.call-done = f32[64,512]{1,0:T(8,128)} async-done(((f32[2048,512]{1,0:T(8,128)}), f32[64,512]{1,0:T(8,128)}) %reduce-scatter.26.cloned.1.call-update) | async-done | bytes 131088 | tf_op jit(solution)/shard_map/reduce_scatter | solution.py:354
  2108.8 705.0 %reduce-scatter.22.cloned.1.call-done = f32[64,4096]{1,0:T(8,128)} async-done(((f32[2048,4096]{1,0:T(8,128)}), f32[64,4096]{1,0:T(8,128)}) %reduce-scatter.22.cloned.1.call-update) | async-done | bytes 1048592 | tf_op jit(solution)/shard_map/reduce_scatter | solution.py:352
  2813.8 714.5 %reduce-scatter.28.cloned.1.call-done = f32[128,2048]{1,0:T(8,128)} async-done(((f32[4096,2048]{1,0:T(8,128)}), f32[128,2048]{1,0:T(8,128)}) %reduce-scatter.28.cloned.1.call-update) | async-done | bytes 1048592 | tf_op jit(solution)/shard_map/reduce_scatter | solution.py:355
  (514 shorter events, 654.9 us)
Async XLA Ops:
  8.0 62.5 %all-gather.18.cloned.1.call-start = ((), (), s32[]{:S(2)}) async-start(), calls=%async_computation.22 | async-start | bytes 2162688 | tf_op jit(solution)/shard_map/all_gather | solution.py:69
  8.8 119.6 %all-gather.12.cloned.1.call-start = ((), (), s32[]{:S(2)}) async-start(), calls=%async_computation.19 | async-start | bytes 2162688 | tf_op jit(solution)/shard_map/all_gather | solution.py:70
  9.5 173.8 %all-gather.20.cloned.1.call-start = ((), (), s32[]{:S(2)}) async-start(), calls=%async_computation.23 | async-start | bytes 1114112 | tf_op jit(solution)/shard_map/all_gather | solution.py:86
  53.2 674.4 %copy-start.74 = (f32[64]{0:T(128)}, f32[64]{0:T(128)S(1)}, u32[]{:S(2)}) copy-start(f32[64]{0:T(128)S(1)} %add_rsqrt_fusion.5) | copy-start | bytes 772
  53.3 674.4 %copy-start.38 = (f32[2048]{0:T(1024)}, f32[2048]{0:T(1024)S(1)}, u32[]{:S(2)}) copy-start(f32[2048]{0:T(1024)S(1)} %get-tuple-element.94) | copy-start | bytes 24580
  77.3 163.2 %all-gather.14.cloned.1.call-start = ((), (), s32[]{:S(2)}) async-start(), calls=%async_computation.20 | async-start | bytes 1114112 | tf_op jit(solution)/shard_map/all_gather | solution.py:87
  131.2 227.7 %all-gather.16.cloned.1.call-start = ((), (), s32[]{:S(2)}) async-start(), calls=%async_computation.21 | async-start | bytes 17301504 | tf_op jit(solution)/shard_map/all_gather | solution.py:68
  131.7 342.6 %all-gather.22.cloned.1.call-start = ((), (), s32[]{:S(2)}) async-start(), calls=%async_computation.24 | async-start | bytes 17301504 | tf_op jit(solution)/shard_map/all_gather | solution.py:71
  138.2 752.3 %copy-start.55 = (pred[64,1024]{1,0:T(8,128)(4,1)}, pred[64,1024]{1,0:T(8,128)(4,1)S(1)}, u32[]{:S(2)}) copy-start(pred[64,1024]{1,0:T(8,128)(4,1)S(1)} %get-tuple-element.117) | copy-start | bytes 196612
  487.5 123.2 %all-to-all-start = ((bf16[16,40,2048]{2,1,0:T(8,128)(2,1)}), bf16[16,40,2048]{2,1,0:T(8,128)(2,1)}, u32[]{:S(2)}, u32[]{:S(2)}) async-start(bf16[16,40,2048]{2,1,0:T(8,128)(2,1)} %bitcast.562), calls=%async_computation | async-start | bytes 5242880 | tf_op jit(solution)/shard_map/all_to_all | solution.py:92
  492.1 123.7 %all-gather.24.cloned.1.call-start = ((), (), s32[]{:S(2)}) async-start(), calls=%async_computation.25 | async-start | bytes 9437184 | tf_op jit(solution)/shard_map/all_gather | solution.py:79
  610.7 55.1 %all-to-all-start.4 = ((bf16[16,40,2048]{2,1,0:T(8,128)(2,1)}), bf16[16,40,2048]{2,1,0:T(8,128)(2,1)}, u32[]{:S(2)}, u32[]{:S(2)}) async-start(bf16[16,40,2048]{2,1,0:T(8,128)(2,1)} %bitcast.563), calls=%async_computation.4 | async-start | bytes 5242880 | tf_op jit(solution)/shard_map/all_to_all | solution.py:92
  615.2 16.1 all-gather.26.cloned.1.call-start
  713.9 66.4 %all-to-all-start.5 = ((bf16[16,2,40960]{2,1,0:T(2,128)(2,1)}), bf16[16,2,40960]{2,1,0:T(2,128)(2,1)}, u32[]{:S(2)}, u32[]{:S(2)}) async-start(bf16[16,2,40960]{2,1,0:T(2,128)(2,1)} %reshape.1207), calls=%async_computation.5 | async-start | bytes 5242880 | tf_op jit(solution)/shard_map/all_to_all | solution.py:96
  726.9 89.2 %all-gather.30.cloned.1.call-start = ((), (), s32[]{:S(2)}) async-start(), calls=%async_computation.28 | async-start | bytes 1114112 | tf_op jit(solution)/shard_map/all_gather | solution.py:86
  727.6 155.3 %all-gather.28.cloned.1.call-start = ((), (), s32[]{:S(2)}) async-start(), calls=%async_computation.27 | async-start | bytes 1114112 | tf_op jit(solution)/shard_map/all_gather | solution.py:87
  780.3 152.1 %all-to-all-start.1 = ((bf16[16,2,40960]{2,1,0:T(2,128)(2,1)}), bf16[16,2,40960]{2,1,0:T(2,128)(2,1)}, u32[]{:S(2)}, u32[]{:S(2)}) async-start(bf16[16,2,40960]{2,1,0:T(2,128)(2,1)} %reshape.1203), calls=%async_computation.1 | async-start | bytes 5242880 | tf_op jit(solution)/shard_map/all_to_all | solution.py:96
  962.6 55.3 %all-to-all-start.2 = ((bf16[16,40,2048]{2,1,0:T(8,128)(2,1)}), bf16[16,40,2048]{2,1,0:T(8,128)(2,1)}, u32[]{:S(2)}, u32[]{:S(2)}) async-start(bf16[16,40,2048]{2,1,0:T(8,128)(2,1)} %bitcast.43), calls=%async_computation.2 | async-start | bytes 5242880 | tf_op jit(solution)/shard_map/all_to_all | solution.py:92
  1017.8 63.6 %all-to-all-start.6 = ((bf16[16,40,2048]{2,1,0:T(8,128)(2,1)}), bf16[16,40,2048]{2,1,0:T(8,128)(2,1)S(1)}, u32[]{:S(2)}, u32[]{:S(2)}) async-start(bf16[16,40,2048]{2,1,0:T(8,128)(2,1)} %bitcast.564), calls=%async_computation.7 | async-start | bytes 5242880 | tf_op jit(solution)/shard_map/all_to_all | solution.py:92
  1124.9 63.6 %all-to-all-start.7 = ((bf16[16,2,40960]{2,1,0:T(2,128)(2,1)}), bf16[16,2,40960]{2,1,0:T(2,128)(2,1)}, u32[]{:S(2)}, u32[]{:S(2)}) async-start(bf16[16,2,40960]{2,1,0:T(2,128)(2,1)} %reshape.1205), calls=%async_computation.8 | async-start | bytes 5242880 | tf_op jit(solution)/shard_map/all_to_all | solution.py:96
  1188.6 63.5 %all-to-all-start.3 = ((bf16[16,2,40960]{2,1,0:T(2,128)(2,1)}), bf16[16,2,40960]{2,1,0:T(2,128)(2,1)}, u32[]{:S(2)}, u32[]{:S(2)}) async-start(bf16[16,2,40960]{2,1,0:T(2,128)(2,1)} %reshape.1201), calls=%async_computation.3 | async-start | bytes 5242880 | tf_op jit(solution)/shard_map/all_to_all | solution.py:96
  1201.3 203.6 %reduce-scatter.20.cloned.1.call-start = ((), (), s32[]{:S(2)}) async-start(), calls=%async_computation.30 | async-start | bytes 1114112 | tf_op jit(solution)/shard_map/reduce_scatter | solution.py:313
  1318.6 153.9 %reduce-scatter.18.cloned.1.call-start = ((), (), s32[]{:S(2)}) async-start(), calls=%async_computation.29 | async-start | bytes 1114112 | tf_op jit(solution)/shard_map/reduce_scatter | solution.py:313
  1357.4 192.3 %reduce-scatter.34.cloned.1.call-start = ((), (), s32[]{:S(2)}) async-start(), calls=%async_computation.37 | async-start | bytes 1114112
  1363.8 263.1 %reduce-scatter.36.cloned.1.call-start = ((), (), s32[]{:S(2)}) async-start(), calls=%async_computation.38 | async-start | bytes 1114112
  1370.2 406.7 %reduce-scatter.38.cloned.1.call-start = ((), (), s32[]{:S(2)}) async-start(), calls=%async_computation.39 | async-start | bytes 1081344
  1379.3 407.9 %reduce-scatter.32.cloned.1.call-start = ((), (), s32[]{:S(2)}) async-start(), calls=%async_computation.36 | async-start | bytes 4718592 | tf_op jit(solution)/shard_map/reduce_scatter | solution.py:363
  1387.6 451.1 %reduce-scatter.30.cloned.1.call-start = ((), (), s32[]{:S(2)}) async-start(), calls=%async_computation.35 | async-start | bytes 9437184 | tf_op jit(solution)/shard_map/reduce_scatter | solution.py:360
  1404.8 553.7 %reduce-scatter.24.cloned.1.call-start = ((), (), s32[]{:S(2)}) async-start(), calls=%async_computation.32 | async-start | bytes 4325376 | tf_op jit(solution)/shard_map/reduce_scatter | solution.py:353
  1478.8 630.0 %reduce-scatter.26.cloned.1.call-start = ((), (), s32[]{:S(2)}) async-start(), calls=%async_computation.33 | async-start | bytes 4325376 | tf_op jit(solution)/shard_map/reduce_scatter | solution.py:354
  1631.9 1181.9 %reduce-scatter.22.cloned.1.call-start = ((), (), s32[]{:S(2)}) async-start(), calls=%async_computation.31 | async-start | bytes 34603008 | tf_op jit(solution)/shard_map/reduce_scatter | solution.py:352
  1687.8 1840.4 %reduce-scatter.28.cloned.1.call-start = ((), (), s32[]{:S(2)}) async-start(), calls=%async_computation.34 | async-start | bytes 34603008 | tf_op jit(solution)/shard_map/reduce_scatter | solution.py:355
  (103 other events, 5105.1 us)
Sparse Core Ops, SparseCore 0:
  11.7 58.7 all-gather.17
  73.3 54.9 all-gather.11
  131.7 51.5 all-gather.19
  186.5 53.9 all-gather.13
  243.3 115.5 all-gather.15
  361.7 112.5 all-gather.21
  731.0 85.0 all-gather.29
  819.4 63.4 all-gather.27
  1318.8 75.3 reduce-scatter.19
  1396.9 75.6 reduce-scatter.17
  1474.8 74.8 reduce-scatter.33
  1551.8 75.0 reduce-scatter.35
  1629.1 147.6 reduce-scatter.37
  1779.5 7.6 reduce-scatter.31
  1790.0 16.0 reduce-scatter.29
  1808.8 149.7 reduce-scatter.23
  1961.3 147.4 reduce-scatter.25
  2111.5 702.2 reduce-scatter.21
  2816.7 711.5 reduce-scatter.27
Sparse Core Ops, SparseCore 1:
  494.1 17.8 all-gather.23
  617.2 14.0 all-gather.25
where the time goes:
time: 3550 us; the launch traced here: 3540 us
  waiting for transfers between devices  2540 us (72%)
  matrix products  359 us (10%)
  local copies, waits for them, and re-layouts  209 us (6%)
  blocking collectives  193 us (5%)
  other arithmetic  134 us (4%)
  starting transfers between devices  81.1 us (2%)
    reduce_scatter x1, waiting for transfers between devices, on_device(): lax.psum_scatter(o_grad_sum, ('dp', 'ctx'), scatter_dimension=0, tiled=True)  714 us
    reduce_scatter x1, waiting for transfers between devices, on_device(): lax.psum_scatter(q_grad_sum, ('dp', 'ctx'), scatter_dimension=0, tiled=True)  705 us
    unnamed x24, waiting for transfers between devices  172 us
    reduce_scatter x1, waiting for transfers between devices, on_device(): lax.psum_scatter(v_grad_sum, ('dp', 'ctx'), scatter_dimension=0, tiled=True)  150 us
    all_to_all x4, waiting for transfers between devices, to_experts(): lax.all_to_all(slot_rows, 'ctx', split_axis=0, concat_axis=1, tiled=True)  121 us
    all_gather x2, waiting for transfers between devices, gather_keys(): lax.all_gather(v_local, 'ctx', axis=0, tiled=True)  120 us
    all_gather x1, waiting for transfers between devices, attention_weights(): lax.all_gather(q_weight, ('dp', 'ctx'), axis=0, tiled=True)  116 us
    reduce_scatter x1, waiting for transfers between devices, on_device(): lax.psum_scatter(k_grad_sum, ('dp', 'ctx'), scatter_dimension=0, tiled=True)  114 us
  transfers between devices with their start and end apart: 29, of which 24 were waited for; matrix products, arithmetic and copies ran while one was open for 14% of the time, Pallas kernels for 0%

commit v1 on v0

v1 whole, which is shorter than its diff:
```python
import jax
import jax.numpy as jnp
from jax import lax
from jax.sharding import Mesh, PartitionSpec as P

H = 32
KV = 4
HD = 128
TOPK = 8

eps_norm = 1e-06
rope_base = 1000000.0
neg_big = -1e30
f32 = jnp.float32
bf16 = jnp.bfloat16


def rms_scale(operand):
    return lax.rsqrt(jnp.mean(operand * operand, axis=-1, keepdims=True) + eps_norm)


def norm_back(operand, scale_rows, gain_vec, upstream):
    weighted = gain_vec * upstream
    inner_mean = jnp.mean(operand * weighted, axis=-1, keepdims=True)
    return scale_rows * weighted - operand * scale_rows * scale_rows * scale_rows * inner_mean


def rope_tables(positions, head_size):
    frequency = rope_base ** (-(jnp.arange(head_size // 2, dtype=f32) * 2.0 / head_size))
    angles = positions.astype(f32)[:, None] * frequency[None, :]
    angles = jnp.concatenate([angles, angles], axis=-1)
    return (jnp.cos(angles), jnp.sin(angles))


def rotate(operand, cosine, sine_table):
    half_width = operand.shape[-1] // 2
    turned = jnp.concatenate([-operand[..., half_width:], operand[..., :half_width]], axis=-1)
    return operand * cosine + turned * sine_table


def rotate_back(upstream, cosine, sine_table):
    shifted = upstream * sine_table
    half_width = upstream.shape[-1] // 2
    return upstream * cosine + jnp.concatenate(
        [shifted[..., half_width:], -shifted[..., :half_width]], axis=-1
    )


def dot(a, b):
    return jnp.dot(a, b, preferred_element_type=f32)


def dot_nt(a, b):
    return lax.dot_general(a, b, (((1,), (1,)), ((), ())), preferred_element_type=f32)


def dot_tn(a, b):
    return lax.dot_general(a, b, (((0,), (0,)), ((), ())), preferred_element_type=f32)


def take(v, index, axis=0):
    return lax.dynamic_index_in_dim(v, index, axis, keepdims=False)


def add_low(a, b):
    return (a.astype(f32) + b.astype(f32)).astype(bf16)


def flip(v, axis, bit):
    n = lax.axis_size(axis)
    return lax.ppermute(v, axis, [(i, i ^ bit) for i in range(n)])


def px(v):
    return flip(v, "cl", 1)


def py(v):
    return flip(v, "cl", 2)


def shift(v, by):
    n = lax.axis_size("sq")
    return lax.ppermute(v, "sq", [(i, (i + by) % n) for i in range(n)])


def bits_of(axis):
    n, bit, out = lax.axis_size(axis), 1, []
    while bit < n:
        out.append(bit)
        bit *= 2
    return out


def tree_gather(v, axes):
    v = v[None]
    for axis in reversed(axes):
        index = lax.axis_index(axis)
        for bit in bits_of(axis):
            other = flip(v, axis, bit)
            upper = (index & bit) != 0
            v = jnp.concatenate(
                [jnp.where(upper, other, v), jnp.where(upper, v, other)], axis=0
            )
    return v


def tree_scatter(v, axes):
    for axis in axes:
        index = lax.axis_index(axis)
        for bit in reversed(bits_of(axis)):
            half = v.shape[0] // 2
            upper = (index & bit) != 0
            own = jnp.where(upper, v[half:], v[:half])
            other = jnp.where(upper, v[:half], v[half:])
            v = own + flip(other, axis, bit)
    return v[0]


def dp_gather(v):
    v = v[None]
    index = lax.axis_index("dp")
    for bit in bits_of("dp"):
        other = flip(v, "dp", bit)
        upper = (index & bit) != 0
        v = jnp.concatenate([jnp.where(upper, other, v), jnp.where(upper, v, other)], axis=0)
    return v


def dp_scatter(v):
    index = lax.axis_index("dp")
    for bit in reversed(bits_of("dp")):
        half = v.shape[0] // 2
        upper = (index & bit) != 0
        own = lax.dynamic_slice_in_dim(v, jnp.where(upper, half, 0), half, 0)
        other = lax.dynamic_slice_in_dim(v, jnp.where(upper, 0, half), half, 0)
        v = own.astype(f32) + flip(other.astype(bf16), "dp", bit).astype(f32)
    return v[0]


def dp_sum(v):
    for bit in bits_of("dp"):
        v = v + flip(v.astype(bf16), "dp", bit).astype(f32)
    return v


def to_sequence(v):
    nl, n_dp, n_sq = v.shape[0], lax.axis_size("dp"), lax.axis_size("sq")
    zi = lax.axis_index("sq")
    got = []
    for m in range(nl):
        pairs = [
            (d * n_sq + z, (z // nl) * n_sq + nl * d + (m + z) % nl)
            for d in range(n_dp)
            for z in range(n_sq)
        ]
        got.append(lax.ppermute(take(v, (m + zi) % nl), ("dp", "sq"), pairs))
    return jnp.stack(got)


def from_sequence(v):
    nl, n_dp, n_sq = v.shape[0], lax.axis_size("dp"), lax.axis_size("sq")
    zi = lax.axis_index("sq")
    got = []
    for m in range(nl):
        pairs = [
            ((z // nl) * n_sq + nl * d + (m + z) % nl, d * n_sq + z)
            for d in range(n_dp)
            for z in range(n_sq)
        ]
        got.append(lax.ppermute(v[m], ("dp", "sq"), pairs))
    got = jnp.stack(got)
    return jnp.stack([take(got, (j - zi) % nl) for j in range(nl)])


def plane_gather(v):
    cl = lax.axis_index("cl")
    half = v.shape[1] // 2
    a, b = v[:, :half], v[:, half:]
    a1, b1 = px(a), py(b)
    a2, b2 = py(jnp.stack([a, a1])), px(jnp.stack([b, b1]))
    parts = [
        jnp.concatenate([a, b], axis=1),
        jnp.concatenate([a1, b2[0]], axis=1),
        jnp.concatenate([a2[0], b1], axis=1),
        jnp.concatenate([a2[1], b2[1]], axis=1),
    ]
    full = jnp.zeros((4,) + v.shape, v.dtype)
    for k in range(4):
        full = lax.dynamic_update_index_in_dim(full, parts[k], cl ^ k, 0)
    return dp_gather(full)


def plane_scatter(v):
    cl = lax.axis_index("cl")
    v = dp_scatter(v)
    half = v.shape[-1] // 2
    piece = lambda k, lo: take(v[:, :, lo : lo + half], cl ^ k)
    a = [piece(k, 0) for k in range(4)]
    b = [piece(k, half) for k in range(4)]
    ra = py(jnp.stack([a[2], a[3]]).astype(bf16))
    rb = px(jnp.stack([b[1], b[3]]).astype(bf16))
    a0, a1 = a[0] + ra[0].astype(f32), a[1] + ra[1].astype(f32)
    b0, b2 = b[0] + rb[0].astype(f32), b[2] + rb[1].astype(f32)
    a0 = a0 + px(a1.astype(bf16)).astype(f32)
    b0 = b0 + py(b2.astype(bf16)).astype(f32)
    return jnp.concatenate([a0, b0], axis=1)


def ring_gather(v):
    got = [v]
    for _ in range(lax.axis_size("sq") - 1):
        got.append(shift(got[-1], 1))
    return got


def ring_scatter(parts, low=True):
    moving = parts[-1]
    for t in range(len(parts) - 2, -1, -1):
        got = shift(moving.astype(bf16), -1)
        total = parts[t].astype(f32) + got.astype(f32)
        moving = total.astype(bf16) if (t or low) else total
    return moving


def column_cuts(width):
    units = width // 128
    first = max(1, (units * 5) // 16)
    last = max(0, (units - 2 * first) // 2)
    return [0, first * 128, 2 * first * 128, (2 * first + last) * 128, width]


def wide_gather(v):
    cuts = column_cuts(v.shape[1])
    ab, e, f = v[:, : cuts[2]], v[:, cuts[2] : cuts[3]], v[:, cuts[3] :]
    e1, f1 = px(e), py(f)
    z = ring_gather(ab)
    n = len(z)
    e2, f2 = py(jnp.stack([e, e1])), px(jnp.stack([f, f1]))
    e4 = jnp.stack([e, e1, e2[0], e2[1]])
    f4 = jnp.stack([f, f2[0], f1, f2[1]])
    ef = jnp.concatenate([e4, f4], axis=-1)
    a = jnp.stack([q[:, : cuts[1]] for q in z])
    b = jnp.stack([q[:, cuts[1] :] for q in z])
    a1, b1 = px(a), py(b)
    zef = ring_gather(ef)
    a2, b2 = py(jnp.stack([a, a1])), px(jnp.stack([b, b1]))
    a4 = jnp.stack([a, a1, a2[0], a2[1]], axis=1)
    b4 = jnp.stack([b, b2[0], b1, b2[1]], axis=1)
    return jnp.concatenate([a4, b4, jnp.stack(zef)], axis=-1)


def wide_scatter(v):
    cuts = column_cuts(v.shape[-1])
    a, b = v[..., : cuts[1]], v[..., cuts[1] : cuts[2]]
    ef = v[..., cuts[2] :]
    we = cuts[3] - cuts[2]
    ra = py(a[:, 2:])
    rb = px(jnp.stack([b[:, 1], b[:, 3]], axis=1))
    ef = ring_scatter([ef[t] for t in range(v.shape[0])])
    a = add_low(a[:, :2], ra)
    b = add_low(jnp.stack([b[:, 0], b[:, 2]], axis=1), rb)
    a = add_low(a[:, 0], px(a[:, 1]))
    b = add_low(b[:, 0], py(b[:, 1]))
    ab = jnp.concatenate([a, b], axis=-1)
    e, f = ef[..., :we], ef[..., we:]
    re = py(e[2:])
    rf = px(jnp.stack([f[1], f[3]]))
    e = add_low(e[:2], re)
    f = add_low(jnp.stack([f[0], f[2]]), rf)
    e = add_low(e[0], px(e[1]))
    f = add_low(f[0], py(f[1]))
    ab = ring_scatter([ab[t] for t in range(v.shape[0])])
    return jnp.concatenate([ab, e, f], axis=-1)


def on_device(
    tokens,
    segment_ids,
    routes,
    cotangent,
    q_weight,
    k_weight,
    v_weight,
    o_weight,
    router_weight,
    norm_gains,
    gate_up_weight,
    down_weight,
):
    n_dp, n_sq, n_cl = lax.axis_size("dp"), lax.axis_size("sq"), lax.axis_size("cl")
    dp, zi, cl = lax.axis_index("dp"), lax.axis_index("sq"), lax.axis_index("cl")
    nl, bl, width = tokens.shape
    rows = nl * bl
    n_ctx = n_sq * n_cl
    length = bl * n_ctx
    n_all = n_dp * n_ctx
    tp = n_cl * n_dp
    experts = n_ctx
    expert = zi * n_cl + cl
    capacity = max(2, (5 * bl * TOPK + 4 * experts - 1) // (4 * experts))
    ff = down_weight.shape[1]
    heads = H // tp
    hw = heads * HD
    kvw = 2 * HD // n_dp
    pack = hw + kvw
    score_scale = HD ** (-0.5)
    shard = width // n_all

    hit = jnp.any(
        routes[:, :, :, None] == jnp.arange(experts, dtype=jnp.int32), axis=2
    ).astype(bf16)
    below = jnp.tril(jnp.ones((bl, bl), bf16), -1)
    earlier = jnp.einsum("pq,jqe->jpe", below, hit, preferred_element_type=f32)
    codes = jnp.where(hit > 0, jnp.minimum(earlier + 1.0, capacity + 1.0), 0.0).astype(bf16)
    codes = jnp.pad(codes, ((0, 0), (0, 0), (0, 128 - experts)))

    small = jnp.concatenate(
        [router_weight.T.reshape(-1), norm_gains.reshape(-1)]
    )
    n_small = small.shape[0]
    n_router = experts * shard
    small = jnp.pad(small, (0, -n_small % 128)).reshape(-1, 128)
    small = tree_gather(small, ("dp", "sq", "cl")).reshape(n_all, -1)
    router_t = small[:, :n_router].reshape(n_all, experts, shard)
    router_t = jnp.transpose(router_t, (1, 0, 2)).reshape(experts, width)
    gains = small[:, n_router:n_small].reshape(-1).astype(f32)
    attn_gain = gains[:width]
    ffn_gain = gains[width : 2 * width]
    q_gain = gains[2 * width : 2 * width + HD]
    k_gain = gains[2 * width + HD :]

    inputs = to_sequence(tokens).reshape(rows, width).astype(f32)

    kv_weight = jnp.concatenate(
        [k_weight.reshape(shard, n_cl, HD), v_weight.reshape(shard, n_cl, HD)], axis=-1
    )
    packed = jnp.concatenate(
        [
            q_weight.reshape(shard, n_cl, n_dp, hw),
            kv_weight.reshape(shard, n_cl, n_dp, kvw),
        ],
        axis=-1,
    )
    packed = jnp.transpose(packed, (1, 2, 0, 3)).reshape(tp, shard, pack)
    packed = lax.all_to_all(packed, ("cl", "dp"), split_axis=0, concat_axis=0, tiled=True)
    packed = jnp.transpose(packed.reshape(n_cl, n_dp, shard, pack), (1, 0, 2, 3))
    qkv_w = jnp.zeros((n_dp, n_sq, n_cl, shard, pack), bf16)
    for t, piece in enumerate(ring_gather(packed)):
        qkv_w = lax.dynamic_update_index_in_dim(qkv_w, piece, (zi - t) % n_sq, 1)
    qkv_w = qkv_w.reshape(width, pack)

    o_pairs = []
    for f in range(n_all):
        r, q = f // n_sq, f % n_sq
        o_pairs.append((f, ((r % n_dp) * n_sq + q) * n_cl + r // n_dp))
    o_mine = lax.ppermute(o_weight, ("dp", "sq", "cl"), o_pairs)
    o_full = jnp.zeros((n_sq,) + o_mine.shape, bf16)
    for t, piece in enumerate(ring_gather(o_mine)):
        o_full = lax.dynamic_update_index_in_dim(o_full, piece, (zi - t) % n_sq, 0)
    o_full = o_full.reshape(hw, width)

    gu_full = dp_gather(gate_up_weight[0]).reshape(width, 2 * ff)
    down_full = jnp.concatenate(list(dp_gather(down_weight[0])), axis=1)

    upstream_low = to_sequence(jnp.concatenate([cotangent, codes], axis=-1)).reshape(rows, -1)
    upstream = upstream_low[:, :width].astype(f32)
    own_codes = upstream_low[:, width : width + experts].astype(f32)
    grads_all = wide_gather(upstream_low).reshape(n_ctx * rows, -1)

    block_of = (zi - jnp.arange(nl)) % nl
    d_ids = jnp.arange(n_dp)[:, None, None, None]
    c_ids = jnp.arange(n_cl)[None, :, None, None]
    positions = ((d_ids * nl + block_of[None, None, :, None]) * n_cl + c_ids) * bl + jnp.arange(
        bl
    )[None, None, None, :]
    positions = positions.reshape(length).astype(jnp.int32)
    segments = take(tree_gather(segment_ids, ("dp",)).reshape(n_dp * nl, length), zi)
    segments = segments.reshape(n_dp, nl, n_cl, bl)
    segments = jnp.stack([take(segments, (zi - m) % nl, 1) for m in range(nl)], axis=2)
    segments = segments.reshape(length)
    cosine, sine_table = rope_tables(positions, HD)
    cosine, sine_table = cosine[:, None, :], sine_table[:, None, :]

    first_scale = rms_scale(inputs)
    normed = (inputs * first_scale * attn_gain).astype(bf16)
    normed_all = plane_gather(normed).reshape(length, width)
    proj = dot(normed_all, qkv_w)
    q_proj = proj[:, :hw].reshape(length, heads, HD)
    kv_proj = dp_gather(proj[:, hw:])
    kv_proj = jnp.concatenate(list(kv_proj), axis=-1)
    k_proj = kv_proj[:, None, :HD]
    values = kv_proj[:, HD:].astype(bf16)
    q_scale = rms_scale(q_proj)
    k_scale = rms_scale(k_proj)
    queries = rotate(q_proj * q_scale * q_gain, cosine, sine_table).astype(bf16)
    keys = rotate(k_proj * k_scale * k_gain, cosine, sine_table).astype(bf16)[:, 0]
    allowed = (positions[None, :] <= positions[:, None]) & (
        segments[None, :] == segments[:, None]
    )
    scores = jnp.einsum("qhd,kd->hqk", queries, keys, preferred_element_type=f32) * score_scale
    scores = jnp.where(allowed[None], scores, neg_big)
    terms = jnp.exp(scores - jnp.max(scores, axis=-1, keepdims=True))
    probs = terms / jnp.sum(terms, axis=-1, keepdims=True)
    prob_low = probs.astype(bf16)
    attended = jnp.einsum("hqk,kd->qhd", prob_low, values, preferred_element_type=f32)
    attended = attended.reshape(length, hw).astype(bf16)
    mixed = plane_scatter(dot(attended, o_full).reshape(n_dp, n_cl, rows, width))
    middle = inputs + mixed
    second_scale = rms_scale(middle)
    hidden = (middle * second_scale * ffn_gain).astype(bf16)
    logits = dot_nt(hidden, router_t)
    routed = own_codes > 0
    top = jnp.max(jnp.where(routed, logits, neg_big), axis=-1, keepdims=True)
    gate_terms = jnp.where(routed, jnp.exp(logits - top), 0.0)
    gates = gate_terms / jnp.sum(gate_terms, axis=-1, keepdims=True)
    gates_high = gates.astype(bf16)
    gates_low = (gates - gates_high.astype(f32)).astype(bf16)
    extra = jnp.pad(
        jnp.concatenate([gates_high, gates_low], axis=-1), ((0, 0), (0, 128 - 2 * experts))
    )
    hidden_all = wide_gather(jnp.concatenate([hidden, extra], axis=-1)).reshape(n_ctx * rows, -1)

    n_rows = n_ctx * rows
    per = min(4, n_rows // bl)
    n_groups = n_rows // (per * bl)
    lanes = jnp.arange(128)
    code = jnp.sum(jnp.where(lanes == expert, grads_all[:, width:].astype(f32), 0.0), axis=-1)
    pick = (lanes == expert) | (lanes == experts + expert)
    gate_mine = jnp.sum(jnp.where(pick, hidden_all[:, width:].astype(f32), 0.0), axis=-1)
    in_group = (jnp.arange(n_rows) // bl) % per
    code = jnp.where((code > 0) & (code <= capacity), code + in_group * 128.0, -1.0)
    code = code.reshape(n_groups, 1, per * bl)
    slot_ids = jnp.arange(per * capacity)
    slot_ids = ((slot_ids // capacity) * 128 + slot_ids % capacity + 1).astype(f32)
    select = code == slot_ids[None, :, None]
    select_low = select.astype(bf16)
    n_slots = n_groups * per * capacity

    def pull(v):
        v = v.reshape(n_groups, per * bl, -1)
        got = jnp.einsum("grt,gtd->grd", select_low, v, preferred_element_type=f32)
        return got.astype(bf16).reshape(n_slots, -1)

    def push(v):
        v = v.reshape(n_groups, per * capacity, -1)
        got = jnp.einsum("grt,grd->gtd", select_low, v, preferred_element_type=f32)
        return got.astype(bf16).reshape(n_rows, -1)

    gate_slot = jnp.sum(
        jnp.where(select, gate_mine.reshape(n_groups, 1, per * bl), 0.0), axis=-1
    ).reshape(n_slots, 1)
    expert_in = pull(hidden_all[:, :width])
    grad_slot = pull(grads_all[:, :width]).astype(f32)
    gate_up = dot(expert_in, gu_full)
    gate_part, up_part = gate_up[:, :ff], gate_up[:, ff:]
    sigmoid_gate = jax.nn.sigmoid(gate_part)
    activated = (gate_part * sigmoid_gate * up_part).astype(bf16)
    expert_out = dot(activated, down_full).astype(bf16)
    out_wide = expert_out.astype(f32)
    pair_grad = jnp.sum(grad_slot * out_wide, axis=-1)
    moe = wide_scatter(push((gate_slot * out_wide).astype(bf16)).reshape(n_sq, n_cl, rows, width))
    output = (middle + moe.astype(f32)).astype(bf16)

    out_grad = (gate_slot * grad_slot).astype(bf16)
    act_grad = dot_nt(out_grad, down_full)
    gate_back = act_grad * up_part * sigmoid_gate * (1.0 + gate_part * (1.0 - sigmoid_gate))
    up_back = act_grad * gate_part * sigmoid_gate
    gu_grad = jnp.concatenate([gate_back, up_back], axis=-1).astype(bf16)
    row_grad = dot_nt(gu_grad, gu_full).astype(bf16)
    pair_token = jnp.sum(
        jnp.where(select, pair_grad.reshape(n_groups, per * capacity, 1), 0.0), axis=1
    ).reshape(n_rows, 1)
    pair_high = pair_token.astype(bf16)
    pair_low = (pair_token - pair_high.astype(f32)).astype(bf16)
    pair_extra = jnp.where(
        lanes == expert, pair_high, jnp.where(lanes == experts + expert, pair_low, 0)
    ).astype(bf16)
    back = wide_scatter(
        jnp.concatenate([push(row_grad), pair_extra], axis=-1).reshape(n_sq, n_cl, rows, -1)
    ).astype(f32)

    gu_share = dp_scatter(dot_tn(expert_in, gu_grad).reshape(n_dp, -1, 2 * ff))
    down_share = dp_scatter(
        jnp.stack(jnp.split(dot_tn(activated, out_grad), n_dp, axis=1))
    )

    pair_own = back[:, width : width + experts] + back[:, width + experts : width + 2 * experts]
    chosen_grad = gates * (pair_own - jnp.sum(gates * pair_own, axis=-1, keepdims=True))
    logit_grad = chosen_grad.astype(bf16)
    hidden_grad = back[:, :width] + dot(logit_grad, router_t)
    router_grad = dot_tn(logit_grad, hidden)
    ffn_gain_grad = jnp.sum(hidden_grad * middle * second_scale, axis=0)
    middle_grad = upstream + norm_back(middle, second_scale, ffn_gain, hidden_grad)

    middle_low = plane_gather(middle_grad.astype(bf16)).reshape(length, width)
    attended_grad = dot_nt(middle_low, o_full).astype(bf16).reshape(length, heads, HD)
    o_grad = dot_tn(attended, middle_low).reshape(n_sq, -1, width)
    o_share = ring_scatter([take(o_grad, (zi - t) % n_sq) for t in range(n_sq)])
    o_share = lax.ppermute(
        o_share, ("dp", "sq", "cl"), [(b, a) for a, b in o_pairs]
    ).astype(f32)
    prob_grad = jnp.einsum("qhd,kd->hqk", attended_grad, values, preferred_element_type=f32)
    inner_sum = jnp.sum(probs * prob_grad, axis=-1, keepdims=True)
    score_grad = (probs * (prob_grad - inner_sum)).astype(bf16)
    value_part = jnp.einsum("hqk,qhd->kd", prob_low, attended_grad, preferred_element_type=f32)
    key_part = (
        jnp.einsum("hqk,qhd->kd", score_grad, queries, preferred_element_type=f32) * score_scale
    )
    query_grad = (
        jnp.einsum("hqk,kd->qhd", score_grad, keys, preferred_element_type=f32) * score_scale
    )
    kv_sum = dp_sum(jnp.concatenate([key_part, value_part], axis=-1))
    key_rot_grad = rotate_back(kv_sum[:, None, :HD], cosine, sine_table)
    k_gain_grad = jnp.sum(key_rot_grad * k_proj * k_scale, axis=(0, 1))
    k_gain_grad = jnp.where(dp == 0, k_gain_grad, 0.0)
    k_low = norm_back(k_proj, k_scale, k_gain, key_rot_grad)[:, 0].astype(bf16)
    kv_low = jnp.concatenate([k_low, kv_sum[:, HD:].astype(bf16)], axis=-1)
    kv_low = lax.dynamic_slice_in_dim(kv_low, dp * kvw, kvw, 1)
    query_rot_grad = rotate_back(query_grad, cosine, sine_table)
    q_gain_grad = jnp.sum(query_rot_grad * q_proj * q_scale, axis=(0, 1))
    q_low = norm_back(q_proj, q_scale, q_gain, query_rot_grad).reshape(length, hw).astype(bf16)
    qkv_low = jnp.concatenate([q_low, kv_low], axis=-1)
    normed_grad = plane_scatter(dot_nt(qkv_low, qkv_w).reshape(n_dp, n_cl, rows, width))
    attn_gain_grad = jnp.sum(normed_grad * inputs * first_scale, axis=0)
    input_grad = middle_grad + norm_back(inputs, first_scale, attn_gain, normed_grad)
    input_grad = from_sequence(input_grad.astype(bf16).reshape(nl, bl, width))
    output = from_sequence(output.reshape(nl, bl, width))

    w_grad = dot_tn(normed_all, qkv_low).reshape(n_dp, n_sq, n_cl, shard, pack)
    w_grad = ring_scatter([take(w_grad, (zi - t) % n_sq, 1) for t in range(n_sq)])
    w_grad = jnp.transpose(w_grad, (1, 0, 2, 3)).reshape(tp, shard, pack)
    w_grad = lax.all_to_all(w_grad, ("cl", "dp"), split_axis=0, concat_axis=0, tiled=True)
    w_grad = jnp.transpose(w_grad.reshape(n_cl, n_dp, shard, pack), (2, 0, 1, 3)).astype(f32)
    q_share = w_grad[..., :hw].reshape(shard, -1)
    kv_share = w_grad[..., hw:].reshape(shard, n_cl, 2 * HD)
    k_share = kv_share[..., :HD].reshape(shard, -1)
    v_share = kv_share[..., HD:].reshape(shard, -1)

    gain_grads = jnp.concatenate([attn_gain_grad, ffn_gain_grad, q_gain_grad, k_gain_grad])
    router_grad = jnp.transpose(router_grad.reshape(experts, n_all, shard), (1, 0, 2))
    small_grad = jnp.concatenate(
        [router_grad.reshape(n_all, n_router), gain_grads.reshape(n_all, -1)], axis=-1
    )
    small_grad = jnp.pad(small_grad, ((0, 0), (0, -n_small % 128))).reshape(n_all, -1, 128)
    small_grad = tree_scatter(small_grad, ("dp", "sq", "cl")).reshape(-1)
    router_share = small_grad[:n_router].reshape(experts, shard).T
    gains_share = small_grad[n_router:n_small]
    return (
        output,
        input_grad,
        q_share,
        k_share,
        v_share,
        o_share,
        router_share,
        gains_share,
        gu_share[None],
        down_share[None],
    )


def solution(mesh):
    n_dp, n_ctx = mesh.devices.shape
    n_cl = KV
    fine = Mesh(mesh.devices.reshape(n_dp, n_ctx // n_cl, n_cl), ("dp", "sq", "cl"))
    ctx = ("sq", "cl")
    every = ("dp", "sq", "cl")
    rows = P("dp", ctx, None)
    placed = (
        rows,
        P("dp", None),
        rows,
        rows,
        P(every, None),
        P(every, None),
        P(every, None),
        P(every, None),
        P(every, None),
        P(every),
        P(ctx, "dp", None),
        P(ctx, None, "dp"),
    )
    return jax.shard_map(
        on_device,
        mesh=fine,
        in_specs=placed,
        out_specs=(
            rows,
            rows,
            P(every, None),
            P(every, None),
            P(every, None),
            P(every, None),
            P(every, None),
            P(every),
            P(ctx, "dp", None),
            P(ctx, None, "dp"),
        ),
        check_vma=False,
    )
```

time: 3550 us -> 1120 us (0.32)
  waiting for transfers between devices: 2540 us -> 356 us
  matrix products: 359 us -> 153 us
  blocking collectives: 193 us -> 0 us
  starting transfers between devices: 81.1 us -> 167 us
  other arithmetic: 134 us -> 213 us
    reduce_scatter x8 -> x0, waiting for transfers between devices: 1760 us -> none  [the longest x1 714 us: on_device(): lax.psum_scatter(o_grad_sum, ('dp', 'ctx'), scatter_dimension=0, tiled=True)]
    all_gather x10 -> x0, waiting for transfers between devices: 434 us -> none  [the longest x2 120 us: gather_keys(): lax.all_gather(v_local, 'ctx', axis=0, tiled=True)]
    ppermute x0 -> x115, waiting for transfers between devices: none -> 356 us  [the longest x36 214 us: shift(): return lax.ppermute(v, 'sq', [(i, (i + by) % n) for i in range(n)])]
    dot_general x54 -> x25, matrix products: 336 us -> 137 us  [the longest x5 31.4 us: dot_tn(): lax.dot_general(a, b, (((0,), (0,)), ((), ())), preferred_element_type=f32)]
    all_to_all x8 -> x2, waiting for transfers between devices: 175 us -> 0.01 us  [the longest x1 0.01 us: on_device(): lax.all_to_all(packed, ('cl', 'dp'), split_axis=0, concat_axis=0, tiled=T...]
    unnamed x24 -> x0, waiting for transfers between devices: 172 us -> none
    ppermute x0 -> x115, starting transfers between devices: none -> 156 us  [the longest x69 97.7 us: flip(): return lax.ppermute(v, axis, [(i, i ^ bit) for i in range(n)])]
    all_gather x1 -> x0, blocking collectives: 111 us -> none  [attention_weights(): lax.all_gather(router_weight, ('dp', 'ctx'), axis=0, tiled=True)]
  transfers between devices with their start and end apart: 29 -> 117, of which waited for: 24 -> 51; matrix products, arithmetic and copies ran while one was open for 14% -> 33% of each run, Pallas kernels for 0% -> 0%
where the time goes in v1:
time: 1120 us; the launch traced here: 1100 us
  waiting for transfers between devices  356 us (32%)
  other arithmetic  213 us (19%)
  local copies, waits for them, and re-layouts  211 us (19%)
  starting transfers between devices  167 us (15%)
  matrix products  153 us (14%)
    ppermute x36, waiting for transfers between devices, shift(): return lax.ppermute(v, 'sq', [(i, (i + by) % n) for i in range(n)])  214 us
    ppermute x69, waiting for transfers between devices, flip(): return lax.ppermute(v, axis, [(i, i ^ bit) for i in range(n)])  110 us
    ppermute x69, starting transfers between devices, flip(): return lax.ppermute(v, axis, [(i, i ^ bit) for i in range(n)])  97.7 us
    unnamed x367, local copies, waits for them, and re-layouts  59.3 us
    concatenate x2, other arithmetic, wide_gather(): return jnp.concatenate([a4, b4, jnp.stack(zef)], axis=-1)  53.1 us
    ppermute x4, waiting for transfers between devices, from_sequence(): got.append(lax.ppermute(v[m], ('dp', 'sq'), pairs))  32 us
    dot_general x5, matrix products, dot_tn(): lax.dot_general(a, b, (((0,), (0,)), ((), ())), preferred_element_type=f32)  31.4 us
    ppermute x36, starting transfers between devices, shift(): return lax.ppermute(v, 'sq', [(i, (i + by) % n) for i in range(n)])  28.5 us
  transfers between devices with their start and end apart: 117, of which 51 were waited for; matrix products, arithmetic and copies ran while one was open for 33% of the time, Pallas kernels for 0%

profile of v1, /device:TPU:1, one launch (start us, length us, event | category | flops | bytes accessed | tf_op | source)
XLA Modules:
  0.0 1104.6 jit_solution(15129076573621023033)
XLA Ops:
  63.8 21.0 %collective-permute-done.35 = bf16[128,384]{1,0:T(8,128)(2,1)S(1)} collective-permute-done((bf16[128,384]{1,0:T(8,128)(2,1)S(1)}, bf16[128,384]{1,0:T(8,128)(2,1)S(1)}, u32[]{:S(2)}, u32[]{:S(2)}) %collective-permute-start.35) | collective-permute-done | bytes 98336 | tf_op jit(solution)/shard_map/ppermute | solution.py:71
  131.5 10.7 collective-permute-done.19
  143.0 13.2 %collective-permute-done.13 = bf16[2,4,64,640]{3,2,0,1:T(8,128)(2,1)S(1)} collective-permute-done((bf16[2,4,64,640]{3,2,0,1:T(8,128)(2,1)}, bf16[2,4,64,640]{3,2,0,1:T(8,128)(2,1)S(1)}, u32[]{:S(2)}, u32[]{:S(2)}) %collective-permute-start.13) | collective-permute-done | bytes 655392 | tf_op jit(solution)/shard_map/ppermute | solution.py:84
  156.6 10.8 collective-permute-done.20
  168.4 20.3 %collective-permute-done.28 = bf16[128,1280]{1,0:T(8,128)(2,1)} collective-permute-done((bf16[128,1280]{1,0:T(8,128)(2,1)S(1)}, bf16[128,1280]{1,0:T(8,128)(2,1)}, u32[]{:S(2)}, u32[]{:S(2)}) %collective-permute-start.28) | collective-permute-done | bytes 327712 | tf_op jit(solution)/shard_map/ppermute | solution.py:84
  203.7 16.6 %fusion.229 = (f32[4,1024]{1,0:T(4,128)}, f32[4,1024,1024]{1,2,0:T(8,128)}) fusion(pred[1024,1024]{0,1:T(8,128)(4,1)} %compare_and_fusion, bf16[1024,4,128]{0,2,1:T(8,128)(2,1)} %bitcast.748, f32[1024,1,1,1,1,1,64]{0,6,5,4,3,2,1:T(8,128)} %get-tuple-element.218, f32[1024,1,1,1,1,1,64]{0,6,5,4,3,2,1:T(8,128)} %get-tuple-element.143, ...), kind=kOutput, calls=%fused_computation.618 | convolution fusion | flops 1091568640 | bytes 20206080 | tf_op jit(solution)/shard_map/sub | solution.py:403
  245.7 24.5 %collective-permute-done.30 = bf16[128,1280]{1,0:T(8,128)(2,1)S(1)} collective-permute-done((bf16[128,1280]{1,0:T(8,128)(2,1)}, bf16[128,1280]{1,0:T(8,128)(2,1)S(1)}, u32[]{:S(2)}, u32[]{:S(2)}) %collective-permute-start.30) | collective-permute-done | bytes 327712 | tf_op jit(solution)/shard_map/ppermute | solution.py:84
  310.6 19.7 %collective-permute-done.24 = bf16[2,128,1024]{1,2,0:T(8,128)(2,1)S(1)} collective-permute-done((bf16[2,128,1024]{1,2,0:T(8,128)(2,1)S(1)}, bf16[2,128,1024]{1,2,0:T(8,128)(2,1)S(1)}, u32[]{:S(2)}, u32[]{:S(2)}) %collective-permute-start.24) | collective-permute-done | bytes 524320 | tf_op jit(solution)/shard_map/ppermute | solution.py:71
  362.4 9.4 collective-permute-done.44
  376.3 11.4 %collective-permute-done.53 = bf16[4,128,896]{1,2,0:T(8,128)(2,1)} collective-permute-done((bf16[4,128,896]{1,2,0:T(8,128)(2,1)S(1)}, bf16[4,128,896]{1,2,0:T(8,128)(2,1)}, u32[]{:S(2)}, u32[]{:S(2)}) %collective-permute-start.53) | collective-permute-done | bytes 917536 | tf_op jit(solution)/shard_map/ppermute | solution.py:84
  425.3 47.6 %maximum_maximum_fusion.1 = bf16[4,4,128,2176]{2,3,1,0:T(8,128)(2,1)} fusion(bf16[1,4,128,896]{2,3,1,0:T(8,128)(2,1)S(1)} %bitcast.754, bf16[1,4,128,896]{2,3,1,0:T(8,128)(2,1)} %bitcast.135, bf16[1,4,128,896]{2,3,1,0:T(8,128)(2,1)} %bitcast.134, bf16[1,4,128,896]{2,3,1,0:T(8,128)(2,1)S(1)} %fusion.276, bf16[4,1,128,640]{2,3,1,0:T(8,128)(2,1)S(1)} %get-tuple-element.104, ...), kind=kLoop, calls=%fused_computation.16 | loop fusion | flops 84148224 | bytes 17825792 | tf_op jit(solution)/shard_map/concatenate | solution.py:250
  472.9 11.8 %copy.372 = bf16[4,4,128,2176]{3,2,1,0:T(8,128)(2,1)} copy(bf16[4,4,128,2176]{2,3,1,0:T(8,128)(2,1)} %maximum_maximum_fusion.1) | data formatting | bytes 17825792 | tf_op jit(solution)/shard_map/concatenate | solution.py:250
  484.7 8.4 slice.802
  501.6 12.7 %fusion.238 = f32[1280,1536]{1,0:T(8,128)S(1)} fusion(bf16[1280,2048]{1,0:T(8,128)(2,1)} %bitcast.671, bf16[2048,1536]{1,0:T(8,128)(2,1)} %bitcast.704), kind=kOutput, calls=%fused_computation.620 | convolution fusion | flops 8053063680 | bytes 19398656 | tf_op jit(solution)/shard_map/dot_general | solution.py:50
  526.2 12.1 %fusion.6 = (bf16[1280,2048]{1,0:T(8,128)(2,1)}, bf16[1280,2048]{1,0:T(8,128)(2,1)}) fusion(bf16[8,160,2048]{2,1,0:T(8,128)(2,1)} %convolution_convert_fusion.4, f32[1280]{0:T(1024)S(1)} %mul.727, bf16[1280,2048]{1,0:T(8,128)(2,1)} %get-tuple-element.225), kind=kLoop, calls=%fused_computation.13 | loop fusion | flops 15728640 | bytes 20976640 | tf_op jit(solution)/shard_map/convert_element_type | solution.py:465
  549.4 9.4 multiply_convert_fusion.1
  558.9 8.7 convolution_convert_fusion
  575.0 11.4 %copy.392 = bf16[4,4,128,2048]{2,3,1,0:T(8,128)(2,1)} copy(bf16[4,4,128,2048]{3,2,1,0:T(8,128)(2,1)} %bitcast.659) | data formatting | bytes 16777216 | tf_op jit(solution)/shard_map/concatenate | solution.py:480
  586.4 10.1 fusion.240
  625.3 11.0 fusion.15
  671.8 12.5 %collective-permute-start.113 = (bf16[1,1024,1536]{2,1,0:T(8,128)(2,1)}, bf16[1,1024,1536]{2,1,0:T(8,128)(2,1)}, u32[]{:S(2)}, u32[]{:S(2)}) collective-permute-start(bf16[1,1024,1536]{2,1,0:T(8,128)(2,1)} %dynamic-slice_convert_fusion), channel_id=1, source_target_pairs={{0,16},{16,0},{1,17},{17,1},{2,18},{18,2},{3,19},{19,3},{4,20},{20... | collective-permute-start | bytes 9437192 | tf_op jit(solution)/shard_map/ppermute | solution.py:71
  697.9 8.8 collective-permute-done.66
  710.6 15.6 %collective-permute-done.82 = bf16[4,128,896]{1,2,0:T(8,128)(2,1)S(1)} collective-permute-done((bf16[4,128,896]{1,2,0:T(8,128)(2,1)S(1)}, bf16[4,128,896]{1,2,0:T(8,128)(2,1)S(1)}, u32[]{:S(2)}, u32[]{:S(2)}) %collective-permute-start.82) | collective-permute-done | bytes 917536 | tf_op jit(solution)/shard_map/ppermute | solution.py:84
  728.9 20.6 %collective-permute-done.78 = bf16[128,1280]{0,1:T(8,128)(2,1)S(1)} collective-permute-done((bf16[128,1280]{0,1:T(8,128)(2,1)S(1)}, bf16[128,1280]{0,1:T(8,128)(2,1)S(1)}, u32[]{:S(2)}, u32[]{:S(2)}) %collective-permute-start.78) | collective-permute-done | bytes 327712 | tf_op jit(solution)/shard_map/ppermute | solution.py:84
  751.9 24.2 %collective-permute-done.79 = bf16[128,1280]{0,1:T(8,128)(2,1)S(1)} collective-permute-done((bf16[128,1280]{0,1:T(8,128)(2,1)S(1)}, bf16[128,1280]{0,1:T(8,128)(2,1)S(1)}, u32[]{:S(2)}, u32[]{:S(2)}) %collective-permute-start.79) | collective-permute-done | bytes 327712 | tf_op jit(solution)/shard_map/ppermute | solution.py:84
  780.2 9.9 collective-permute-done.80
  870.7 8.4 fusion.1
  930.9 9.0 collective-permute-done.101
  1002.6 8.8 collective-permute-done.97
  1033.5 9.4 collective-permute-start.109
  1066.6 9.0 collective-permute-done.99
  1081.9 16.7 %collective-permute-done.72 = bf16[64,2048]{0,1:T(8,128)(2,1)S(1)} collective-permute-done((bf16[64,2048]{0,1:T(8,128)(2,1)}, bf16[64,2048]{0,1:T(8,128)(2,1)S(1)}, u32[]{:S(2)}, u32[]{:S(2)}) %collective-permute-start.72) | collective-permute-done | bytes 262176 | tf_op jit(solution)/shard_map/ppermute | solution.py:171
  (948 shorter events, 646.9 us)
Async XLA Ops:
  8.2 49.6 %collective-permute-start.26 = (bf16[64,2176]{1,0:T(8,128)(2,1)}, bf16[64,2176]{1,0:T(8,128)(2,1)}, u32[]{:S(2)}, u32[]{:S(2)}) collective-permute-start(bf16[64,2176]{1,0:T(8,128)(2,1)} %get-tuple-element.137), channel_id=1, source_target_pairs={{0,0},{4,4},{8,16},{12,20},{16,8},{20,12},{24,24},{28,28},{1,1},{5... | collective-permute-start | bytes 835592 | tf_op jit(solution)/shard_map/ppermute | solution.py:157
  12.3 45.5 %collective-permute-start.27 = (bf16[64,2176]{1,0:T(8,128)(2,1)}, bf16[64,2176]{1,0:T(8,128)(2,1)}, u32[]{:S(2)}, u32[]{:S(2)}) collective-permute-start(bf16[64,2176]{1,0:T(8,128)(2,1)} %get-tuple-element.138), channel_id=1, source_target_pairs={{0,4},{4,0},{8,20},{12,16},{16,12},{20,8},{24,28},{28,24},{1,5},{5... | collective-permute-start | bytes 835592 | tf_op jit(solution)/shard_map/ppermute | solution.py:157
  13.9 39.5 %collective-permute-start = (bf16[64,2048]{1,0:T(8,128)(2,1)S(1)}, bf16[64,2048]{1,0:T(8,128)(2,1)S(1)}, u32[]{:S(2)}, u32[]{:S(2)}) collective-permute-start(bf16[64,2048]{1,0:T(8,128)(2,1)S(1)} %get-tuple-element.169), channel_id=1, source_target_pairs={{0,0},{4,4},{8,16},{12,20},{16,8},{20,12},{24,24},{28,28},{1,1},{5... | collective-permute-start | bytes 786440 | tf_op jit(solution)/shard_map/ppermute | solution.py:157
  18.7 80.9 %all-to-all-start = ((bf16[8,64,640]{2,1,0:T(8,128)(2,1)}), bf16[8,64,640]{2,1,0:T(8,128)(2,1)}, u32[]{:S(2)}, u32[]{:S(2)}) async-start(bf16[8,64,640]{2,1,0:T(8,128)(2,1)} %bitcast.21), calls=%async_computation | async-start | bytes 1310720 | tf_op jit(solution)/shard_map/all_to_all | solution.py:346
  48.3 46.0 %collective-permute-start.17 = (bf16[128,2048]{1,0:T(8,128)(2,1)}, bf16[128,2048]{1,0:T(8,128)(2,1)}, u32[]{:S(2)}, u32[]{:S(2)}) collective-permute-start(bf16[128,2048]{1,0:T(8,128)(2,1)} %param.19), channel_id=1, source_target_pairs={{0,0},{1,4},{2,8},{3,12},{4,16},{5,20},{6,24},{7,28},{8,1},{9,5},{... | collective-permute-start | bytes 1572872 | tf_op jit(solution)/shard_map/ppermute | solution.py:357
  53.4 221.3 %collective-permute-start.57 = (bf16[1,768,1024]{2,1,0:T(8,128)(2,1)}, bf16[1,768,1024]{2,1,0:T(8,128)(2,1)}, u32[]{:S(2)}, u32[]{:S(2)}) collective-permute-start(bf16[1,768,1024]{2,1,0:T(8,128)(2,1)} %param.23), channel_id=1, source_target_pairs={{0,16},{16,0},{1,17},{17,1},{2,18},{18,2},{3,19},{19,3},{4,20},{20... | collective-permute-start | bytes 4718600 | tf_op jit(solution)/shard_map/ppermute | solution.py:71
  85.5 221.0 %collective-permute-start.56 = (bf16[1,1024,1536]{2,1,0:T(8,128)(2,1)}, bf16[1,1024,1536]{2,1,0:T(8,128)(2,1)}, u32[]{:S(2)}, u32[]{:S(2)}) collective-permute-start(bf16[1,1024,1536]{2,1,0:T(8,128)(2,1)} %param.22), channel_id=1, source_target_pairs={{0,16},{16,0},{1,17},{17,1},{2,18},{18,2},{3,19},{19,3},{4,20},{20... | collective-permute-start | bytes 9437192 | tf_op jit(solution)/shard_map/ppermute | solution.py:71
  124.5 65.2 %collective-permute-start.11 = (bf16[1,4,128,2048]{3,2,1,0:T(8,128)(2,1)}, bf16[1,4,128,2048]{3,2,1,0:T(8,128)(2,1)S(1)}, u32[]{:S(2)}, u32[]{:S(2)}) collective-permute-start(bf16[1,4,128,2048]{3,2,1,0:T(8,128)(2,1)} %constant_dynamic-update-slice_fusion.5), channel_id=1, source_target_pairs={{0,16},{16,0},{1,17},{17,1},{2,18},{18,2},{3,19},{19,3},{4,20},{20... | collective-permute-start | bytes 6291464 | tf_op jit(solution)/shard_map/ppermute | solution.py:71
  156.2 33.2 %collective-permute-start.14 = (bf16[2,4,64,640]{3,2,0,1:T(8,128)(2,1)S(1)}, bf16[2,4,64,640]{3,2,0,1:T(8,128)(2,1)S(1)}, u32[]{:S(2)}, u32[]{:S(2)}) collective-permute-start(bf16[2,4,64,640]{3,2,0,1:T(8,128)(2,1)S(1)} %collective-permute-done.13), channel_id=1, source_target_pairs={{0,4},{4,8},{8,12},{12,0},{1,5},{5,9},{9,13},{13,1},{2,6},{6,10},{... | collective-permute-start | bytes 1966088 | tf_op jit(solution)/shard_map/ppermute | solution.py:84
  188.7 48.8 %collective-permute-start.36 = (bf16[2,128,384]{2,1,0:T(8,128)(2,1)}, bf16[2,128,384]{2,1,0:T(8,128)(2,1)}, u32[]{:S(2)}, u32[]{:S(2)}) collective-permute-start(bf16[2,128,384]{2,1,0:T(8,128)(2,1)} %pad_maximum_fusion.44), channel_id=1, source_target_pairs={{0,2},{1,3},{2,0},{3,1},{4,6},{5,7},{6,4},{7,5},{8,10},{9,11},{10,... | collective-permute-start | bytes 589832 | tf_op jit(solution)/shard_map/ppermute | solution.py:71
  189.4 52.1 %collective-permute-start.29 = (bf16[128,1280]{1,0:T(8,128)(2,1)}, bf16[128,1280]{1,0:T(8,128)(2,1)}, u32[]{:S(2)}, u32[]{:S(2)}) collective-permute-start(bf16[128,1280]{1,0:T(8,128)(2,1)} %collective-permute-done.28), channel_id=1, source_target_pairs={{0,4},{4,8},{8,12},{12,0},{1,5},{5,9},{9,13},{13,1},{2,6},{6,10},{... | collective-permute-start | bytes 983048 | tf_op jit(solution)/shard_map/ppermute | solution.py:84
  236.1 66.6 %collective-permute-start.21 = (bf16[1,4,128,2048]{2,3,1,0:T(8,128)(2,1)S(1)}, bf16[1,4,128,2048]{2,3,1,0:T(8,128)(2,1)}, u32[]{:S(2)}, u32[]{:S(2)}) collective-permute-start(bf16[1,4,128,2048]{2,3,1,0:T(8,128)(2,1)S(1)} %dynamic-slice_convert_fusion.2), channel_id=1, source_target_pairs={{0,16},{16,0},{1,17},{17,1},{2,18},{18,2},{3,19},{19,3},{4,20},{20... | collective-permute-start | bytes 6291464 | tf_op jit(solution)/shard_map/ppermute | solution.py:71
  239.4 34.2 %collective-permute-start.39 = (bf16[4,128,896]{2,1,0:T(8,128)(2,1)}, bf16[4,128,896]{2,1,0:T(8,128)(2,1)}, u32[]{:S(2)}, u32[]{:S(2)}) collective-permute-start(bf16[4,128,896]{2,1,0:T(8,128)(2,1)} %maximum_maximum_fusion.2), channel_id=1, source_target_pairs={{0,4},{4,8},{8,12},{12,0},{1,5},{5,9},{9,13},{13,1},{2,6},{6,10},{... | collective-permute-start | bytes 2752520 | tf_op jit(solution)/shard_map/ppermute | solution.py:84
  288.6 83.8 %collective-permute-start.32 = (bf16[2,4,128,640]{3,2,1,0:T(8,128)(2,1)}, bf16[2,4,128,640]{3,2,1,0:T(8,128)(2,1)}, u32[]{:S(2)}, u32[]{:S(2)}) collective-permute-start(bf16[2,4,128,640]{3,2,1,0:T(8,128)(2,1)} %pad_maximum_fusion.11), channel_id=1, source_target_pairs={{0,2},{1,3},{2,0},{3,1},{4,6},{5,7},{6,4},{7,5},{8,10},{9,11},{10,... | collective-permute-start | bytes 3932168 | tf_op jit(solution)/shard_map/ppermute | solution.py:71
  290.8 83.0 %collective-permute-start.34 = (bf16[2,4,128,640]{3,2,1,0:T(8,128)(2,1)}, bf16[2,4,128,640]{3,2,1,0:T(8,128)(2,1)}, u32[]{:S(2)}, u32[]{:S(2)}) collective-permute-start(bf16[2,4,128,640]{3,2,1,0:T(8,128)(2,1)} %pad_maximum_fusion.12), channel_id=1, source_target_pairs={{0,1},{1,0},{2,3},{3,2},{4,5},{5,4},{6,7},{7,6},{8,9},{9,8},{10,11... | collective-permute-start | bytes 3932168 | tf_op jit(solution)/shard_map/ppermute | solution.py:71
  296.1 93.4 %collective-permute-start.41 = (bf16[4,128,896]{2,1,0:T(8,128)(2,1)}, bf16[4,128,896]{2,1,0:T(8,128)(2,1)}, u32[]{:S(2)}, u32[]{:S(2)}) collective-permute-start(bf16[4,128,896]{2,1,0:T(8,128)(2,1)} %collective-permute-done.40), channel_id=1, source_target_pairs={{0,4},{4,8},{8,12},{12,0},{1,5},{5,9},{9,13},{13,1},{2,6},{6,10},{... | collective-permute-start | bytes 2752520 | tf_op jit(solution)/shard_map/ppermute | solution.py:84
  609.3 76.5 %collective-permute-start.60 = (bf16[4,2,128,640]{2,3,0,1:T(8,128)(2,1)}, bf16[4,2,128,640]{2,3,0,1:T(8,128)(2,1)}, u32[]{:S(2)}, u32[]{:S(2)}) collective-permute-start(bf16[4,2,128,640]{2,3,0,1:T(8,128)(2,1)} %pad_maximum_fusion.15), channel_id=1, source_target_pairs={{0,1},{1,0},{2,3},{3,2},{4,5},{5,4},{6,7},{7,6},{8,9},{9,8},{10,11... | collective-permute-start | bytes 3932168 | tf_op jit(solution)/shard_map/ppermute | solution.py:71
  612.2 58.0 %collective-permute-start.65 = (bf16[4,128,768]{1,2,0:T(8,128)(2,1)}, bf16[4,128,768]{1,2,0:T(8,128)(2,1)}, u32[]{:S(2)}, u32[]{:S(2)}) collective-permute-start(bf16[4,128,768]{1,2,0:T(8,128)(2,1)} %bitcast.761), channel_id=1, source_target_pairs={{0,12},{4,0},{8,4},{12,8},{1,13},{5,1},{9,5},{13,9},{2,14},{6,2},{... | collective-permute-start | bytes 2359304 | tf_op jit(solution)/shard_map/ppermute | solution.py:84
  617.1 72.5 %collective-permute-start.58 = (bf16[4,2,128,640]{2,3,0,1:T(8,128)(2,1)}, bf16[4,2,128,640]{2,3,0,1:T(8,128)(2,1)}, u32[]{:S(2)}, u32[]{:S(2)}) collective-permute-start(bf16[4,2,128,640]{2,3,0,1:T(8,128)(2,1)} %copy.437), channel_id=1, source_target_pairs={{0,2},{1,3},{2,0},{3,1},{4,6},{5,7},{6,4},{7,5},{8,10},{9,11},{10,... | collective-permute-start | bytes 3932168 | tf_op jit(solution)/shard_map/ppermute | solution.py:71
  620.9 66.8 %collective-permute-start.76 = (bf16[4,2,128,640]{2,3,0,1:T(8,128)(2,1)}, bf16[4,2,128,640]{2,3,0,1:T(8,128)(2,1)}, u32[]{:S(2)}, u32[]{:S(2)}) collective-permute-start(bf16[4,2,128,640]{2,3,0,1:T(8,128)(2,1)} %pad_maximum_fusion.16), channel_id=1, source_target_pairs={{0,1},{1,0},{2,3},{3,2},{4,5},{5,4},{6,7},{7,6},{8,9},{9,8},{10,11... | collective-permute-start | bytes 3932168 | tf_op jit(solution)/shard_map/ppermute | solution.py:71
  624.4 47.4 %collective-permute-start.81 = (bf16[4,128,896]{1,2,0:T(8,128)(2,1)}, bf16[4,128,896]{1,2,0:T(8,128)(2,1)}, u32[]{:S(2)}, u32[]{:S(2)}) collective-permute-start(bf16[4,128,896]{1,2,0:T(8,128)(2,1)} %fusion.75), channel_id=1, source_target_pairs={{0,12},{4,0},{8,4},{12,8},{1,13},{5,1},{9,5},{13,9},{2,14},{6,2},{... | collective-permute-start | bytes 2752520 | tf_op jit(solution)/shard_map/ppermute | solution.py:84
  671.8 288.1 %collective-permute-start.113 = (bf16[1,1024,1536]{2,1,0:T(8,128)(2,1)}, bf16[1,1024,1536]{2,1,0:T(8,128)(2,1)}, u32[]{:S(2)}, u32[]{:S(2)}) collective-permute-start(bf16[1,1024,1536]{2,1,0:T(8,128)(2,1)} %dynamic-slice_convert_fusion), channel_id=1, source_target_pairs={{0,16},{16,0},{1,17},{17,1},{2,18},{18,2},{3,19},{19,3},{4,20},{20... | collective-permute-start | bytes 9437192 | tf_op jit(solution)/shard_map/ppermute | solution.py:71
  689.6 36.7 %collective-permute-start.82 = (bf16[4,128,896]{1,2,0:T(8,128)(2,1)S(1)}, bf16[4,128,896]{1,2,0:T(8,128)(2,1)S(1)}, u32[]{:S(2)}, u32[]{:S(2)}) collective-permute-start(bf16[4,128,896]{1,2,0:T(8,128)(2,1)S(1)} %fusion.28), channel_id=1, source_target_pairs={{0,12},{4,0},{8,4},{12,8},{1,13},{5,1},{9,5},{13,9},{2,14},{6,2},{... | collective-permute-start | bytes 2752520 | tf_op jit(solution)/shard_map/ppermute | solution.py:84
  708.1 43.5 %collective-permute-start.59 = (bf16[4,128,640]{1,2,0:T(8,128)(2,1)S(1)}, bf16[4,128,640]{1,2,0:T(8,128)(2,1)S(1)}, u32[]{:S(2)}, u32[]{:S(2)}) collective-permute-start(bf16[4,128,640]{1,2,0:T(8,128)(2,1)S(1)} %slice_bitcast_fusion.8), channel_id=1, source_target_pairs={{0,1},{1,0},{2,3},{3,2},{4,5},{5,4},{6,7},{7,6},{8,9},{9,8},{10,11... | collective-permute-start | bytes 1966088 | tf_op jit(solution)/shard_map/ppermute | solution.py:71
  708.9 102.6 %collective-permute-start.67 = (bf16[4,128,768]{1,2,0:T(8,128)(2,1)S(1)}, bf16[4,128,768]{1,2,0:T(8,128)(2,1)S(1)}, u32[]{:S(2)}, u32[]{:S(2)}) collective-permute-start(bf16[4,128,768]{1,2,0:T(8,128)(2,1)S(1)} %fusion.34), channel_id=1, source_target_pairs={{0,12},{4,0},{8,4},{12,8},{1,13},{5,1},{9,5},{13,9},{2,14},{6,2},{... | collective-permute-start | bytes 2359304 | tf_op jit(solution)/shard_map/ppermute | solution.py:84
  728.6 49.7 %collective-permute-start.83 = (bf16[4,128,896]{1,2,0:T(8,128)(2,1)S(1)}, bf16[4,128,896]{1,2,0:T(8,128)(2,1)S(1)}, u32[]{:S(2)}, u32[]{:S(2)}) collective-permute-start(bf16[4,128,896]{1,2,0:T(8,128)(2,1)S(1)} %fusion.29), channel_id=1, source_target_pairs={{0,12},{4,0},{8,4},{12,8},{1,13},{5,1},{9,5},{13,9},{2,14},{6,2},{... | collective-permute-start | bytes 2752520 | tf_op jit(solution)/shard_map/ppermute | solution.py:84
  751.9 52.4 %collective-permute-start.62 = (bf16[128,1280]{0,1:T(8,128)(2,1)S(1)}, bf16[128,1280]{0,1:T(8,128)(2,1)S(1)}, u32[]{:S(2)}, u32[]{:S(2)}) collective-permute-start(bf16[128,1280]{0,1:T(8,128)(2,1)S(1)} %fusion.129), channel_id=1, source_target_pairs={{0,12},{4,0},{8,4},{12,8},{1,13},{5,1},{9,5},{13,9},{2,14},{6,2},{... | collective-permute-start | bytes 983048 | tf_op jit(solution)/shard_map/ppermute | solution.py:84
  805.0 46.9 %collective-permute-start.63 = (bf16[128,1280]{0,1:T(8,128)(2,1)}, bf16[128,1280]{0,1:T(8,128)(2,1)}, u32[]{:S(2)}, u32[]{:S(2)}) collective-permute-start(bf16[128,1280]{0,1:T(8,128)(2,1)} %fusion.82), channel_id=1, source_target_pairs={{0,12},{4,0},{8,4},{12,8},{1,13},{5,1},{9,5},{13,9},{2,14},{6,2},{... | collective-permute-start | bytes 983048 | tf_op jit(solution)/shard_map/ppermute | solution.py:84
  853.8 46.5 %collective-permute-start.64 = (bf16[128,1280]{0,1:T(8,128)(2,1)}, bf16[128,1280]{0,1:T(8,128)(2,1)S(1)}, u32[]{:S(2)}, u32[]{:S(2)}) collective-permute-start(bf16[128,1280]{0,1:T(8,128)(2,1)} %fusion.83), channel_id=1, source_target_pairs={{0,12},{4,0},{8,4},{12,8},{1,13},{5,1},{9,5},{13,9},{2,14},{6,2},{... | collective-permute-start | bytes 983048 | tf_op jit(solution)/shard_map/ppermute | solution.py:84
  902.7 43.1 %collective-permute-start.105 = (bf16[128,2048]{1,0:T(8,128)(2,1)S(1)}, bf16[128,2048]{1,0:T(8,128)(2,1)}, u32[]{:S(2)}, u32[]{:S(2)}) collective-permute-start(bf16[128,2048]{1,0:T(8,128)(2,1)S(1)} %fusion.65), channel_id=1, source_target_pairs={{0,12},{4,0},{8,4},{12,8},{1,13},{5,1},{9,5},{13,9},{2,14},{6,2},{... | collective-permute-start | bytes 1572872 | tf_op jit(solution)/shard_map/ppermute | solution.py:84
  944.4 46.1 %collective-permute-start.94 = (bf16[1,4,128,2048]{2,3,1,0:T(8,128)(2,1)}, bf16[1,4,128,2048]{2,3,1,0:T(8,128)(2,1)}, u32[]{:S(2)}, u32[]{:S(2)}) collective-permute-start(bf16[1,4,128,2048]{2,3,1,0:T(8,128)(2,1)} %dynamic-slice_convert_fusion.1), channel_id=1, source_target_pairs={{0,16},{16,0},{1,17},{17,1},{2,18},{18,2},{3,19},{19,3},{4,20},{20... | collective-permute-start | bytes 6291464 | tf_op jit(solution)/shard_map/ppermute | solution.py:71
  1059.3 39.4 %collective-permute-start.72 = (bf16[64,2048]{0,1:T(8,128)(2,1)}, bf16[64,2048]{0,1:T(8,128)(2,1)S(1)}, u32[]{:S(2)}, u32[]{:S(2)}) collective-permute-start(bf16[64,2048]{0,1:T(8,128)(2,1)} %get-tuple-element.156), channel_id=1, source_target_pairs={{0,0},{4,4},{16,8},{20,12},{8,16},{12,20},{24,24},{28,28},{1,1},{5... | collective-permute-start | bytes 786440 | tf_op jit(solution)/shard_map/ppermute | solution.py:171
  (257 other events, 3546.4 us)

commit v2 on v1

v2 whole, which is shorter than its diff:
```python
import jax
import jax.numpy as jnp
from jax import lax
from jax.experimental import pallas as pl
from jax.experimental.pallas import tpu as pltpu
from jax.sharding import Mesh, PartitionSpec as P

H = 32
KV = 4
HD = 128
TOPK = 8

eps_norm = 1e-06
rope_base = 1000000.0
neg_big = -1e30
f32 = jnp.float32
bf16 = jnp.bfloat16


def tie(*v):
    return lax.optimization_barrier(v)


def rms_scale(operand):
    return lax.rsqrt(jnp.mean(operand * operand, axis=-1, keepdims=True) + eps_norm)


def norm_back(operand, scale_rows, gain_vec, upstream):
    weighted = gain_vec * upstream
    inner_mean = jnp.mean(operand * weighted, axis=-1, keepdims=True)
    return scale_rows * weighted - operand * scale_rows * scale_rows * scale_rows * inner_mean


def rope_tables(positions, head_size):
    frequency = rope_base ** (-(jnp.arange(head_size // 2, dtype=f32) * 2.0 / head_size))
    angles = positions.astype(f32)[:, None] * frequency[None, :]
    angles = jnp.concatenate([angles, angles], axis=-1)
    return (jnp.cos(angles), jnp.sin(angles))


def rotate(operand, cosine, sine_table):
    half_width = operand.shape[-1] // 2
    turned = jnp.concatenate([-operand[..., half_width:], operand[..., :half_width]], axis=-1)
    return operand * cosine + turned * sine_table


def rotate_back(upstream, cosine, sine_table):
    shifted = upstream * sine_table
    half_width = upstream.shape[-1] // 2
    return upstream * cosine + jnp.concatenate(
        [shifted[..., half_width:], -shifted[..., :half_width]], axis=-1
    )


def dot(a, b):
    return jnp.dot(a, b, preferred_element_type=f32)


def dot_nt(a, b):
    return lax.dot_general(a, b, (((1,), (1,)), ((), ())), preferred_element_type=f32)


def dot_tn(a, b):
    return lax.dot_general(a, b, (((0,), (0,)), ((), ())), preferred_element_type=f32)


def take(v, index, axis=0):
    return lax.dynamic_index_in_dim(v, index, axis, keepdims=False)


def flip(v, axis, bit):
    n = lax.axis_size(axis)
    return lax.ppermute(v, axis, [(i, i ^ bit) for i in range(n)])


def px(v):
    return flip(v, "cl", 1)


def py(v):
    return flip(v, "cl", 2)


def shift(v, by):
    n = lax.axis_size("sq")
    return lax.ppermute(v, "sq", [(i, (i + by) % n) for i in range(n)])


def bits_of(axis):
    n, bit, out = lax.axis_size(axis), 1, []
    while bit < n:
        out.append(bit)
        bit *= 2
    return out


def every_gather(v):
    n = lax.axis_size("dp") * lax.axis_size("sq") * lax.axis_size("cl")
    v = jnp.broadcast_to(v[None], (n,) + v.shape)
    return lax.all_to_all(v, ("dp", "sq", "cl"), split_axis=0, concat_axis=0, tiled=True)


def every_scatter(v):
    v = lax.all_to_all(v, ("dp", "sq", "cl"), split_axis=0, concat_axis=0, tiled=True)
    return jnp.sum(v, axis=0)


def xor_groups(v, bit):
    rest = v.shape[1:]
    v = v.reshape((-1, 2, bit) + rest)
    return jnp.concatenate([v[:, 1:], v[:, :1]], axis=1).reshape((-1,) + rest)


def dp_gather(v):
    v = v[None]
    index = lax.axis_index("dp")
    for bit in bits_of("dp"):
        other = flip(v, "dp", bit)
        upper = (index & bit) != 0
        v = jnp.concatenate([jnp.where(upper, other, v), jnp.where(upper, v, other)], axis=0)
    return v


def dp_columns(v):
    v = v[None]
    index = lax.axis_index("dp")
    for bit in bits_of("dp"):
        other = flip(v, "dp", bit)
        other = jnp.swapaxes(xor_groups(jnp.swapaxes(other, 0, 1), bit), 0, 1)
        upper = (index & bit) != 0
        v = jnp.concatenate([jnp.where(upper, other, v), jnp.where(upper, v, other)], axis=0)
    return v


def dp_rows(v):
    v = v[None]
    for bit in bits_of("dp"):
        v = jnp.concatenate([v, flip(v, "dp", bit)], axis=0)
    return v


def dp_fold(parts):
    for bit in reversed(bits_of("dp")):
        parts = [
            parts[m].astype(f32) + flip(parts[m + bit].astype(bf16), "dp", bit).astype(f32)
            for m in range(bit)
        ]
    return parts[0]


def dp_sum(v):
    for bit in bits_of("dp"):
        v = v + xor_groups(flip(v.astype(bf16), "dp", bit), bit).astype(f32)
    return v


def to_sequence(v):
    nl, n_dp, n_sq = v.shape[0], lax.axis_size("dp"), lax.axis_size("sq")
    zi = lax.axis_index("sq")
    got = []
    for m in range(nl):
        pairs = [
            (d * n_sq + z, (z // nl) * n_sq + nl * d + (m + z) % nl)
            for d in range(n_dp)
            for z in range(n_sq)
        ]
        got.append(lax.ppermute(take(v, (m + zi) % nl), ("dp", "sq"), pairs))
    return jnp.stack(got)


def from_sequence(v):
    nl, n_dp, n_sq = v.shape[0], lax.axis_size("dp"), lax.axis_size("sq")
    zi = lax.axis_index("sq")
    got = []
    for m in range(nl):
        pairs = [
            ((z // nl) * n_sq + nl * d + (m + z) % nl, d * n_sq + z)
            for d in range(n_dp)
            for z in range(n_sq)
        ]
        got.append(lax.ppermute(v[m], ("dp", "sq"), pairs))
    got = jnp.stack(got)
    return jnp.stack([take(got, (j - zi) % nl) for j in range(nl)])


def head_pairs():
    n_dp, n_sq, n_cl = lax.axis_size("dp"), lax.axis_size("sq"), lax.axis_size("cl")
    pairs = []
    for f in range(n_dp * n_sq * n_cl):
        r, q = f // n_sq, f % n_sq
        pairs.append((f, ((r % n_dp) * n_sq + (q + r) % n_sq) * n_cl + r // n_dp))
    return pairs


def spread(v):
    h = v.shape[0] // 2
    a, b = v[:h], v[h:]
    a1, b1 = px(a), py(b)
    a2, b2 = py(a), px(b)
    a3, b3 = py(a1), px(b1)
    return [a, a1, a2, a3, b, b1, b2, b3]


def fold_first(v):
    ra, rb = py(v[:, 0, 2:].astype(bf16)), px(v[:, 1, 2:].astype(bf16))
    return v[:, :, :2], ra, rb


def fold_last(first):
    v, ra, rb = first
    a = v[:, 0].astype(f32) + ra.astype(f32)
    b = v[:, 1].astype(f32) + rb.astype(f32)
    a0 = a[:, 0] + px(a[:, 1].astype(bf16)).astype(f32)
    b0 = b[:, 0] + py(b[:, 1].astype(bf16)).astype(f32)
    return jnp.stack([a0, b0], axis=1)


def fold(v):
    return fold_last(fold_first(v[None]))[0]


def ring_gather(v):
    got = [v]
    for _ in range(lax.axis_size("sq") - 1):
        got.append(shift(got[-1], 1))
    return got


def ring_scatter(parts):
    moving = parts[1]
    for t in list(range(2, len(parts))) + [0]:
        got = shift(moving.astype(bf16), 1)
        moving = parts[t].astype(f32) + got.astype(f32)
    return moving


def pull_kernel(chosen, *refs):
    *pieces, main, tail = refs
    groups, slots = chosen.shape[:2]
    n = len(pieces) // groups
    width = main.shape[-1]
    for g in range(groups):
        rows = jnp.concatenate([piece[...] for piece in pieces[g * n : (g + 1) * n]], axis=0)
        got = jnp.dot(chosen[g], rows, preferred_element_type=f32).astype(bf16)
        main[pl.ds(g * slots, slots), :] = got[:, :width]
        tail[pl.ds(g * slots, slots), :] = got[:, width:]


def pull_pieces(chosen, pieces, width):
    slots = chosen.shape[0] * chosen.shape[1]
    rest = pieces[0].shape[1] - width
    return pl.pallas_call(
        pull_kernel,
        out_shape=(
            jax.ShapeDtypeStruct((slots, width), bf16),
            jax.ShapeDtypeStruct((slots, rest), bf16),
        ),
        name="pull",
    )(chosen, *pieces)


def pull_blocks_kernel(index, chosen, *refs):
    *blocks, out = refs
    rows = jnp.concatenate([block[0] for block in blocks], axis=0)
    out[...] = jnp.dot(chosen[0], rows, preferred_element_type=f32).astype(bf16)


def pull_blocks(index, chosen, blocks, width):
    groups, slots, depth = chosen.shape
    n = index.shape[1]
    block = (1, depth // n, width)
    specs = [pl.BlockSpec((1, slots, depth), lambda g, at: (g, 0, 0))]
    for i in range(n):
        specs.append(pl.BlockSpec(block, lambda g, at, i=i: (at[g, i], 0, 0)))
    return pl.pallas_call(
        pull_blocks_kernel,
        grid_spec=pltpu.PrefetchScalarGridSpec(
            num_scalar_prefetch=1,
            grid=(groups,),
            in_specs=specs,
            out_specs=pl.BlockSpec((slots, width), lambda g, at: (g, 0)),
        ),
        out_shape=jax.ShapeDtypeStruct((groups * slots, width), bf16),
        name="pull_blocks",
    )(index, chosen, *([blocks] * n))


def on_device(
    tokens,
    segment_ids,
    routes,
    cotangent,
    q_weight,
    k_weight,
    v_weight,
    o_weight,
    router_weight,
    norm_gains,
    gate_up_weight,
    down_weight,
):
    n_dp, n_sq, n_cl = lax.axis_size("dp"), lax.axis_size("sq"), lax.axis_size("cl")
    dp, zi, cl = lax.axis_index("dp"), lax.axis_index("sq"), lax.axis_index("cl")
    nl, bl, width = tokens.shape
    rows = nl * bl
    n_ctx = n_sq * n_cl
    length = bl * n_ctx
    n_all = n_dp * n_ctx
    tp = n_cl * n_dp
    experts = n_ctx
    expert = zi * n_cl + cl
    capacity = max(2, (5 * bl * TOPK + 4 * experts - 1) // (4 * experts))
    ff = down_weight.shape[1]
    heads = H // tp
    hw = heads * HD
    kvw = 2 * HD // n_dp
    pack = hw + kvw
    score_scale = HD ** (-0.5)
    shard = width // n_all

    hit = jnp.any(
        routes[:, :, :, None] == jnp.arange(experts, dtype=jnp.int32), axis=2
    ).astype(bf16)
    below = jnp.tril(jnp.ones((bl, bl), bf16), -1)
    earlier = jnp.einsum("pq,jqe->jpe", below, hit, preferred_element_type=f32)
    codes = jnp.where(hit > 0, jnp.minimum(earlier + 1.0, capacity + 1.0), 0.0).astype(bf16)
    codes = jnp.pad(codes, ((0, 0), (0, 0), (0, 128 - experts)))

    small = jnp.concatenate(
        [router_weight.T.reshape(-1), norm_gains.reshape(-1)]
    )
    n_small = small.shape[0]
    n_router = experts * shard
    small = jnp.pad(small, (0, -n_small % 128)).reshape(-1, 128)
    small = every_gather(small).reshape(n_all, -1)
    router_t = small[:, :n_router].reshape(n_all, experts, shard)
    router_t = jnp.transpose(router_t, (1, 0, 2)).reshape(experts, width)
    gains = small[:, n_router:n_small].reshape(-1).astype(f32)
    attn_gain = gains[:width]
    ffn_gain = gains[width : 2 * width]
    q_gain = gains[2 * width : 2 * width + HD]
    k_gain = gains[2 * width + HD :]

    inputs_low = to_sequence(tokens).reshape(rows, width)
    inputs = inputs_low.astype(f32)
    inputs_all = dp_rows(jnp.concatenate(spread(inputs_low))).reshape(length, width).astype(f32)

    kv_weight = jnp.concatenate(
        [k_weight.reshape(shard, n_cl, HD), v_weight.reshape(shard, n_cl, HD)], axis=-1
    )
    packed = jnp.concatenate(
        [
            q_weight.reshape(shard, n_cl, n_dp, hw),
            kv_weight.reshape(shard, n_cl, n_dp, kvw),
        ],
        axis=-1,
    )
    packed = jnp.transpose(packed, (1, 2, 0, 3)).reshape(tp, shard, pack)
    packed = lax.all_to_all(packed, ("cl", "dp"), split_axis=0, concat_axis=0, tiled=True)
    packed = jnp.transpose(packed.reshape(n_cl, n_dp, shard, pack), (1, 0, 2, 3))
    qkv_w = jnp.zeros((n_dp, n_sq, n_cl, shard, pack), bf16)
    rank = cl * n_dp + dp
    o_mine = lax.ppermute(o_weight, ("dp", "sq", "cl"), head_pairs())
    qkv_pieces = [packed, shift(packed, 1)]
    qkv_pieces[1], o_mine = tie(qkv_pieces[1], o_mine)
    for _ in range(2, n_sq):
        qkv_pieces.append(shift(qkv_pieces[-1], 1))

    upstream_low = jnp.concatenate([cotangent, codes], axis=-1)
    qkv_pieces[-2], upstream_low = tie(qkv_pieces[-2], upstream_low)
    qkv_pieces[-1] = shift(qkv_pieces[-2], 1)
    upstream_low = to_sequence(upstream_low).reshape(rows, -1)
    upstream = upstream_low[:, :width].astype(f32)
    own_codes = upstream_low[:, width : width + experts].astype(f32)
    qkv_pieces[-1], upstream_low, o_mine = tie(qkv_pieces[-1], upstream_low, o_mine)
    grads_all = lax.all_gather(upstream_low, ("sq", "cl"))
    o_pieces = [o_mine, shift(o_mine, 1)]
    for t, piece in enumerate(qkv_pieces):
        qkv_w = lax.dynamic_update_index_in_dim(qkv_w, piece, (zi - t) % n_sq, 1)
    qkv_w = qkv_w.reshape(width, pack)

    gu_full = dp_gather(gate_up_weight[0]).reshape(width, 2 * ff)
    down_full = jnp.concatenate(list(dp_gather(down_weight[0])), axis=1)

    order = jnp.array([[0, 1, 2, 3], [0, 2, 1, 3]], jnp.int32)
    chip_of = order ^ cl
    hb = nl // 2
    block_of = (zi - jnp.arange(nl).reshape(2, hb)) % nl
    d_ids = (jnp.arange(n_dp) ^ dp)[:, None, None, None]
    block_ids = (d_ids * nl + block_of[None, :, None, :]) * n_cl + chip_of[None, :, :, None]
    positions = block_ids[..., None] * bl + jnp.arange(bl)
    positions = positions.reshape(length).astype(jnp.int32)
    segments = take(dp_gather(segment_ids).reshape(n_dp * nl, length), zi)
    segments = segments.reshape(1, n_dp * nl * n_cl, bl)
    found = block_ids.reshape(-1, 1, 1) == jnp.arange(n_dp * nl * n_cl)[None, :, None]
    segments = jnp.sum(jnp.where(found, segments, 0), axis=1).reshape(length)
    cosine, sine_table = rope_tables(positions, HD)
    cosine, sine_table = cosine[:, None, :], sine_table[:, None, :]

    first_scale = rms_scale(inputs)
    inputs_all, gu_full, down_full = tie(inputs_all, gu_full, down_full)
    normed_all = (inputs_all * rms_scale(inputs_all) * attn_gain).astype(bf16)
    proj = dot(normed_all, qkv_w)
    q_proj = proj[:, :hw].reshape(length, heads, HD)
    kv_proj = dp_columns(proj[:, hw:].reshape(n_dp, -1, kvw)).reshape(n_dp, length, kvw)
    kv_proj = jnp.concatenate(list(kv_proj), axis=-1)
    k_proj = kv_proj[:, None, :HD]
    values = kv_proj[:, HD:].astype(bf16)
    q_scale = rms_scale(q_proj)
    k_scale = rms_scale(k_proj)
    queries = rotate(q_proj * q_scale * q_gain, cosine, sine_table).astype(bf16)
    keys = rotate(k_proj * k_scale * k_gain, cosine, sine_table).astype(bf16)[:, 0]
    queries, o_pieces[1] = tie(queries, o_pieces[1])
    o_pieces.append(shift(o_pieces[1], 1))
    values, o_pieces[2] = tie(values, o_pieces[2])
    for _ in range(3, n_sq):
        o_pieces.append(shift(o_pieces[-1], 1))
    allowed = (positions[None, :] <= positions[:, None]) & (
        segments[None, :] == segments[:, None]
    )
    scores = jnp.einsum("qhd,kd->hqk", queries, keys, preferred_element_type=f32) * score_scale
    scores = jnp.where(allowed[None], scores, neg_big)
    terms = jnp.exp(scores - jnp.max(scores, axis=-1, keepdims=True))
    probs = terms / jnp.sum(terms, axis=-1, keepdims=True)
    prob_low = probs.astype(bf16)
    attended = jnp.einsum("hqk,kd->qhd", prob_low, values, preferred_element_type=f32)
    attended = attended.reshape(length, hw).astype(bf16)
    attended, o_pieces[-1] = tie(attended, o_pieces[-1])
    o_full = jnp.zeros((n_sq,) + o_weight.shape, bf16)
    for t, piece in enumerate(o_pieces):
        o_full = lax.dynamic_update_index_in_dim(o_full, piece, (zi - t - rank) % n_sq, 0)
    o_full = o_full.reshape(hw, width)
    mixed = [dot(attended_m, o_full) for attended_m in attended.reshape(n_dp, -1, hw)]
    mixed = fold(dp_fold(mixed).reshape(2, n_cl, rows // 2, width)).reshape(rows, width)
    middle = inputs + mixed
    second_scale = rms_scale(middle)
    hidden = (middle * second_scale * ffn_gain).astype(bf16)
    logits = dot_nt(hidden, router_t)
    routed = own_codes > 0
    top = jnp.max(jnp.where(routed, logits, neg_big), axis=-1, keepdims=True)
    gate_terms = jnp.where(routed, jnp.exp(logits - top), 0.0)
    gates = gate_terms / jnp.sum(gate_terms, axis=-1, keepdims=True)
    gates_high = gates.astype(bf16)
    gates_low = (gates - gates_high.astype(f32)).astype(bf16)
    extra = jnp.pad(
        jnp.concatenate([gates_high, gates_low], axis=-1), ((0, 0), (0, 128 - 2 * experts))
    )
    hidden_wide = jnp.concatenate([hidden, extra], axis=-1)

    lanes = jnp.arange(128)
    half = rows // 2
    n_slot = n_cl * hb * capacity
    z_of = (zi - jnp.arange(n_sq)) % n_sq
    at = (z_of[:, None, None] * n_cl + chip_of) * 2 + jnp.arange(2)[:, None]
    at = at.reshape(2 * n_sq, n_cl).astype(jnp.int32)
    code = jnp.where(lanes == expert, grads_all[:, :, width:].astype(f32), 0.0)
    code = jnp.sum(code, axis=-1).reshape(1, n_ctx * 2, half)
    found = at.reshape(-1, 1, 1) == jnp.arange(n_ctx * 2)[:, None]
    code = jnp.sum(jnp.where(found, code, 0.0), axis=1)
    code = jnp.where(code <= capacity, code, 0.0).reshape(n_sq, 2, 1, n_cl * half)
    place = (jnp.arange(n_cl * half) // bl) * 128.0
    ids = jnp.arange(n_slot)
    ids = ((ids // capacity) * 128 + ids % capacity + 1).astype(f32)
    select = (jnp.where(code > 0, code + place, -1.0) == ids[:, None]).astype(bf16)
    pick = (lanes == expert) | (lanes == experts + expert)

    def push(chosen, v):
        v = v.reshape(chosen.shape[:2] + (-1,))
        got = jnp.einsum("grt,grd->gtd", chosen, v, preferred_element_type=f32)
        return got.astype(bf16)

    per = 2
    n_chunk = n_sq // per
    select = select.reshape(n_chunk, per * 2, n_slot, -1)
    grad_slots = pull_blocks(
        at, select.reshape((-1,) + select.shape[2:]), grads_all.reshape(n_ctx * 2, half, -1), width
    )
    grad_slots = list(grad_slots.reshape(n_chunk, -1, width))

    ins, actives, out_grads, gu_grads, backs = [], [], [], [], []
    arrived = []
    moving = hidden_wide
    for t in range(n_sq):
        arrived += spread(moving)
        if t == 0:
            moving, grad_slots = tie(shift(moving, 1), grad_slots)
        elif t + 1 < n_sq:
            moving = shift(moving, 1)
    for chunk in range(n_chunk):
        pieces = arrived[chunk * per * 8 : (chunk + 1) * per * 8]
        chosen = select[chunk]
        expert_in, gate_lanes = pull_pieces(chosen, pieces, width)
        gate_slot = jnp.sum(
            jnp.where(pick, gate_lanes.astype(f32), 0.0), axis=-1, keepdims=True
        )
        grad_slot = grad_slots[chunk].astype(f32)
        gate_up = dot(expert_in, gu_full)
        gate_part, up_part = gate_up[:, :ff], gate_up[:, ff:]
        sigmoid_gate = jax.nn.sigmoid(gate_part)
        activated = (gate_part * sigmoid_gate * up_part).astype(bf16)
        if chunk:
            activated, back_first = tie(activated, back_first)
            backs += list(fold_last(back_first))
        expert_out = dot(activated, down_full).astype(bf16)
        out_wide = expert_out.astype(f32)
        pair_grad = jnp.sum(grad_slot * out_wide, axis=-1, keepdims=True)
        out_grad = (gate_slot * grad_slot).astype(bf16)
        act_grad = dot_nt(out_grad, down_full)
        gate_back = act_grad * up_part * sigmoid_gate * (1.0 + gate_part * (1.0 - sigmoid_gate))
        up_back = act_grad * gate_part * sigmoid_gate
        gu_grad = jnp.concatenate([gate_back, up_back], axis=-1).astype(bf16)
        if chunk:
            gu_grad, backs = tie(gu_grad, backs)
        row_grad = dot_nt(gu_grad, gu_full).astype(bf16)
        pair_high = pair_grad.astype(bf16)
        pair_low = (pair_grad - pair_high.astype(f32)).astype(bf16)
        pair_extra = jnp.where(
            lanes == expert, pair_high, jnp.where(lanes == experts + expert, pair_low, 0)
        ).astype(bf16)
        moe = (gate_slot * out_wide).astype(bf16)
        back = push(chosen, jnp.concatenate([row_grad, moe, pair_extra], axis=-1))
        back_first = fold_first(back.reshape(per, 2, n_cl, half, -1))
        ins.append(expert_in)
        actives.append(activated)
        out_grads.append(out_grad)
        gu_grads.append(gu_grad)
    backs = [v.reshape(rows, -1) for v in backs + list(fold_last(back_first))]
    back = ring_scatter(backs).astype(bf16).astype(f32)
    output = (middle + back[:, width : 2 * width]).astype(bf16)

    pair_own = back[:, 2 * width :]
    pair_own = pair_own[:, :experts] + pair_own[:, experts : 2 * experts]
    chosen_grad = gates * (pair_own - jnp.sum(gates * pair_own, axis=-1, keepdims=True))
    logit_grad = chosen_grad.astype(bf16)
    hidden_grad = back[:, :width] + dot(logit_grad, router_t)
    router_grad = dot_tn(logit_grad, hidden)
    ffn_gain_grad = jnp.sum(hidden_grad * middle * second_scale, axis=0)
    middle_grad = upstream + norm_back(middle, second_scale, ffn_gain, hidden_grad)

    middle_low = dp_rows(jnp.concatenate(spread(middle_grad.astype(bf16)))).reshape(length, width)
    o_grad = dot_tn(attended, middle_low).reshape(n_sq, -1, width)
    attended_grad = dot_nt(middle_low, o_full).astype(bf16).reshape(length, heads, HD)
    attended_grad, o_grad = tie(attended_grad, o_grad)
    o_parts = [take(o_grad, (zi - t - rank) % n_sq) for t in range(n_sq)]
    o_got = shift(o_parts[1].astype(bf16), 1)
    prob_grad = jnp.einsum("qhd,kd->hqk", attended_grad, values, preferred_element_type=f32)
    inner_sum = jnp.sum(probs * prob_grad, axis=-1, keepdims=True)
    score_grad = (probs * (prob_grad - inner_sum)).astype(bf16)
    value_part = jnp.einsum("hqk,qhd->kd", prob_low, attended_grad, preferred_element_type=f32)
    key_part = (
        jnp.einsum("hqk,qhd->kd", score_grad, queries, preferred_element_type=f32) * score_scale
    )
    query_grad = (
        jnp.einsum("hqk,kd->qhd", score_grad, keys, preferred_element_type=f32) * score_scale
    )
    kv_sum = jnp.concatenate([key_part, value_part], axis=-1).reshape(n_dp, -1, 2 * HD)
    kv_sum, o_got = tie(kv_sum, o_got)
    o_got = o_parts[2].astype(f32) + o_got.astype(f32)
    o_got = shift(o_got.astype(bf16), 1)
    kv_sum = dp_sum(kv_sum).reshape(length, 2 * HD)
    query_grad, o_got = tie(query_grad, o_got)
    for t in list(range(3, n_sq)) + [0]:
        o_got = o_parts[t].astype(f32) + o_got.astype(f32)
        if t:
            o_got = shift(o_got.astype(bf16), 1)
    o_share = lax.ppermute(
        o_got.astype(bf16), ("dp", "sq", "cl"), [(b, a) for a, b in head_pairs()]
    ).astype(f32)
    key_rot_grad = rotate_back(kv_sum[:, None, :HD], cosine, sine_table)
    k_gain_grad = jnp.sum(key_rot_grad * k_proj * k_scale, axis=(0, 1))
    k_gain_grad = jnp.where(dp == 0, k_gain_grad, 0.0)
    k_low = norm_back(k_proj, k_scale, k_gain, key_rot_grad)[:, 0].astype(bf16)
    kv_low = jnp.concatenate([k_low, kv_sum[:, HD:].astype(bf16)], axis=-1)
    kv_low = lax.dynamic_slice_in_dim(kv_low, dp * kvw, kvw, 1)
    query_rot_grad = rotate_back(query_grad, cosine, sine_table)
    q_gain_grad = jnp.sum(query_rot_grad * q_proj * q_scale, axis=(0, 1))
    q_low = norm_back(q_proj, q_scale, q_gain, query_rot_grad).reshape(length, hw).astype(bf16)
    qkv_low = jnp.concatenate([q_low, kv_low], axis=-1)
    qkv_low, gu_grads, out_grads = tie(qkv_low, gu_grads, out_grads)
    w_grad = dot_tn(normed_all, qkv_low).reshape(n_dp, n_sq, n_cl, shard, pack)
    w_parts = [take(w_grad, (zi - t) % n_sq, 1) for t in range(n_sq)]
    w_got = shift(w_parts[1].astype(bf16), 1)
    normed_grad = [dot_nt(low_m, qkv_w) for low_m in qkv_low.reshape(n_dp, -1, pack)]
    normed_first = fold_first(dp_fold(normed_grad).reshape(1, 2, n_cl, rows // 2, width))
    normed_first, w_got = tie(normed_first, w_got)
    w_got = shift((w_parts[2] + w_got.astype(f32)).astype(bf16), 1)
    normed_grad = fold_last(normed_first).reshape(rows, width)
    normed_grad, w_got = tie(normed_grad, w_got)
    for t in range(3, n_sq):
        w_got = shift((w_parts[t] + w_got.astype(f32)).astype(bf16), 1)
    attn_gain_grad = jnp.sum(normed_grad * inputs * first_scale, axis=0)
    input_grad = middle_grad + norm_back(inputs, first_scale, attn_gain, normed_grad)
    input_grad = from_sequence(input_grad.astype(bf16).reshape(nl, bl, width))
    output = from_sequence(output.reshape(nl, bl, width))

    gu_grad = jnp.concatenate(gu_grads)
    activated = jnp.concatenate(actives)

    def columns(parts, m):
        size = width // n_dp
        at = (dp ^ m) * size
        return jnp.concatenate([lax.dynamic_slice_in_dim(v, at, size, 1) for v in parts])

    gu_share = dp_fold([dot_tn(columns(ins, m), gu_grad) for m in range(n_dp)])
    down_share = dp_fold([dot_tn(activated, columns(out_grads, m)) for m in range(n_dp)])

    w_grad = (w_parts[0] + w_got.astype(f32)).astype(bf16)
    w_grad = jnp.transpose(w_grad, (1, 0, 2, 3)).reshape(tp, shard, pack)
    w_grad = lax.all_to_all(w_grad, ("cl", "dp"), split_axis=0, concat_axis=0, tiled=True)
    w_grad = jnp.transpose(w_grad.reshape(n_cl, n_dp, shard, pack), (2, 0, 1, 3)).astype(f32)
    q_share = w_grad[..., :hw].reshape(shard, -1)
    kv_share = w_grad[..., hw:].reshape(shard, n_cl, 2 * HD)
    k_share = kv_share[..., :HD].reshape(shard, -1)
    v_share = kv_share[..., HD:].reshape(shard, -1)

    gain_grads = jnp.concatenate([attn_gain_grad, ffn_gain_grad, q_gain_grad, k_gain_grad])
    router_grad = jnp.transpose(router_grad.reshape(experts, n_all, shard), (1, 0, 2))
    small_grad = jnp.concatenate(
        [router_grad.reshape(n_all, n_router), gain_grads.reshape(n_all, -1)], axis=-1
    )
    small_grad = jnp.pad(small_grad, ((0, 0), (0, -n_small % 128))).reshape(n_all, -1, 128)
    small_grad = every_scatter(small_grad).reshape(-1)
    router_share = small_grad[:n_router].reshape(experts, shard).T
    gains_share = small_grad[n_router:n_small]
    return (
        output,
        input_grad,
        q_share,
        k_share,
        v_share,
        o_share,
        router_share,
        gains_share,
        gu_share[None],
        down_share[None],
    )


def solution(mesh):
    n_dp, n_ctx = mesh.devices.shape
    n_cl = KV
    fine = Mesh(mesh.devices.reshape(n_dp, n_ctx // n_cl, n_cl), ("dp", "sq", "cl"))
    ctx = ("sq", "cl")
    every = ("dp", "sq", "cl")
    rows = P("dp", ctx, None)
    placed = (
        rows,
        P("dp", None),
        rows,
        rows,
        P(every, None),
        P(every, None),
        P(every, None),
        P(every, None),
        P(every, None),
        P(every),
        P(ctx, "dp", None),
        P(ctx, None, "dp"),
    )
    return jax.shard_map(
        on_device,
        mesh=fine,
        in_specs=placed,
        out_specs=(
            rows,
            rows,
            P(every, None),
            P(every, None),
            P(every, None),
            P(every, None),
            P(every, None),
            P(every),
            P(ctx, "dp", None),
            P(ctx, None, "dp"),
        ),
        check_vma=False,
    )
```

time: 1120 us -> 886 us (0.79)
  other arithmetic: 213 us -> 87.2 us
  local copies, waits for them, and re-layouts: 211 us -> 88.6 us
  Pallas kernels: 0 us -> 19.5 us
  matrix products: 153 us -> 139 us
  between operations: 4.08 us -> 16.8 us
    ppermute x36 -> x18, waiting for transfers between devices: 214 us -> 135 us  [shift(): return lax.ppermute(v, 'sq', [(i, (i + by) % n) for i in range(n)])]
    ppermute x69 -> x63, waiting for transfers between devices: 110 us -> 165 us  [flip(): return lax.ppermute(v, axis, [(i, i ^ bit) for i in range(n)])]
    concatenate x13 -> x12, other arithmetic: 57.1 us -> 12.8 us  [the longest x2 4.73 us: dp_rows(): v = jnp.concatenate([v, flip(v, 'dp', bit)], axis=0)]
    ppermute x4, waiting for transfers between devices: 32 us -> 2.58 us  [from_sequence(): got.append(lax.ppermute(v[m], ('dp', 'sq'), pairs))]
    unnamed x367 -> x267, local copies, waits for them, and re-layouts: 59.3 us -> 31 us
    concatenate x2 -> x3, local copies, waits for them, and re-layouts: 23.2 us -> 0.87 us  [the longest x1 0.72 us: on_device(): jnp.concatenate(spread(middle_grad.astype(bf16)))]
    ppermute x4, waiting for transfers between devices: 0.01 us -> 20.6 us  [to_sequence(): got.append(lax.ppermute(take(v, (m + zi) % nl), ('dp', 'sq'), pairs))]
    all_to_all x0 -> x2, waiting for transfers between devices: none -> 20.6 us  [the longest x1 19.7 us: every_gather(): lax.all_to_all(v, ('dp', 'sq', 'cl'), split_axis=0, concat_axis=0, tiled=...]
  transfers between devices with their start and end apart: 117 -> 96, of which waited for: 51 -> 43; matrix products, arithmetic and copies ran while one was open for 33% -> 28% of each run, Pallas kernels for 0% -> 2%
where the time goes in v2:
time: 886 us; the launch traced here: 875 us
  waiting for transfers between devices  351 us (40%)
  starting transfers between devices  172 us (19%)
  matrix products  139 us (16%)
  local copies, waits for them, and re-layouts  88.6 us (10%)
  other arithmetic  87.2 us (10%)
  Pallas kernels  19.5 us (2%)
  between operations  16.8 us (2%)
    ppermute x63, waiting for transfers between devices, flip(): return lax.ppermute(v, axis, [(i, i ^ bit) for i in range(n)])  165 us
    ppermute x18, waiting for transfers between devices, shift(): return lax.ppermute(v, 'sq', [(i, (i + by) % n) for i in range(n)])  135 us
    ppermute x63, starting transfers between devices, flip(): return lax.ppermute(v, axis, [(i, i ^ bit) for i in range(n)])  82.6 us
    dot_general x8, matrix products, dot_nt(): lax.dot_general(a, b, (((1,), (1,)), ((), ())), preferred_element_type=f32)  32.5 us
    ppermute x18, starting transfers between devices, shift(): return lax.ppermute(v, 'sq', [(i, (i + by) % n) for i in range(n)])  32.2 us
    dot_general x8, matrix products, dot(): return jnp.dot(a, b, preferred_element_type=f32)  31.2 us
    unnamed x267, local copies, waits for them, and re-layouts  31 us
    dot_general x7, matrix products, dot_tn(): lax.dot_general(a, b, (((0,), (0,)), ((), ())), preferred_element_type=f32)  29.3 us
  transfers between devices with their start and end apart: 96, of which 43 were waited for; matrix products, arithmetic and copies ran while one was open for 28% of the time, Pallas kernels for 2%

profile of v2, /device:TPU:1, one launch (start us, length us, event | category | flops | bytes accessed | tf_op | source)
XLA Modules:
  0.0 875.0 jit_solution(1651441627245315938)
XLA Ops:
  32.5 19.7 %all-to-all-done = bf16[32,10,128]{2,1,0:T(8,128)(2,1)S(1)} async-done(((bf16[32,10,128]{2,1,0:T(8,128)(2,1)}), bf16[32,10,128]{2,1,0:T(8,128)(2,1)S(1)}, u32[]{:S(2)}, u32[]{:S(2)}) %all-to-all-start) | async-done | bytes 81952 | tf_op jit(solution)/shard_map/all_to_all | solution.py:100
  60.3 11.8 %collective-permute-done.2 = bf16[64,2048]{1,0:T(8,128)(2,1)} collective-permute-done((bf16[64,2048]{1,0:T(8,128)(2,1)S(1)}, bf16[64,2048]{1,0:T(8,128)(2,1)}, u32[]{:S(2)}, u32[]{:S(2)}) %collective-permute-start.2) | collective-permute-done | bytes 262176 | tf_op jit(solution)/shard_map/ppermute | solution.py:73
  87.3 13.4 %collective-permute-done.11 = bf16[2,4,64,640]{3,2,0,1:T(8,128)(2,1)S(1)} collective-permute-done((bf16[2,4,64,640]{3,2,0,1:T(8,128)(2,1)}, bf16[2,4,64,640]{3,2,0,1:T(8,128)(2,1)S(1)}, u32[]{:S(2)}, u32[]{:S(2)}) %collective-permute-start.11) | collective-permute-done | bytes 655392 | tf_op jit(solution)/shard_map/ppermute | solution.py:86
  105.4 11.6 %collective-permute-done.13 = bf16[2,4,64,640]{3,2,0,1:T(8,128)(2,1)S(1)} collective-permute-done((bf16[2,4,64,640]{3,2,0,1:T(8,128)(2,1)S(1)}, bf16[2,4,64,640]{3,2,0,1:T(8,128)(2,1)S(1)}, u32[]{:S(2)}, u32[]{:S(2)}) %collective-permute-start.13) | collective-permute-done | bytes 655392 | tf_op jit(solution)/shard_map/ppermute | solution.py:86
  124.8 20.6 %collective-permute-done.15 = bf16[64,2176]{1,0:T(8,128)(2,1)S(1)} collective-permute-done((bf16[64,2176]{1,0:T(8,128)(2,1)S(1)}, bf16[64,2176]{1,0:T(8,128)(2,1)S(1)}, u32[]{:S(2)}, u32[]{:S(2)}) %collective-permute-start.15) | collective-permute-done | bytes 278560 | tf_op jit(solution)/shard_map/ppermute | solution.py:167
  158.6 6.3 broadcast_select_fusion.1
  186.2 10.9 %fusion.193 = (f32[4,1024]{1,0:T(4,128)S(1)}, f32[4,1024,1024]{1,2,0:T(8,128)}) fusion(pred[1024,1024]{0,1:T(8,128)(4,1)} %compare_and_fusion, bf16[1024,128,1]{0,1,2:T(8,128)(2,1)S(1)} %copy-done.53, bf16[1024,4,128]{0,2,1:T(8,128)(2,1)} %fusion.51), kind=kOutput, calls=%fused_computation.475 | convolution fusion | flops 1090520064 | bytes 19152896 | tf_op jit(solution)/shard_map/sub | solution.py:423
  199.1 14.0 %collective-permute-done.19 = bf16[128,2048]{1,0:T(8,128)(2,1)} collective-permute-done((bf16[128,2048]{1,0:T(8,128)(2,1)}, bf16[128,2048]{1,0:T(8,128)(2,1)}, u32[]{:S(2)}, u32[]{:S(2)}) %collective-permute-start.19) | collective-permute-done | bytes 524320 | tf_op jit(solution)/shard_map/ppermute | solution.py:86
  217.1 7.2 fusion.59
  225.9 10.6 %collective-permute-done.21 = bf16[128,2048]{1,0:T(8,128)(2,1)S(1)} collective-permute-done((bf16[128,2048]{1,0:T(8,128)(2,1)}, bf16[128,2048]{1,0:T(8,128)(2,1)S(1)}, u32[]{:S(2)}, u32[]{:S(2)}) %collective-permute-start.21) | collective-permute-done | bytes 524320 | tf_op jit(solution)/shard_map/ppermute | solution.py:86
  255.1 13.9 %collective-permute-done.23 = bf16[1,2,64,2048]{3,2,1,0:T(8,128)(2,1)S(1)} collective-permute-done((bf16[1,2,64,2048]{3,2,1,0:T(8,128)(2,1)S(1)}, bf16[1,2,64,2048]{3,2,1,0:T(8,128)(2,1)S(1)}, u32[]{:S(2)}, u32[]{:S(2)}) %collective-permute-start.23) | collective-permute-done | bytes 524320 | tf_op jit(solution)/shard_map/ppermute | solution.py:73
  300.9 9.8 %pull_blocks.1 = bf16[1280,2048]{1,0:T(8,128)(2,1)} custom-call(s32[8,4]{1,0:T(8,128)} %multiply_add_fusion.index, bf16[8,160,256]{2,1,0:T(8,128)(2,1)} %compare_convert_fusion.chosen, bf16[32,64,2176]{2,1,0:T(8,128)(2,1)} %bitcast.485, bf16[32,64,2176]{2,1,0:T(8,128)(2,1)} %bitcast.486, bf16[32,64,2176]{2,1,0:T(8,128)(2,1)} %bitcast.487, ...), custom_call_target="tpu_custom_call" | custom-call | tf_op jit(solution)/shard_map/pull_blocks/pallas_call | solution.py:275
  359.0 9.7 %fusion.195 = f32[640,1536]{1,0:T(8,128)} fusion(bf16[640,2048]{1,0:T(8,128)(2,1)} %get-tuple-element.79, bf16[2048,1536]{1,0:T(8,128)(2,1)} %bitcast.525), kind=kOutput, calls=%fused_computation.477 | convolution fusion | flops 4026531840 | bytes 12845056 | tf_op jit(solution)/shard_map/dot_general | solution.py:56
  381.0 6.0 multiply_convert_fusion.3
  414.2 18.7 %collective-permute-done.54 = bf16[2,2,64,4224]{3,2,0,1:T(8,128)(2,1)} collective-permute-done((bf16[2,2,64,4224]{3,2,0,1:T(8,128)(2,1)}, bf16[2,2,64,4224]{3,2,0,1:T(8,128)(2,1)}, u32[]{:S(2)}, u32[]{:S(2)}) %collective-permute-start.54) | collective-permute-done | bytes 2162720 | tf_op jit(solution)/shard_map/ppermute | solution.py:73
  446.1 14.5 %collective-permute-done.57 = bf16[2,64,4224]{2,1,0:T(8,128)(2,1)S(1)} collective-permute-done((bf16[2,64,4224]{2,1,0:T(8,128)(2,1)S(1)}, bf16[2,64,4224]{2,1,0:T(8,128)(2,1)S(1)}, u32[]{:S(2)}, u32[]{:S(2)}) %collective-permute-start.57) | collective-permute-done | bytes 1081376 | tf_op jit(solution)/shard_map/ppermute | solution.py:73
  481.3 27.0 %collective-permute-done.58 = bf16[2,2,64,4224]{3,2,0,1:T(8,128)(2,1)S(1)} collective-permute-done((bf16[2,2,64,4224]{3,2,0,1:T(8,128)(2,1)S(1)}, bf16[2,2,64,4224]{3,2,0,1:T(8,128)(2,1)S(1)}, u32[]{:S(2)}, u32[]{:S(2)}) %collective-permute-start.58) | collective-permute-done | bytes 2162720 | tf_op jit(solution)/shard_map/ppermute | solution.py:73
  510.7 24.0 %collective-permute-done.59 = bf16[2,64,4224]{2,1,0:T(8,128)(2,1)S(1)} collective-permute-done((bf16[2,64,4224]{2,1,0:T(8,128)(2,1)S(1)}, bf16[2,64,4224]{2,1,0:T(8,128)(2,1)S(1)}, u32[]{:S(2)}, u32[]{:S(2)}) %collective-permute-start.59) | collective-permute-done | bytes 1081376 | tf_op jit(solution)/shard_map/ppermute | solution.py:73
  540.4 13.4 %collective-permute-done.63 = bf16[128,4224]{1,0:T(8,128)(2,1)S(1)} collective-permute-done((bf16[128,4224]{1,0:T(8,128)(2,1)S(1)}, bf16[128,4224]{1,0:T(8,128)(2,1)S(1)}, u32[]{:S(2)}, u32[]{:S(2)}) %collective-permute-start.63) | collective-permute-done | bytes 1081376 | tf_op jit(solution)/shard_map/ppermute | solution.py:86
  555.2 25.1 %collective-permute-done.64 = bf16[128,4224]{1,0:T(8,128)(2,1)S(1)} collective-permute-done((bf16[128,4224]{1,0:T(8,128)(2,1)S(1)}, bf16[128,4224]{1,0:T(8,128)(2,1)S(1)}, u32[]{:S(2)}, u32[]{:S(2)}) %collective-permute-start.64) | collective-permute-done | bytes 1081376 | tf_op jit(solution)/shard_map/ppermute | solution.py:86
  599.3 20.9 %collective-permute-start.73 = (bf16[1,512,2048]{2,1,0:T(8,128)(2,1)}, bf16[1,512,2048]{2,1,0:T(8,128)(2,1)}, u32[]{:S(2)}, u32[]{:S(2)}) collective-permute-start(bf16[1,512,2048]{2,1,0:T(8,128)(2,1)} %bitcast.103), channel_id=1, source_target_pairs={{0,16},{16,0},{1,17},{17,1},{2,18},{18,2},{3,19},{19,3},{4,20},{20... | collective-permute-start | bytes 6291464 | tf_op jit(solution)/shard_map/ppermute | solution.py:73
  639.2 10.5 %fusion.1 = (f32[4,1024]{1,0:T(4,128)S(1)}, f32[1024,1024,4]{1,0,2:T(8,128)}) fusion(f32[4,1024,1024]{1,2,0:T(8,128)S(1)} %bitcast.500, f32[4,1024]{1,0:T(4,128)S(1)} %copy-done.88, bf16[1024,4,128]{0,2,1:T(8,128)(2,1)} %bitcast.583, bf16[1024,128]{0,1:T(8,128)(2,1)} %copy-done.76), kind=kOutput, calls=%fused_computation.3 | convolution fusion | flops 1086320640 | bytes 34897920 | tf_op jit(solution)/shard_map/qhd,kd->hqk/dot_general | solution.py:546
  655.0 8.0 fusion.3
  681.5 10.8 %collective-permute-done.75 = bf16[128,2048]{1,0:T(8,128)(2,1)S(1)} collective-permute-done((bf16[128,2048]{1,0:T(8,128)(2,1)S(1)}, bf16[128,2048]{1,0:T(8,128)(2,1)S(1)}, u32[]{:S(2)}, u32[]{:S(2)}) %collective-permute-start.75) | collective-permute-done | bytes 524320 | tf_op jit(solution)/shard_map/ppermute | solution.py:86
  724.4 10.7 %collective-permute-done.87 = bf16[128,2048]{1,0:T(8,128)(2,1)S(1)} collective-permute-done((bf16[128,2048]{1,0:T(8,128)(2,1)S(1)}, bf16[128,2048]{1,0:T(8,128)(2,1)S(1)}, u32[]{:S(2)}, u32[]{:S(2)}) %collective-permute-start.87) | collective-permute-done | bytes 524320 | tf_op jit(solution)/shard_map/ppermute | solution.py:86
  739.6 6.7 collective-permute-done.88
  752.0 15.8 %collective-permute-start.78 = (bf16[1,2,64,2048]{3,2,1,0:T(8,128)(2,1)S(1)}, bf16[1,2,64,2048]{3,2,1,0:T(8,128)(2,1)S(1)}, u32[]{:S(2)}, u32[]{:S(2)}) collective-permute-start(bf16[1,2,64,2048]{3,2,1,0:T(8,128)(2,1)S(1)} %get-tuple-element.170), channel_id=1, source_target_pairs={{0,2},{1,3},{2,0},{3,1},{4,6},{5,7},{6,4},{7,5},{8,10},{9,11},{10,... | collective-permute-start | bytes 1572872 | tf_op jit(solution)/shard_map/ppermute | solution.py:73
  775.1 18.0 %collective-permute-start.65 = (bf16[64,2048]{1,0:T(8,128)(2,1)S(1)}, bf16[64,2048]{1,0:T(8,128)(2,1)}, u32[]{:S(2)}, u32[]{:S(2)}) collective-permute-start(bf16[64,2048]{1,0:T(8,128)(2,1)S(1)} %copy-done.77), channel_id=1, source_target_pairs={{0,0},{4,4},{16,8},{20,12},{8,16},{12,20},{24,24},{28,28},{1,1},{5... | collective-permute-start | bytes 786440 | tf_op jit(solution)/shard_map/ppermute | solution.py:181
  798.3 6.2 collective-permute-done.81
  804.9 8.0 collective-permute-done.82
  814.8 7.7 add_bitcast_fusion
  835.7 13.1 %collective-permute-done.86 = bf16[2,4,64,640]{3,2,0,1:T(8,128)(2,1)S(1)} collective-permute-done((bf16[2,4,64,640]{3,2,0,1:T(8,128)(2,1)S(1)}, bf16[2,4,64,640]{3,2,0,1:T(8,128)(2,1)S(1)}, u32[]{:S(2)}, u32[]{:S(2)}) %collective-permute-start.86) | collective-permute-done | bytes 655392 | tf_op jit(solution)/shard_map/ppermute | solution.py:86
  (703 shorter events, 433.3 us)
Async XLA Ops:
  8.4 48.9 %collective-permute-start = (bf16[64,2048]{1,0:T(8,128)(2,1)S(1)}, bf16[64,2048]{1,0:T(8,128)(2,1)S(1)}, u32[]{:S(2)}, u32[]{:S(2)}) collective-permute-start(bf16[64,2048]{1,0:T(8,128)(2,1)S(1)} %get-tuple-element.210), channel_id=1, source_target_pairs={{0,0},{4,4},{8,16},{12,20},{16,8},{20,12},{24,24},{28,28},{1,1},{5... | collective-permute-start | bytes 786440 | tf_op jit(solution)/shard_map/ppermute | solution.py:167
  14.0 46.0 %collective-permute-start.1 = (bf16[64,2048]{1,0:T(8,128)(2,1)S(1)}, bf16[64,2048]{1,0:T(8,128)(2,1)S(1)}, u32[]{:S(2)}, u32[]{:S(2)}) collective-permute-start(bf16[64,2048]{1,0:T(8,128)(2,1)S(1)} %get-tuple-element.211), channel_id=1, source_target_pairs={{0,4},{4,0},{8,20},{12,16},{16,12},{20,8},{24,28},{28,24},{1,5},{5... | collective-permute-start | bytes 786440 | tf_op jit(solution)/shard_map/ppermute | solution.py:167
  15.1 88.4 %collective-permute-start.10 = (bf16[1,768,1024]{2,1,0:T(8,128)(2,1)}, bf16[1,768,1024]{2,1,0:T(8,128)(2,1)}, u32[]{:S(2)}, u32[]{:S(2)}) collective-permute-start(bf16[1,768,1024]{2,1,0:T(8,128)(2,1)} %param.24), channel_id=1, source_target_pairs={{0,16},{16,0},{1,17},{17,1},{2,18},{18,2},{3,19},{19,3},{4,20},{20... | collective-permute-start | bytes 4718600 | tf_op jit(solution)/shard_map/ppermute | solution.py:73
  15.1 72.2 %collective-permute-start.12 = (bf16[128,2048]{1,0:T(8,128)(2,1)}, bf16[128,2048]{1,0:T(8,128)(2,1)}, u32[]{:S(2)}, u32[]{:S(2)}) collective-permute-start(bf16[128,2048]{1,0:T(8,128)(2,1)} %param.20), channel_id=1, source_target_pairs={{0,0},{1,4},{2,8},{3,12},{4,20},{5,24},{6,28},{7,16},{8,9},{9,13},... | collective-permute-start | bytes 1572872 | tf_op jit(solution)/shard_map/ppermute | solution.py:363
  20.7 31.5 %all-to-all-start = ((bf16[32,10,128]{2,1,0:T(8,128)(2,1)}), bf16[32,10,128]{2,1,0:T(8,128)(2,1)S(1)}, u32[]{:S(2)}, u32[]{:S(2)}) async-start(bf16[32,10,128]{2,1,0:T(8,128)(2,1)} %broadcast_in_dim.247), calls=%async_computation | async-start | bytes 262144 | tf_op jit(solution)/shard_map/all_to_all | solution.py:100
  52.2 27.2 %all-to-all-start.1 = ((bf16[8,64,640]{2,1,0:T(8,128)(2,1)}), bf16[8,64,640]{2,1,0:T(8,128)(2,1)}, u32[]{:S(2)}, u32[]{:S(2)}) async-start(bf16[8,64,640]{2,1,0:T(8,128)(2,1)} %bitcast.13), calls=%async_computation.1 | async-start | bytes 1310720 | tf_op jit(solution)/shard_map/all_to_all | solution.py:359
  57.1 241.1 %all-gather.3.cloned.1.call-start = ((), (), s32[]{:S(2)}) async-start(), calls=%async_computation.4 | async-start | bytes 9469952 | tf_op jit(solution)/shard_map/all_gather | solution.py:376
  85.0 73.6 %collective-permute-start.9 = (bf16[1,1024,1536]{2,1,0:T(8,128)(2,1)}, bf16[1,1024,1536]{2,1,0:T(8,128)(2,1)}, u32[]{:S(2)}, u32[]{:S(2)}) collective-permute-start(bf16[1,1024,1536]{2,1,0:T(8,128)(2,1)} %param.23), channel_id=1, source_target_pairs={{0,16},{16,0},{1,17},{17,1},{2,18},{18,2},{3,19},{19,3},{4,20},{20... | collective-permute-start | bytes 9437192 | tf_op jit(solution)/shard_map/ppermute | solution.py:73
  100.7 54.6 %collective-permute-start.8 = (bf16[1,512,2048]{2,1,0:T(8,128)(2,1)S(1)}, bf16[1,512,2048]{2,1,0:T(8,128)(2,1)}, u32[]{:S(2)}, u32[]{:S(2)}) collective-permute-start(bf16[1,512,2048]{2,1,0:T(8,128)(2,1)S(1)} %bitcast.553), channel_id=1, source_target_pairs={{0,16},{16,0},{1,17},{17,1},{2,18},{18,2},{3,19},{19,3},{4,20},{20... | collective-permute-start | bytes 6291464 | tf_op jit(solution)/shard_map/ppermute | solution.py:73
  117.0 28.4 %collective-permute-start.15 = (bf16[64,2176]{1,0:T(8,128)(2,1)S(1)}, bf16[64,2176]{1,0:T(8,128)(2,1)S(1)}, u32[]{:S(2)}, u32[]{:S(2)}) collective-permute-start(bf16[64,2176]{1,0:T(8,128)(2,1)S(1)} %get-tuple-element.189), channel_id=1, source_target_pairs={{0,0},{4,4},{8,16},{12,20},{16,8},{20,12},{24,24},{28,28},{1,1},{5... | collective-permute-start | bytes 835592 | tf_op jit(solution)/shard_map/ppermute | solution.py:167
  147.1 38.2 %collective-permute-start.18 = (bf16[128,2048]{1,0:T(8,128)(2,1)}, bf16[128,2048]{1,0:T(8,128)(2,1)}, u32[]{:S(2)}, u32[]{:S(2)}) collective-permute-start(bf16[128,2048]{1,0:T(8,128)(2,1)} %collective-permute-done.12), channel_id=1, source_target_pairs={{0,4},{4,8},{8,12},{12,0},{1,5},{5,9},{9,13},{13,1},{2,6},{6,10},{... | collective-permute-start | bytes 1572872 | tf_op jit(solution)/shard_map/ppermute | solution.py:86
  185.3 27.8 %collective-permute-start.19 = (bf16[128,2048]{1,0:T(8,128)(2,1)}, bf16[128,2048]{1,0:T(8,128)(2,1)}, u32[]{:S(2)}, u32[]{:S(2)}) collective-permute-start(bf16[128,2048]{1,0:T(8,128)(2,1)} %collective-permute-done.18), channel_id=1, source_target_pairs={{0,4},{4,8},{8,12},{12,0},{1,5},{5,9},{9,13},{13,1},{2,6},{6,10},{... | collective-permute-start | bytes 1572872 | tf_op jit(solution)/shard_map/ppermute | solution.py:86
  284.4 35.8 %collective-permute-start.43 = (bf16[64,2176]{1,0:T(8,128)(2,1)}, bf16[64,2176]{1,0:T(8,128)(2,1)}, u32[]{:S(2)}, u32[]{:S(2)}) collective-permute-start(bf16[64,2176]{1,0:T(8,128)(2,1)} %get-tuple-element.184.refs_0_), channel_id=1, source_target_pairs={{0,2},{1,3},{2,0},{3,1},{4,6},{5,7},{6,4},{7,5},{8,10},{9,11},{10,... | collective-permute-start | bytes 835592 | tf_op jit(solution)/shard_map/ppermute | solution.py:73
  285.8 34.7 %collective-permute-start.46 = (bf16[64,2176]{1,0:T(8,128)(2,1)S(1)}, bf16[64,2176]{1,0:T(8,128)(2,1)}, u32[]{:S(2)}, u32[]{:S(2)}) collective-permute-start(bf16[64,2176]{1,0:T(8,128)(2,1)S(1)} %get-tuple-element.183.refs_4_), channel_id=1, source_target_pairs={{0,1},{1,0},{2,3},{3,2},{4,5},{5,4},{6,7},{7,6},{8,9},{9,8},{10,11... | collective-permute-start | bytes 835592 | tf_op jit(solution)/shard_map/ppermute | solution.py:73
  287.9 27.5 %collective-permute-start.27 = (bf16[128,2176]{1,0:T(8,128)(2,1)}, bf16[128,2176]{1,0:T(8,128)(2,1)}, u32[]{:S(2)}, u32[]{:S(2)}) collective-permute-start(bf16[128,2176]{1,0:T(8,128)(2,1)} %pad_maximum_fusion.17), channel_id=1, source_target_pairs={{0,4},{4,8},{8,12},{12,0},{1,5},{5,9},{9,13},{13,1},{2,6},{6,10},{... | collective-permute-start | bytes 1671176 | tf_op jit(solution)/shard_map/ppermute | solution.py:86
  291.2 29.9 %collective-permute-start.44 = (bf16[64,2176]{1,0:T(8,128)(2,1)}, bf16[64,2176]{1,0:T(8,128)(2,1)}, u32[]{:S(2)}, u32[]{:S(2)}) collective-permute-start(bf16[64,2176]{1,0:T(8,128)(2,1)} %collective-permute-done.42.refs_1_), channel_id=1, source_target_pairs={{0,2},{1,3},{2,0},{3,1},{4,6},{5,7},{6,4},{7,5},{8,10},{9,11},{10,... | collective-permute-start | bytes 835592 | tf_op jit(solution)/shard_map/ppermute | solution.py:73
  297.0 33.6 %collective-permute-start.47 = (bf16[64,2176]{1,0:T(8,128)(2,1)}, bf16[64,2176]{1,0:T(8,128)(2,1)}, u32[]{:S(2)}, u32[]{:S(2)}) collective-permute-start(bf16[64,2176]{1,0:T(8,128)(2,1)} %collective-permute-done.45.refs_5_), channel_id=1, source_target_pairs={{0,1},{1,0},{2,3},{3,2},{4,5},{5,4},{6,7},{7,6},{8,9},{9,8},{10,11... | collective-permute-start | bytes 835592 | tf_op jit(solution)/shard_map/ppermute | solution.py:73
  400.1 32.8 %collective-permute-start.54 = (bf16[2,2,64,4224]{3,2,0,1:T(8,128)(2,1)}, bf16[2,2,64,4224]{3,2,0,1:T(8,128)(2,1)}, u32[]{:S(2)}, u32[]{:S(2)}) collective-permute-start(bf16[2,2,64,4224]{3,2,0,1:T(8,128)(2,1)} %bitcast.480), channel_id=1, source_target_pairs={{0,2},{1,3},{2,0},{3,1},{4,6},{5,7},{6,4},{7,5},{8,10},{9,11},{10,... | collective-permute-start | bytes 6488072 | tf_op jit(solution)/shard_map/ppermute | solution.py:73
  402.6 33.7 %collective-permute-start.55 = (bf16[2,2,64,4224]{3,2,0,1:T(8,128)(2,1)}, bf16[2,2,64,4224]{3,2,0,1:T(8,128)(2,1)S(1)}, u32[]{:S(2)}, u32[]{:S(2)}) collective-permute-start(bf16[2,2,64,4224]{3,2,0,1:T(8,128)(2,1)} %bitcast.479), channel_id=1, source_target_pairs={{0,1},{1,0},{2,3},{3,2},{4,5},{5,4},{6,7},{7,6},{8,9},{9,8},{10,11... | collective-permute-start | bytes 6488072 | tf_op jit(solution)/shard_map/ppermute | solution.py:73
  475.4 32.9 %collective-permute-start.58 = (bf16[2,2,64,4224]{3,2,0,1:T(8,128)(2,1)S(1)}, bf16[2,2,64,4224]{3,2,0,1:T(8,128)(2,1)S(1)}, u32[]{:S(2)}, u32[]{:S(2)}) collective-permute-start(bf16[2,2,64,4224]{3,2,0,1:T(8,128)(2,1)S(1)} %bitcast.557), channel_id=1, source_target_pairs={{0,2},{1,3},{2,0},{3,1},{4,6},{5,7},{6,4},{7,5},{8,10},{9,11},{10,... | collective-permute-start | bytes 6488072 | tf_op jit(solution)/shard_map/ppermute | solution.py:73
  476.0 32.9 %collective-permute-start.60 = (bf16[2,2,64,4224]{3,2,0,1:T(8,128)(2,1)S(1)}, bf16[2,2,64,4224]{3,2,0,1:T(8,128)(2,1)S(1)}, u32[]{:S(2)}, u32[]{:S(2)}) collective-permute-start(bf16[2,2,64,4224]{3,2,0,1:T(8,128)(2,1)S(1)} %bitcast.556), channel_id=1, source_target_pairs={{0,1},{1,0},{2,3},{3,2},{4,5},{5,4},{6,7},{7,6},{8,9},{9,8},{10,11... | collective-permute-start | bytes 6488072 | tf_op jit(solution)/shard_map/ppermute | solution.py:73
  477.1 58.9 %collective-permute-start.62 = (bf16[128,4224]{1,0:T(8,128)(2,1)S(1)}, bf16[128,4224]{1,0:T(8,128)(2,1)S(1)}, u32[]{:S(2)}, u32[]{:S(2)}) collective-permute-start(bf16[128,4224]{1,0:T(8,128)(2,1)S(1)} %bitcast.563), channel_id=1, source_target_pairs={{0,4},{4,8},{8,12},{12,0},{1,5},{5,9},{9,13},{13,1},{2,6},{6,10},{... | collective-permute-start | bytes 3244040 | tf_op jit(solution)/shard_map/ppermute | solution.py:86
  599.3 31.2 %collective-permute-start.73 = (bf16[1,512,2048]{2,1,0:T(8,128)(2,1)}, bf16[1,512,2048]{2,1,0:T(8,128)(2,1)}, u32[]{:S(2)}, u32[]{:S(2)}) collective-permute-start(bf16[1,512,2048]{2,1,0:T(8,128)(2,1)} %bitcast.103), channel_id=1, source_target_pairs={{0,16},{16,0},{1,17},{17,1},{2,18},{18,2},{3,19},{19,3},{4,20},{20... | collective-permute-start | bytes 6291464 | tf_op jit(solution)/shard_map/ppermute | solution.py:73
  630.6 224.9 %collective-permute-start.66 = (bf16[64,2048]{1,0:T(8,128)(2,1)}, bf16[64,2048]{1,0:T(8,128)(2,1)}, u32[]{:S(2)}, u32[]{:S(2)}) collective-permute-start(bf16[64,2048]{1,0:T(8,128)(2,1)} %get-tuple-element.204), channel_id=1, source_target_pairs={{4,0},{0,4},{20,8},{16,12},{12,16},{8,20},{28,24},{24,28},{5,1},{1... | collective-permute-start | bytes 786440 | tf_op jit(solution)/shard_map/ppermute | solution.py:181
  705.3 62.5 %collective-permute-start.90 = (bf16[768,1024]{1,0:T(8,128)(2,1)}, bf16[768,1024]{1,0:T(8,128)(2,1)}, u32[]{:S(2)}, u32[]{:S(2)}) collective-permute-start(bf16[768,1024]{1,0:T(8,128)(2,1)} %fusion.56), channel_id=1, source_target_pairs={{0,16},{16,0},{1,17},{17,1},{2,18},{18,2},{3,19},{19,3},{4,20},{20... | collective-permute-start | bytes 4718600 | tf_op jit(solution)/shard_map/ppermute | solution.py:73
  714.3 98.8 %collective-permute-start.89 = (bf16[1024,1536]{1,0:T(8,128)(2,1)}, bf16[1024,1536]{1,0:T(8,128)(2,1)S(1)}, u32[]{:S(2)}, u32[]{:S(2)}) collective-permute-start(bf16[1024,1536]{1,0:T(8,128)(2,1)} %convolution_convert_fusion.2), channel_id=1, source_target_pairs={{0,16},{16,0},{1,17},{17,1},{2,18},{18,2},{3,19},{19,3},{4,20},{20... | collective-permute-start | bytes 9437192 | tf_op jit(solution)/shard_map/ppermute | solution.py:73
  719.9 27.5 %collective-permute-start.77 = (bf16[512,2048]{1,0:T(8,128)(2,1)}, bf16[512,2048]{1,0:T(8,128)(2,1)}, u32[]{:S(2)}, u32[]{:S(2)}) collective-permute-start(bf16[512,2048]{1,0:T(8,128)(2,1)} %convolution_convert_fusion.8), channel_id=1, source_target_pairs={{0,16},{16,0},{1,17},{17,1},{2,18},{18,2},{3,19},{19,3},{4,20},{20... | collective-permute-start | bytes 6291464 | tf_op jit(solution)/shard_map/ppermute | solution.py:73
  746.3 28.0 %collective-permute-start.80 = (bf16[2,4,64,640]{3,2,0,1:T(8,128)(2,1)S(1)}, bf16[2,4,64,640]{3,2,0,1:T(8,128)(2,1)S(1)}, u32[]{:S(2)}, u32[]{:S(2)}) collective-permute-start(bf16[2,4,64,640]{3,2,0,1:T(8,128)(2,1)S(1)} %fusion.95), channel_id=1, source_target_pairs={{0,4},{4,8},{8,12},{12,0},{1,5},{5,9},{9,13},{13,1},{2,6},{6,10},{... | collective-permute-start | bytes 1966088 | tf_op jit(solution)/shard_map/ppermute | solution.py:86
  752.0 41.1 %collective-permute-start.78 = (bf16[1,2,64,2048]{3,2,1,0:T(8,128)(2,1)S(1)}, bf16[1,2,64,2048]{3,2,1,0:T(8,128)(2,1)S(1)}, u32[]{:S(2)}, u32[]{:S(2)}) collective-permute-start(bf16[1,2,64,2048]{3,2,1,0:T(8,128)(2,1)S(1)} %get-tuple-element.170), channel_id=1, source_target_pairs={{0,2},{1,3},{2,0},{3,1},{4,6},{5,7},{6,4},{7,5},{8,10},{9,11},{10,... | collective-permute-start | bytes 1572872 | tf_op jit(solution)/shard_map/ppermute | solution.py:73
  775.1 80.4 %collective-permute-start.65 = (bf16[64,2048]{1,0:T(8,128)(2,1)S(1)}, bf16[64,2048]{1,0:T(8,128)(2,1)}, u32[]{:S(2)}, u32[]{:S(2)}) collective-permute-start(bf16[64,2048]{1,0:T(8,128)(2,1)S(1)} %copy-done.77), channel_id=1, source_target_pairs={{0,0},{4,4},{16,8},{20,12},{8,16},{12,20},{24,24},{28,28},{1,1},{5... | collective-permute-start | bytes 786440 | tf_op jit(solution)/shard_map/ppermute | solution.py:181
  793.3 29.2 %collective-permute-start.83 = (bf16[2,4,64,640]{3,2,0,1:T(8,128)(2,1)S(1)}, bf16[2,4,64,640]{3,2,0,1:T(8,128)(2,1)}, u32[]{:S(2)}, u32[]{:S(2)}) collective-permute-start(bf16[2,4,64,640]{3,2,0,1:T(8,128)(2,1)S(1)} %fusion.64), channel_id=1, source_target_pairs={{0,4},{4,8},{8,12},{12,0},{1,5},{5,9},{9,13},{13,1},{2,6},{6,10},{... | collective-permute-start | bytes 1966088 | tf_op jit(solution)/shard_map/ppermute | solution.py:86
  830.1 27.9 %collective-permute-start.84 = (bf16[64,2048]{1,0:T(8,128)(2,1)S(1)}, bf16[64,2048]{1,0:T(8,128)(2,1)S(1)}, u32[]{:S(2)}, u32[]{:S(2)}) collective-permute-start(bf16[64,2048]{1,0:T(8,128)(2,1)S(1)} %get-tuple-element.194), channel_id=1, source_target_pairs={{0,0},{4,4},{16,8},{20,12},{8,16},{12,20},{24,24},{28,28},{1,1},{5... | collective-permute-start | bytes 786440 | tf_op jit(solution)/shard_map/ppermute | solution.py:181
  (187 other events, 3463.9 us)
Sparse Core Ops, SparseCore 0:
  150.7 131.0 all-gather.2

commit v3 on v2

--- a/solution.py
+++ b/solution.py
@@ -2,13 +2,13 @@
 import jax.numpy as jnp
 from jax import lax
 from jax.experimental import pallas as pl
-from jax.experimental.pallas import tpu as pltpu
 from jax.sharding import Mesh, PartitionSpec as P
 
 H = 32
 KV = 4
 HD = 128
 TOPK = 8
+BLOCK = 64
 
 eps_norm = 1e-06
 rope_base = 1000000.0
@@ -234,55 +234,42 @@
     return moving
 
 
-def pull_kernel(chosen, *refs):
-    *pieces, main, tail = refs
-    groups, slots = chosen.shape[:2]
+def pull_kernel(pick, *refs):
+    *pieces, main, grads, tail, select = refs
+    groups, slots, depth = select.shape
     n = len(pieces) // groups
     width = main.shape[-1]
+    capacity = slots // (depth // BLOCK)
+    place = lax.broadcasted_iota(jnp.int32, (1, depth), 1) // BLOCK
+    place = (place * 128).astype(f32)
+    ids = lax.broadcasted_iota(jnp.int32, (slots, 1), 0)
+    ids = ((ids // capacity) * 128 + ids % capacity + 1).astype(f32)
     for g in range(groups):
-        rows = jnp.concatenate([piece[...] for piece in pieces[g * n : (g + 1) * n]], axis=0)
-        got = jnp.dot(chosen[g], rows, preferred_element_type=f32).astype(bf16)
-        main[pl.ds(g * slots, slots), :] = got[:, :width]
-        tail[pl.ds(g * slots, slots), :] = got[:, width:]
-
-
-def pull_pieces(chosen, pieces, width):
-    slots = chosen.shape[0] * chosen.shape[1]
-    rest = pieces[0].shape[1] - width
+        mine = pieces[g * n : (g + 1) * n]
+        last = jnp.concatenate([piece[:, pl.ds(2 * width, 128)] for piece in mine], axis=0)
+        code = dot_nt(pick[...], last)[:1]
+        kept = (code > 0.0) & (code <= capacity)
+        code = jnp.where(kept, code + place, -1.0)
+        chosen = jnp.where(code == ids, 1.0, 0.0).astype(bf16)
+        select[g] = chosen
+        at = pl.ds(g * slots, slots)
+        for out, first in ((main, 0), (grads, width)):
+            rows = [piece[:, pl.ds(first, width)] for piece in mine]
+            rows = jnp.concatenate(rows, axis=0)
+            out[at, :] = dot(chosen, rows).astype(bf16)
+        tail[at, :] = dot(chosen, last).astype(bf16)
+
+
+def pull_pieces(pick, pieces, groups, capacity, width):
+    depth = len(pieces) // groups * pieces[0].shape[0]
+    slots = depth // BLOCK * capacity
+    shapes = [(groups * slots, width), (groups * slots, width), (groups * slots, 128)]
+    shapes.append((groups, slots, depth))
     return pl.pallas_call(
         pull_kernel,
-        out_shape=(
-            jax.ShapeDtypeStruct((slots, width), bf16),
-            jax.ShapeDtypeStruct((slots, rest), bf16),
-        ),
+        out_shape=tuple(jax.ShapeDtypeStruct(shape, bf16) for shape in shapes),
         name="pull",
-    )(chosen, *pieces)
-
-
-def pull_blocks_kernel(index, chosen, *refs):
-    *blocks, out = refs
-    rows = jnp.concatenate([block[0] for block in blocks], axis=0)
-    out[...] = jnp.dot(chosen[0], rows, preferred_element_type=f32).astype(bf16)
-
-
-def pull_blocks(index, chosen, blocks, width):
-    groups, slots, depth = chosen.shape
-    n = index.shape[1]
-    block = (1, depth // n, width)
-    specs = [pl.BlockSpec((1, slots, depth), lambda g, at: (g, 0, 0))]
-    for i in range(n):
-        specs.append(pl.BlockSpec(block, lambda g, at, i=i: (at[g, i], 0, 0)))
-    return pl.pallas_call(
-        pull_blocks_kernel,
-        grid_spec=pltpu.PrefetchScalarGridSpec(
-            num_scalar_prefetch=1,
-            grid=(groups,),
-            in_specs=specs,
-            out_specs=pl.BlockSpec((slots, width), lambda g, at: (g, 0)),
-        ),
-        out_shape=jax.ShapeDtypeStruct((groups * slots, width), bf16),
-        name="pull_blocks",
-    )(index, chosen, *([blocks] * n))
+    )(pick, *pieces)
 
 
 def on_device(
@@ -332,6 +319,23 @@
     n_small = small.shape[0]
     n_router = experts * shard
     small = jnp.pad(small, (0, -n_small % 128)).reshape(-1, 128)
+    kv_weight = jnp.concatenate(
+        [k_weight.reshape(shard, n_cl, HD), v_weight.reshape(shard, n_cl, HD)], axis=-1
+    )
+    packed = jnp.concatenate(
+        [
+            q_weight.reshape(shard, n_cl, n_dp, hw),
+            kv_weight.reshape(shard, n_cl, n_dp, kvw),
+        ],
+        axis=-1,
+    )
+    packed = jnp.transpose(packed, (1, 2, 0, 3)).reshape(tp, shard, pack)
+    packed = lax.all_to_all(packed, ("cl", "dp"), split_axis=0, concat_axis=0, tiled=True)
+    packed = jnp.transpose(packed.reshape(n_cl, n_dp, shard, pack), (1, 0, 2, 3))
+    gu_full = dp_gather(gate_up_weight[0]).reshape(width, 2 * ff)
+    down_full = jnp.concatenate(list(dp_gather(down_weight[0])), axis=1)
+
+    packed, small = tie(packed, small)
     small = every_gather(small).reshape(n_all, -1)
     router_t = small[:, :n_router].reshape(n_all, experts, shard)
     router_t = jnp.transpose(router_t, (1, 0, 2)).reshape(experts, width)
@@ -341,46 +345,29 @@
     q_gain = gains[2 * width : 2 * width + HD]
     k_gain = gains[2 * width + HD :]
 
-    inputs_low = to_sequence(tokens).reshape(rows, width)
-    inputs = inputs_low.astype(f32)
-    inputs_all = dp_rows(jnp.concatenate(spread(inputs_low))).reshape(length, width).astype(f32)
-
-    kv_weight = jnp.concatenate(
-        [k_weight.reshape(shard, n_cl, HD), v_weight.reshape(shard, n_cl, HD)], axis=-1
-    )
-    packed = jnp.concatenate(
-        [
-            q_weight.reshape(shard, n_cl, n_dp, hw),
-            kv_weight.reshape(shard, n_cl, n_dp, kvw),
-        ],
-        axis=-1,
-    )
-    packed = jnp.transpose(packed, (1, 2, 0, 3)).reshape(tp, shard, pack)
-    packed = lax.all_to_all(packed, ("cl", "dp"), split_axis=0, concat_axis=0, tiled=True)
-    packed = jnp.transpose(packed.reshape(n_cl, n_dp, shard, pack), (1, 0, 2, 3))
     qkv_w = jnp.zeros((n_dp, n_sq, n_cl, shard, pack), bf16)
     rank = cl * n_dp + dp
-    o_mine = lax.ppermute(o_weight, ("dp", "sq", "cl"), head_pairs())
     qkv_pieces = [packed, shift(packed, 1)]
-    qkv_pieces[1], o_mine = tie(qkv_pieces[1], o_mine)
-    for _ in range(2, n_sq):
+    inputs_low = to_sequence(tokens).reshape(rows, width)
+    upstream_low = jnp.concatenate([cotangent, codes], axis=-1)
+    upstream_low = to_sequence(upstream_low).reshape(rows, -1)
+    qkv_pieces[1], inputs_low, upstream_low = tie(qkv_pieces[1], inputs_low, upstream_low)
+    inputs = inputs_low.astype(f32)
+    inputs_all = spread(inputs_low)
+    for _ in range(2, n_sq - 1):
         qkv_pieces.append(shift(qkv_pieces[-1], 1))
-
-    upstream_low = jnp.concatenate([cotangent, codes], axis=-1)
-    qkv_pieces[-2], upstream_low = tie(qkv_pieces[-2], upstream_low)
-    qkv_pieces[-1] = shift(qkv_pieces[-2], 1)
-    upstream_low = to_sequence(upstream_low).reshape(rows, -1)
+    qkv_pieces[-1], inputs_all, gu_full, down_full, o_weight, upstream_low = tie(
+        qkv_pieces[-1], inputs_all, gu_full, down_full, o_weight, upstream_low
+    )
     upstream = upstream_low[:, :width].astype(f32)
     own_codes = upstream_low[:, width : width + experts].astype(f32)
-    qkv_pieces[-1], upstream_low, o_mine = tie(qkv_pieces[-1], upstream_low, o_mine)
-    grads_all = lax.all_gather(upstream_low, ("sq", "cl"))
-    o_pieces = [o_mine, shift(o_mine, 1)]
+    qkv_pieces.append(shift(qkv_pieces[-1], 1))
+    o_mine = lax.ppermute(o_weight, ("dp", "sq", "cl"), head_pairs())
+    inputs_all = dp_rows(jnp.concatenate(inputs_all)).reshape(length, width).astype(f32)
+
     for t, piece in enumerate(qkv_pieces):
         qkv_w = lax.dynamic_update_index_in_dim(qkv_w, piece, (zi - t) % n_sq, 1)
     qkv_w = qkv_w.reshape(width, pack)
-
-    gu_full = dp_gather(gate_up_weight[0]).reshape(width, 2 * ff)
-    down_full = jnp.concatenate(list(dp_gather(down_weight[0])), axis=1)
 
     order = jnp.array([[0, 1, 2, 3], [0, 2, 1, 3]], jnp.int32)
     chip_of = order ^ cl
@@ -398,7 +385,6 @@
     cosine, sine_table = cosine[:, None, :], sine_table[:, None, :]
 
     first_scale = rms_scale(inputs)
-    inputs_all, gu_full, down_full = tie(inputs_all, gu_full, down_full)
     normed_all = (inputs_all * rms_scale(inputs_all) * attn_gain).astype(bf16)
     proj = dot(normed_all, qkv_w)
     q_proj = proj[:, :hw].reshape(length, heads, HD)
@@ -410,10 +396,10 @@
     k_scale = rms_scale(k_proj)
     queries = rotate(q_proj * q_scale * q_gain, cosine, sine_table).astype(bf16)
     keys = rotate(k_proj * k_scale * k_gain, cosine, sine_table).astype(bf16)[:, 0]
-    queries, o_pieces[1] = tie(queries, o_pieces[1])
-    o_pieces.append(shift(o_pieces[1], 1))
-    values, o_pieces[2] = tie(values, o_pieces[2])
-    for _ in range(3, n_sq):
+    queries, o_mine = tie(queries, o_mine)
+    o_pieces = [o_mine, shift(o_mine, 1)]
+    values, o_pieces[1] = tie(values, o_pieces[1])
+    for _ in range(2, n_sq):
         o_pieces.append(shift(o_pieces[-1], 1))
     allowed = (positions[None, :] <= positions[:, None]) & (
         segments[None, :] == segments[:, None]
@@ -425,7 +411,7 @@
     prob_low = probs.astype(bf16)
     attended = jnp.einsum("hqk,kd->qhd", prob_low, values, preferred_element_type=f32)
     attended = attended.reshape(length, hw).astype(bf16)
-    attended, o_pieces[-1] = tie(attended, o_pieces[-1])
+    attended, o_pieces[2] = tie(attended, o_pieces[2])
     o_full = jnp.zeros((n_sq,) + o_weight.shape, bf16)
     for t, piece in enumerate(o_pieces):
         o_full = lax.dynamic_update_index_in_dim(o_full, piece, (zi - t - rank) % n_sq, 0)
@@ -442,26 +428,14 @@
     gates = gate_terms / jnp.sum(gate_terms, axis=-1, keepdims=True)
     gates_high = gates.astype(bf16)
     gates_low = (gates - gates_high.astype(f32)).astype(bf16)
-    extra = jnp.pad(
-        jnp.concatenate([gates_high, gates_low], axis=-1), ((0, 0), (0, 128 - 2 * experts))
-    )
-    hidden_wide = jnp.concatenate([hidden, extra], axis=-1)
+    extra = jnp.concatenate([gates_high, gates_low, own_codes.astype(bf16)], axis=-1)
+    extra = jnp.pad(extra, ((0, 0), (0, 128 - 3 * experts)))
+    hidden_wide = jnp.concatenate([hidden, upstream_low[:, :width], extra], axis=-1)
 
     lanes = jnp.arange(128)
     half = rows // 2
     n_slot = n_cl * hb * capacity
-    z_of = (zi - jnp.arange(n_sq)) % n_sq
-    at = (z_of[:, None, None] * n_cl + chip_of) * 2 + jnp.arange(2)[:, None]
-    at = at.reshape(2 * n_sq, n_cl).astype(jnp.int32)
-    code = jnp.where(lanes == expert, grads_all[:, :, width:].astype(f32), 0.0)
-    code = jnp.sum(code, axis=-1).reshape(1, n_ctx * 2, half)
-    found = at.reshape(-1, 1, 1) == jnp.arange(n_ctx * 2)[:, None]
-    code = jnp.sum(jnp.where(found, code, 0.0), axis=1)
-    code = jnp.where(code <= capacity, code, 0.0).reshape(n_sq, 2, 1, n_cl * half)
-    place = (jnp.arange(n_cl * half) // bl) * 128.0
-    ids = jnp.arange(n_slot)
-    ids = ((ids // capacity) * 128 + ids % capacity + 1).astype(f32)
-    select = (jnp.where(code > 0, code + place, -1.0) == ids[:, None]).astype(bf16)
+    code_pick = jnp.broadcast_to(lanes == 2 * experts + expert, (8, 128)).astype(bf16)
     pick = (lanes == expert) | (lanes == experts + expert)
 
     def push(chosen, v):
@@ -471,29 +445,24 @@
 
     per = 2
     n_chunk = n_sq // per
-    select = select.reshape(n_chunk, per * 2, n_slot, -1)
-    grad_slots = pull_blocks(
-        at, select.reshape((-1,) + select.shape[2:]), grads_all.reshape(n_ctx * 2, half, -1), width
-    )
-    grad_slots = list(grad_slots.reshape(n_chunk, -1, width))
-
     ins, actives, out_grads, gu_grads, backs = [], [], [], [], []
     arrived = []
     moving = hidden_wide
     for t in range(n_sq):
         arrived += spread(moving)
         if t == 0:
-            moving, grad_slots = tie(shift(moving, 1), grad_slots)
+            moving = shift(moving, 1)
         elif t + 1 < n_sq:
             moving = shift(moving, 1)
     for chunk in range(n_chunk):
         pieces = arrived[chunk * per * 8 : (chunk + 1) * per * 8]
-        chosen = select[chunk]
-        expert_in, gate_lanes = pull_pieces(chosen, pieces, width)
+        expert_in, grad_slot, gate_lanes, chosen = pull_pieces(
+            code_pick, pieces, 2 * per, capacity, width
+        )
         gate_slot = jnp.sum(
             jnp.where(pick, gate_lanes.astype(f32), 0.0), axis=-1, keepdims=True
         )
-        grad_slot = grad_slots[chunk].astype(f32)
+        grad_slot = grad_slot.astype(f32)
         gate_up = dot(expert_in, gu_full)
         gate_part, up_part = gate_up[:, :ff], gate_up[:, ff:]
         sigmoid_gate = jax.nn.sigmoid(gate_part)
@@ -519,11 +488,24 @@
         ).astype(bf16)
         moe = (gate_slot * out_wide).astype(bf16)
         back = push(chosen, jnp.concatenate([row_grad, moe, pair_extra], axis=-1))
+        if chunk + 1 < n_chunk:
+            code_pick, back = tie(code_pick, back)
         back_first = fold_first(back.reshape(per, 2, n_cl, half, -1))
         ins.append(expert_in)
         actives.append(activated)
         out_grads.append(out_grad)
         gu_grads.append(gu_grad)
+    gu_grad = jnp.concatenate(gu_grads)
+    activated = jnp.concatenate(actives)
+
+    def columns(parts, m):
+        size = width // n_dp
+        at = (dp ^ m) * size
+        return jnp.concatenate([lax.dynamic_slice_in_dim(v, at, size, 1) for v in parts])
+
+    gu_parts = [dot_tn(columns(ins, m), gu_grad) for m in range(n_dp)]
+    down_parts = [dot_tn(activated, columns(out_grads, m)) for m in range(n_dp)]
+    back_first, gu_parts, down_parts = tie(back_first, gu_parts, down_parts)
     backs = [v.reshape(rows, -1) for v in backs + list(fold_last(back_first))]
     back = ring_scatter(backs).astype(bf16).astype(f32)
     output = (middle + back[:, width : 2 * width]).astype(bf16)
@@ -538,11 +520,13 @@
     middle_grad = upstream + norm_back(middle, second_scale, ffn_gain, hidden_grad)
 
     middle_low = dp_rows(jnp.concatenate(spread(middle_grad.astype(bf16)))).reshape(length, width)
+    output = from_sequence(output.reshape(nl, bl, width))
+    middle_low, output = tie(middle_low, output)
     o_grad = dot_tn(attended, middle_low).reshape(n_sq, -1, width)
     attended_grad = dot_nt(middle_low, o_full).astype(bf16).reshape(length, heads, HD)
     attended_grad, o_grad = tie(attended_grad, o_grad)
     o_parts = [take(o_grad, (zi - t - rank) % n_sq) for t in range(n_sq)]
-    o_got = shift(o_parts[1].astype(bf16), 1)
+    o_got = [shift(o_parts[t].astype(bf16), -t) for t in range(1, n_sq)]
     prob_grad = jnp.einsum("qhd,kd->hqk", attended_grad, values, preferred_element_type=f32)
     inner_sum = jnp.sum(probs * prob_grad, axis=-1, keepdims=True)
     score_grad = (probs * (prob_grad - inner_sum)).astype(bf16)
@@ -554,18 +538,12 @@
         jnp.einsum("hqk,kd->qhd", score_grad, keys, preferred_element_type=f32) * score_scale
     )
     kv_sum = jnp.concatenate([key_part, value_part], axis=-1).reshape(n_dp, -1, 2 * HD)
-    kv_sum, o_got = tie(kv_sum, o_got)
-    o_got = o_parts[2].astype(f32) + o_got.astype(f32)
-    o_got = shift(o_got.astype(bf16), 1)
     kv_sum = dp_sum(kv_sum).reshape(length, 2 * HD)
     query_grad, o_got = tie(query_grad, o_got)
-    for t in list(range(3, n_sq)) + [0]:
-        o_got = o_parts[t].astype(f32) + o_got.astype(f32)
-        if t:
-            o_got = shift(o_got.astype(bf16), 1)
+    o_got = o_parts[0].astype(f32) + sum(v.astype(f32) for v in o_got)
     o_share = lax.ppermute(
         o_got.astype(bf16), ("dp", "sq", "cl"), [(b, a) for a, b in head_pairs()]
-    ).astype(f32)
+    )
     key_rot_grad = rotate_back(kv_sum[:, None, :HD], cosine, sine_table)
     k_gain_grad = jnp.sum(key_rot_grad * k_proj * k_scale, axis=(0, 1))
     k_gain_grad = jnp.where(dp == 0, k_gain_grad, 0.0)
@@ -576,35 +554,23 @@
     q_gain_grad = jnp.sum(query_rot_grad * q_proj * q_scale, axis=(0, 1))
     q_low = norm_back(q_proj, q_scale, q_gain, query_rot_grad).reshape(length, hw).astype(bf16)
     qkv_low = jnp.concatenate([q_low, kv_low], axis=-1)
-    qkv_low, gu_grads, out_grads = tie(qkv_low, gu_grads, out_grads)
+    qkv_low, gu_parts, down_parts = tie(qkv_low, gu_parts, down_parts)
+    gu_share, down_share = dp_fold(gu_parts), dp_fold(down_parts)
     w_grad = dot_tn(normed_all, qkv_low).reshape(n_dp, n_sq, n_cl, shard, pack)
     w_parts = [take(w_grad, (zi - t) % n_sq, 1) for t in range(n_sq)]
-    w_got = shift(w_parts[1].astype(bf16), 1)
+    w_got = [shift(w_parts[t].astype(bf16), -t) for t in range(1, n_sq)]
     normed_grad = [dot_nt(low_m, qkv_w) for low_m in qkv_low.reshape(n_dp, -1, pack)]
     normed_first = fold_first(dp_fold(normed_grad).reshape(1, 2, n_cl, rows // 2, width))
-    normed_first, w_got = tie(normed_first, w_got)
-    w_got = shift((w_parts[2] + w_got.astype(f32)).astype(bf16), 1)
     normed_grad = fold_last(normed_first).reshape(rows, width)
-    normed_grad, w_got = tie(normed_grad, w_got)
-    for t in range(3, n_sq):
-        w_got = shift((w_parts[t] + w_got.astype(f32)).astype(bf16), 1)
+    normed_grad, w_got, gu_share, down_share = tie(normed_grad, w_got, gu_share, down_share)
+    w_got = w_parts[0].astype(f32) + sum(v.astype(f32) for v in w_got)
     attn_gain_grad = jnp.sum(normed_grad * inputs * first_scale, axis=0)
     input_grad = middle_grad + norm_back(inputs, first_scale, attn_gain, normed_grad)
     input_grad = from_sequence(input_grad.astype(bf16).reshape(nl, bl, width))
-    output = from_sequence(output.reshape(nl, bl, width))
-
-    gu_grad = jnp.concatenate(gu_grads)
-    activated = jnp.concatenate(actives)
-
-    def columns(parts, m):
-        size = width // n_dp
-        at = (dp ^ m) * size
-        return jnp.concatenate([lax.dynamic_slice_in_dim(v, at, size, 1) for v in parts])
-
-    gu_share = dp_fold([dot_tn(columns(ins, m), gu_grad) for m in range(n_dp)])
-    down_share = dp_fold([dot_tn(activated, columns(out_grads, m)) for m in range(n_dp)])
-
-    w_grad = (w_parts[0] + w_got.astype(f32)).astype(bf16)
+
+    w_got, o_share = tie(w_got, o_share)
+    o_share = o_share.astype(f32)
+    w_grad = w_got.astype(bf16)
     w_grad = jnp.transpose(w_grad, (1, 0, 2, 3)).reshape(tp, shard, pack)
     w_grad = lax.all_to_all(w_grad, ("cl", "dp"), split_axis=0, concat_axis=0, tiled=True)
     w_grad = jnp.transpose(w_grad.reshape(n_cl, n_dp, shard, pack), (2, 0, 1, 3)).astype(f32)

time: 886 us -> 848 us (0.957)
  starting transfers between devices: 172 us -> 132 us
  other arithmetic: 87.2 us -> 108 us
  between operations: 16.8 us -> 4.04 us
    ppermute x18, starting transfers between devices: 32.2 us -> 9.02 us  [shift(): return lax.ppermute(v, 'sq', [(i, (i + by) % n) for i in range(n)])]
    all_to_all x1, waiting for transfers between devices: 19.7 us -> 3.66 us  [every_gather(): lax.all_to_all(v, ('dp', 'sq', 'cl'), split_axis=0, concat_axis=0, tiled=...]
    ppermute x4, starting transfers between devices: 23.6 us -> 8.12 us  [from_sequence(): got.append(lax.ppermute(v[m], ('dp', 'sq'), pairs))]
    ppermute x63, waiting for transfers between devices: 165 us -> 179 us  [flip(): return lax.ppermute(v, axis, [(i, i ^ bit) for i in range(n)])]
    pallas_call x3 -> x2, Pallas kernels: 19.5 us -> 15.6 us  [pull_pieces(): pl.pallas_call(pull_kernel, out_shape=tuple((jax.ShapeDtypeStruct(shape,...]
    unnamed x267 -> x313, local copies, waits for them, and re-layouts: 31 us -> 28.7 us
  transfers between devices with their start and end apart: 96 -> 95, of which waited for: 43 -> 48; matrix products, arithmetic and copies ran while one was open for 28% -> 28% of each run, Pallas kernels for 2% -> 2%
where the time goes in v3:
time: 848 us; the launch traced here: 834 us
  waiting for transfers between devices  352 us (42%)
  starting transfers between devices  132 us (16%)
  matrix products  131 us (15%)
  other arithmetic  108 us (13%)
  local copies, waits for them, and re-layouts  90.9 us (11%)
  Pallas kernels  15.6 us (2%)
    ppermute x63, waiting for transfers between devices, flip(): return lax.ppermute(v, axis, [(i, i ^ bit) for i in range(n)])  179 us
    ppermute x18, waiting for transfers between devices, shift(): return lax.ppermute(v, 'sq', [(i, (i + by) % n) for i in range(n)])  140 us
    ppermute x63, starting transfers between devices, flip(): return lax.ppermute(v, axis, [(i, i ^ bit) for i in range(n)])  75.6 us
    dot_general x7, matrix products, dot_tn(): lax.dot_general(a, b, (((0,), (0,)), ((), ())), preferred_element_type=f32)  37.5 us
    unnamed x313, local copies, waits for them, and re-layouts  28.7 us
    dot_general x8, matrix products, dot_nt(): lax.dot_general(a, b, (((1,), (1,)), ((), ())), preferred_element_type=f32)  28.4 us
    dot_general x8, matrix products, dot(): return jnp.dot(a, b, preferred_element_type=f32)  23.6 us
    ppermute x4, waiting for transfers between devices, to_sequence(): got.append(lax.ppermute(take(v, (m + zi) % nl), ('dp', 'sq'), pairs))  22.2 us
  transfers between devices with their start and end apart: 95, of which 48 were waited for; matrix products, arithmetic and copies ran while one was open for 28% of the time, Pallas kernels for 2%

profile of v3, /device:TPU:1, one launch (start us, length us, event | category | flops | bytes accessed | tf_op | source)
XLA Modules:
  0.0 834.0 jit_solution(8088322367360657782)
XLA Ops:
  29.9 22.2 %collective-permute-done.3 = bf16[64,2176]{1,0:T(8,128)(2,1)S(1)} collective-permute-done((bf16[64,2176]{1,0:T(8,128)(2,1)S(1)}, bf16[64,2176]{1,0:T(8,128)(2,1)S(1)}, u32[]{:S(2)}, u32[]{:S(2)}) %collective-permute-start.3) | collective-permute-done | bytes 278560 | tf_op jit(solution)/shard_map/ppermute | solution.py:167
  104.5 9.4 %collective-permute-done.15 = bf16[2,4,64,640]{3,2,0,1:T(8,128)(2,1)S(1)} collective-permute-done((bf16[2,4,64,640]{3,2,0,1:T(8,128)(2,1)}, bf16[2,4,64,640]{3,2,0,1:T(8,128)(2,1)S(1)}, u32[]{:S(2)}, u32[]{:S(2)}) %collective-permute-start.15) | collective-permute-done | bytes 655392 | tf_op jit(solution)/shard_map/ppermute | solution.py:86
  137.4 10.9 %fusion.181 = (f32[4,1024]{1,0:T(4,128)S(1)}, f32[4,1024,1024]{1,2,0:T(8,128)}) fusion(pred[1024,1024]{0,1:T(8,128)(4,1)} %compare_and_fusion, bf16[1024,128,1]{0,1,2:T(8,128)(2,1)S(1)} %copy-done.64, bf16[1024,4,128]{0,2,1:T(8,128)(2,1)} %fusion.52), kind=kOutput, calls=%fused_computation.433 | convolution fusion | flops 1090520064 | bytes 19152896 | tf_op jit(solution)/shard_map/sub | solution.py:409
  152.8 7.1 fusion.58
  159.9 7.1 collective-permute-done.20
  168.2 12.0 %collective-permute-done.21 = bf16[128,2048]{1,0:T(8,128)(2,1)S(1)} collective-permute-done((bf16[128,2048]{1,0:T(8,128)(2,1)S(1)}, bf16[128,2048]{1,0:T(8,128)(2,1)S(1)}, u32[]{:S(2)}, u32[]{:S(2)}) %collective-permute-start.21) | collective-permute-done | bytes 524320 | tf_op jit(solution)/shard_map/ppermute | solution.py:86
  195.2 11.8 %collective-permute-done.23 = bf16[1,2,64,2048]{3,2,1,0:T(8,128)(2,1)S(1)} collective-permute-done((bf16[1,2,64,2048]{3,2,1,0:T(8,128)(2,1)}, bf16[1,2,64,2048]{3,2,1,0:T(8,128)(2,1)S(1)}, u32[]{:S(2)}, u32[]{:S(2)}) %collective-permute-start.23) | collective-permute-done | bytes 524320 | tf_op jit(solution)/shard_map/ppermute | solution.py:73
  223.3 8.5 %collective-permute-done.27.refs_1_ = bf16[64,4224]{1,0:T(8,128)(2,1)} collective-permute-done((bf16[64,4224]{1,0:T(8,128)(2,1)S(1)}, bf16[64,4224]{1,0:T(8,128)(2,1)}, u32[]{:S(2)}, u32[]{:S(2)}) %collective-permute-start.27) | collective-permute-done | bytes 540704 | tf_op jit(solution)/shard_map/ppermute | solution.py:73
  233.7 11.2 %collective-permute-done.33 = bf16[128,4224]{1,0:T(8,128)(2,1)} collective-permute-done((bf16[128,4224]{1,0:T(8,128)(2,1)S(1)}, bf16[128,4224]{1,0:T(8,128)(2,1)}, u32[]{:S(2)}, u32[]{:S(2)}) %collective-permute-start.33) | collective-permute-done | bytes 1081376 | tf_op jit(solution)/shard_map/ppermute | solution.py:86
  258.1 9.2 %collective-permute-done.37.refs_13_ = bf16[64,4224]{1,0:T(8,128)(2,1)} collective-permute-done((bf16[64,4224]{1,0:T(8,128)(2,1)S(1)}, bf16[64,4224]{1,0:T(8,128)(2,1)}, u32[]{:S(2)}, u32[]{:S(2)}) %collective-permute-start.37) | collective-permute-done | bytes 540704 | tf_op jit(solution)/shard_map/ppermute | solution.py:73
  281.7 8.6 %collective-permute-done.36.refs_11_ = bf16[64,4224]{1,0:T(8,128)(2,1)S(1)} collective-permute-done((bf16[64,4224]{1,0:T(8,128)(2,1)}, bf16[64,4224]{1,0:T(8,128)(2,1)S(1)}, u32[]{:S(2)}, u32[]{:S(2)}) %collective-permute-start.36) | collective-permute-done | bytes 540704 | tf_op jit(solution)/shard_map/ppermute | solution.py:73
  292.6 7.8 pull.2
  304.0 6.5 fusion.184
  324.1 13.8 %collective-permute-done.47 = bf16[128,4224]{1,0:T(8,128)(2,1)S(1)} collective-permute-done((bf16[128,4224]{1,0:T(8,128)(2,1)S(1)}, bf16[128,4224]{1,0:T(8,128)(2,1)S(1)}, u32[]{:S(2)}, u32[]{:S(2)}) %collective-permute-start.47) | collective-permute-done | bytes 1081376 | tf_op jit(solution)/shard_map/ppermute | solution.py:86
  363.5 9.1 %collective-permute-done.52.refs_14_ = bf16[64,4224]{1,0:T(8,128)(2,1)S(1)} collective-permute-done((bf16[64,4224]{1,0:T(8,128)(2,1)S(1)}, bf16[64,4224]{1,0:T(8,128)(2,1)S(1)}, u32[]{:S(2)}, u32[]{:S(2)}) %collective-permute-start.52) | collective-permute-done | bytes 540704 | tf_op jit(solution)/shard_map/ppermute | solution.py:73
  374.2 10.0 %collective-permute-done.53.refs_15_ = bf16[64,4224]{1,0:T(8,128)(2,1)} collective-permute-done((bf16[64,4224]{1,0:T(8,128)(2,1)}, bf16[64,4224]{1,0:T(8,128)(2,1)}, u32[]{:S(2)}, u32[]{:S(2)}) %collective-permute-start.53) | collective-permute-done | bytes 540704 | tf_op jit(solution)/shard_map/ppermute | solution.py:73
  384.2 7.8 pull.3
  409.7 8.2 collective-permute-done.54
  417.8 12.8 %collective-permute-done.55 = bf16[2,2,64,4224]{3,2,0,1:T(8,128)(2,1)} collective-permute-done((bf16[2,2,64,4224]{3,2,0,1:T(8,128)(2,1)}, bf16[2,2,64,4224]{3,2,0,1:T(8,128)(2,1)}, u32[]{:S(2)}, u32[]{:S(2)}) %collective-permute-start.55) | collective-permute-done | bytes 2162720 | tf_op jit(solution)/shard_map/ppermute | solution.py:73
  441.9 9.3 %collective-permute-done.57 = bf16[2,64,4224]{2,1,0:T(8,128)(2,1)S(1)} collective-permute-done((bf16[2,64,4224]{2,1,0:T(8,128)(2,1)S(1)}, bf16[2,64,4224]{2,1,0:T(8,128)(2,1)S(1)}, u32[]{:S(2)}, u32[]{:S(2)}) %collective-permute-start.57) | collective-permute-done | bytes 1081376 | tf_op jit(solution)/shard_map/ppermute | solution.py:73
  473.4 8.5 %fusion.20 = f32[1024,1536]{1,0:T(8,128)} fusion(bf16[640,1024]{1,0:T(8,128)(2,1)S(1)} %copy-done.54, bf16[640,1024]{1,0:T(8,128)(2,1)S(1)} %copy-done.51, bf16[640,1536]{1,0:T(8,128)(2,1)S(1)} %copy-done.47, bf16[640,768]{1,0:T(8,128)(2,1)} %copy-done.131, bf16[640,768]{1,0:T(8,128)(2,1)S(1)} %copy-done.130), kind=kOutput, calls=%fused_computation.64 | convolution fusion | flops 4043571200 | bytes 12845056 | tf_op jit(solution)/shard_map/dot_general | solution.py:64
  481.9 11.3 %fusion.24 = bf16[1024,1536]{1,0:T(8,128)(2,1)} fusion(bf16[640,1024]{1,0:T(8,128)(2,1)S(1)} %copy-done.53, bf16[640,1024]{1,0:T(8,128)(2,1)S(1)} %copy-done.50, bf16[640,1536]{1,0:T(8,128)(2,1)S(1)} %copy-done.47, bf16[640,768]{1,0:T(8,128)(2,1)S(1)} %copy-done.132, bf16[640,768]{1,0:T(8,128)(2,1)S(1)} %copy-done.130), kind=kOutput, calls=%fused_computation.68 | convolution fusion | flops 4043571200 | bytes 9699328 | tf_op jit(solution)/shard_map/dot_general | solution.py:64
  493.2 9.4 %collective-permute-done.58 = bf16[2,2,64,4224]{3,2,0,1:T(8,128)(2,1)S(1)} collective-permute-done((bf16[2,2,64,4224]{3,2,0,1:T(8,128)(2,1)S(1)}, bf16[2,2,64,4224]{3,2,0,1:T(8,128)(2,1)S(1)}, u32[]{:S(2)}, u32[]{:S(2)}) %collective-permute-start.58) | collective-permute-done | bytes 2162720 | tf_op jit(solution)/shard_map/ppermute | solution.py:73
  507.1 19.3 %collective-permute-done.60 = bf16[2,64,4224]{2,1,0:T(8,128)(2,1)S(1)} collective-permute-done((bf16[2,64,4224]{2,1,0:T(8,128)(2,1)S(1)}, bf16[2,64,4224]{2,1,0:T(8,128)(2,1)S(1)}, u32[]{:S(2)}, u32[]{:S(2)}) %collective-permute-start.60) | collective-permute-done | bytes 1081376 | tf_op jit(solution)/shard_map/ppermute | solution.py:73
  528.8 15.8 %collective-permute-done.63 = bf16[128,4224]{1,0:T(8,128)(2,1)S(1)} collective-permute-done((bf16[128,4224]{1,0:T(8,128)(2,1)S(1)}, bf16[128,4224]{1,0:T(8,128)(2,1)S(1)}, u32[]{:S(2)}, u32[]{:S(2)}) %collective-permute-start.63) | collective-permute-done | bytes 1081376 | tf_op jit(solution)/shard_map/ppermute | solution.py:86
  544.9 23.2 %collective-permute-done.64 = bf16[128,4224]{1,0:T(8,128)(2,1)S(1)} collective-permute-done((bf16[128,4224]{1,0:T(8,128)(2,1)S(1)}, bf16[128,4224]{1,0:T(8,128)(2,1)S(1)}, u32[]{:S(2)}, u32[]{:S(2)}) %collective-permute-start.64) | collective-permute-done | bytes 1081376 | tf_op jit(solution)/shard_map/ppermute | solution.py:86
  587.2 14.6 %collective-permute-start.71 = (bf16[1,512,2048]{2,1,0:T(8,128)(2,1)}, bf16[1,512,2048]{2,1,0:T(8,128)(2,1)}, u32[]{:S(2)}, u32[]{:S(2)}) collective-permute-start(bf16[1,512,2048]{2,1,0:T(8,128)(2,1)} %bitcast.89), channel_id=1, source_target_pairs={{0,16},{16,0},{1,17},{17,1},{2,18},{18,2},{3,19},{19,3},{4,20},{20... | collective-permute-start | bytes 6291464 | tf_op jit(solution)/shard_map/ppermute | solution.py:73
  626.8 7.1 fusion.1
  644.4 8.0 fusion.3
  669.2 20.8 %collective-permute-done.75 = bf16[128,2048]{1,0:T(8,128)(2,1)} collective-permute-done((bf16[128,2048]{1,0:T(8,128)(2,1)}, bf16[128,2048]{1,0:T(8,128)(2,1)}, u32[]{:S(2)}, u32[]{:S(2)}) %collective-permute-start.75) | collective-permute-done | bytes 524320 | tf_op jit(solution)/shard_map/ppermute | solution.py:86
  742.2 9.8 %collective-permute-done.79 = bf16[1,2,64,2048]{3,2,1,0:T(8,128)(2,1)S(1)} collective-permute-done((bf16[1,2,64,2048]{3,2,1,0:T(8,128)(2,1)S(1)}, bf16[1,2,64,2048]{3,2,1,0:T(8,128)(2,1)S(1)}, u32[]{:S(2)}, u32[]{:S(2)}) %collective-permute-start.79) | collective-permute-done | bytes 524320 | tf_op jit(solution)/shard_map/ppermute | solution.py:73
  774.3 22.6 %collective-permute-done.84 = bf16[2,4,64,640]{3,2,1,0:T(8,128)(2,1)} collective-permute-done((bf16[2,4,64,640]{3,2,1,0:T(8,128)(2,1)S(1)}, bf16[2,4,64,640]{3,2,1,0:T(8,128)(2,1)}, u32[]{:S(2)}, u32[]{:S(2)}) %collective-permute-start.84) | collective-permute-done | bytes 655392 | tf_op jit(solution)/shard_map/ppermute | solution.py:86
  (728 shorter events, 456.5 us)
Async XLA Ops:
  1.8 25.3 %collective-permute-start.1 = (bf16[64,2048]{1,0:T(8,128)(2,1)S(1)}, bf16[64,2048]{1,0:T(8,128)(2,1)S(1)}, u32[]{:S(2)}, u32[]{:S(2)}) collective-permute-start(bf16[64,2048]{1,0:T(8,128)(2,1)S(1)} %get-tuple-element.254), channel_id=1, source_target_pairs={{0,0},{4,4},{8,16},{12,20},{16,8},{20,12},{24,24},{28,28},{1,1},{5... | collective-permute-start | bytes 786440 | tf_op jit(solution)/shard_map/ppermute | solution.py:167
  15.1 54.1 %collective-permute-start.12 = (bf16[1,1024,1536]{2,1,0:T(8,128)(2,1)}, bf16[1,1024,1536]{2,1,0:T(8,128)(2,1)}, u32[]{:S(2)}, u32[]{:S(2)}) collective-permute-start(bf16[1,1024,1536]{2,1,0:T(8,128)(2,1)} %param.23), channel_id=1, source_target_pairs={{0,16},{16,0},{1,17},{17,1},{2,18},{18,2},{3,19},{19,3},{4,20},{20... | collective-permute-start | bytes 9437192 | tf_op jit(solution)/shard_map/ppermute | solution.py:73
  15.1 40.9 %collective-permute-start.13 = (bf16[1,768,1024]{2,1,0:T(8,128)(2,1)}, bf16[1,768,1024]{2,1,0:T(8,128)(2,1)}, u32[]{:S(2)}, u32[]{:S(2)}) collective-permute-start(bf16[1,768,1024]{2,1,0:T(8,128)(2,1)} %param.24), channel_id=1, source_target_pairs={{0,16},{16,0},{1,17},{17,1},{2,18},{18,2},{3,19},{19,3},{4,20},{20... | collective-permute-start | bytes 4718600 | tf_op jit(solution)/shard_map/ppermute | solution.py:73
  23.4 28.8 %collective-permute-start.3 = (bf16[64,2176]{1,0:T(8,128)(2,1)S(1)}, bf16[64,2176]{1,0:T(8,128)(2,1)S(1)}, u32[]{:S(2)}, u32[]{:S(2)}) collective-permute-start(bf16[64,2176]{1,0:T(8,128)(2,1)S(1)} %get-tuple-element.230), channel_id=1, source_target_pairs={{0,0},{4,4},{8,16},{12,20},{16,8},{20,12},{24,24},{28,28},{1,1},{5... | collective-permute-start | bytes 835592 | tf_op jit(solution)/shard_map/ppermute | solution.py:167
  27.1 25.0 %collective-permute-start.4 = (bf16[64,2176]{1,0:T(8,128)(2,1)S(1)}, bf16[64,2176]{1,0:T(8,128)(2,1)S(1)}, u32[]{:S(2)}, u32[]{:S(2)}) collective-permute-start(bf16[64,2176]{1,0:T(8,128)(2,1)S(1)} %get-tuple-element.231), channel_id=1, source_target_pairs={{0,4},{4,0},{8,20},{12,16},{16,12},{20,8},{24,28},{28,24},{1,5},{5... | collective-permute-start | bytes 835592 | tf_op jit(solution)/shard_map/ppermute | solution.py:167
  78.8 36.0 %collective-permute-start.14 = (bf16[1,512,2048]{2,1,0:T(8,128)(2,1)S(1)}, bf16[1,512,2048]{2,1,0:T(8,128)(2,1)}, u32[]{:S(2)}, u32[]{:S(2)}) collective-permute-start(bf16[1,512,2048]{2,1,0:T(8,128)(2,1)S(1)} %bitcast.442), channel_id=1, source_target_pairs={{0,16},{16,0},{1,17},{17,1},{2,18},{18,2},{3,19},{19,3},{4,20},{20... | collective-permute-start | bytes 6291464 | tf_op jit(solution)/shard_map/ppermute | solution.py:73
  99.0 38.4 %collective-permute-start.17 = (bf16[128,2048]{1,0:T(8,128)(2,1)}, bf16[128,2048]{1,0:T(8,128)(2,1)}, u32[]{:S(2)}, u32[]{:S(2)}) collective-permute-start(bf16[128,2048]{1,0:T(8,128)(2,1)} %param.20), channel_id=1, source_target_pairs={{0,0},{1,4},{2,8},{3,12},{4,20},{5,24},{6,28},{7,16},{8,9},{9,13},... | collective-permute-start | bytes 1572872 | tf_op jit(solution)/shard_map/ppermute | solution.py:365
  220.1 24.9 %collective-permute-start.33 = (bf16[128,4224]{1,0:T(8,128)(2,1)S(1)}, bf16[128,4224]{1,0:T(8,128)(2,1)}, u32[]{:S(2)}, u32[]{:S(2)}) collective-permute-start(bf16[128,4224]{1,0:T(8,128)(2,1)S(1)} %pad_maximum_fusion.15), channel_id=1, source_target_pairs={{0,4},{4,8},{8,12},{12,0},{1,5},{5,9},{9,13},{13,1},{2,6},{6,10},{... | collective-permute-start | bytes 3244040 | tf_op jit(solution)/shard_map/ppermute | solution.py:86
  221.5 26.1 %collective-permute-start.28 = (bf16[64,4224]{1,0:T(8,128)(2,1)S(1)}, bf16[64,4224]{1,0:T(8,128)(2,1)S(1)}, u32[]{:S(2)}, u32[]{:S(2)}) collective-permute-start(bf16[64,4224]{1,0:T(8,128)(2,1)S(1)} %get-tuple-element.229.refs_0_), channel_id=1, source_target_pairs={{0,2},{1,3},{2,0},{3,1},{4,6},{5,7},{6,4},{7,5},{8,10},{9,11},{10,... | collective-permute-start | bytes 1622024 | tf_op jit(solution)/shard_map/ppermute | solution.py:73
  223.0 27.3 %collective-permute-start.31 = (bf16[64,4224]{1,0:T(8,128)(2,1)S(1)}, bf16[64,4224]{1,0:T(8,128)(2,1)}, u32[]{:S(2)}, u32[]{:S(2)}) collective-permute-start(bf16[64,4224]{1,0:T(8,128)(2,1)S(1)} %get-tuple-element.228.refs_4_), channel_id=1, source_target_pairs={{0,1},{1,0},{2,3},{3,2},{4,5},{5,4},{6,7},{7,6},{8,9},{9,8},{10,11... | collective-permute-start | bytes 1622024 | tf_op jit(solution)/shard_map/ppermute | solution.py:73
  272.5 49.4 %collective-permute-start.41 = (bf16[64,4224]{1,0:T(8,128)(2,1)S(1)}, bf16[64,4224]{1,0:T(8,128)(2,1)}, u32[]{:S(2)}, u32[]{:S(2)}) collective-permute-start(bf16[64,4224]{1,0:T(8,128)(2,1)S(1)} %get-tuple-element.225.refs_0_), channel_id=1, source_target_pairs={{0,1},{1,0},{2,3},{3,2},{4,5},{5,4},{6,7},{7,6},{8,9},{9,8},{10,11... | collective-permute-start | bytes 1622024 | tf_op jit(solution)/shard_map/ppermute | solution.py:73
  278.8 68.9 %collective-permute-start.42 = (bf16[64,4224]{1,0:T(8,128)(2,1)S(1)}, bf16[64,4224]{1,0:T(8,128)(2,1)}, u32[]{:S(2)}, u32[]{:S(2)}) collective-permute-start(bf16[64,4224]{1,0:T(8,128)(2,1)S(1)} %get-tuple-element.225.refs_0_), channel_id=1, source_target_pairs={{0,2},{1,3},{2,0},{3,1},{4,6},{5,7},{6,4},{7,5},{8,10},{9,11},{10,... | collective-permute-start | bytes 1622024 | tf_op jit(solution)/shard_map/ppermute | solution.py:73
  280.7 59.9 %collective-permute-start.44 = (bf16[64,4224]{1,0:T(8,128)(2,1)S(1)}, bf16[64,4224]{1,0:T(8,128)(2,1)}, u32[]{:S(2)}, u32[]{:S(2)}) collective-permute-start(bf16[64,4224]{1,0:T(8,128)(2,1)S(1)} %get-tuple-element.224.refs_4_), channel_id=1, source_target_pairs={{0,2},{1,3},{2,0},{3,1},{4,6},{5,7},{6,4},{7,5},{8,10},{9,11},{10,... | collective-permute-start | bytes 1622024 | tf_op jit(solution)/shard_map/ppermute | solution.py:73
  290.4 57.5 %collective-permute-start.45 = (bf16[64,4224]{1,0:T(8,128)(2,1)S(1)}, bf16[64,4224]{1,0:T(8,128)(2,1)}, u32[]{:S(2)}, u32[]{:S(2)}) collective-permute-start(bf16[64,4224]{1,0:T(8,128)(2,1)S(1)} %get-tuple-element.224.refs_4_), channel_id=1, source_target_pairs={{0,1},{1,0},{2,3},{3,2},{4,5},{5,4},{6,7},{7,6},{8,9},{9,8},{10,11... | collective-permute-start | bytes 1622024 | tf_op jit(solution)/shard_map/ppermute | solution.py:73
  321.9 26.2 %collective-permute-start.43 = (bf16[64,4224]{1,0:T(8,128)(2,1)}, bf16[64,4224]{1,0:T(8,128)(2,1)S(1)}, u32[]{:S(2)}, u32[]{:S(2)}) collective-permute-start(bf16[64,4224]{1,0:T(8,128)(2,1)} %collective-permute-done.41.refs_1_), channel_id=1, source_target_pairs={{0,2},{1,3},{2,0},{3,1},{4,6},{5,7},{6,4},{7,5},{8,10},{9,11},{10,... | collective-permute-start | bytes 1622024 | tf_op jit(solution)/shard_map/ppermute | solution.py:73
  348.1 24.5 %collective-permute-start.52 = (bf16[64,4224]{1,0:T(8,128)(2,1)S(1)}, bf16[64,4224]{1,0:T(8,128)(2,1)S(1)}, u32[]{:S(2)}, u32[]{:S(2)}) collective-permute-start(bf16[64,4224]{1,0:T(8,128)(2,1)S(1)} %get-tuple-element.222.refs_12_), channel_id=1, source_target_pairs={{0,1},{1,0},{2,3},{3,2},{4,5},{5,4},{6,7},{7,6},{8,9},{9,8},{10,11... | collective-permute-start | bytes 1622024 | tf_op jit(solution)/shard_map/ppermute | solution.py:73
  351.1 33.1 %collective-permute-start.53 = (bf16[64,4224]{1,0:T(8,128)(2,1)}, bf16[64,4224]{1,0:T(8,128)(2,1)}, u32[]{:S(2)}, u32[]{:S(2)}) collective-permute-start(bf16[64,4224]{1,0:T(8,128)(2,1)} %collective-permute-done.51.refs_13_), channel_id=1, source_target_pairs={{0,1},{1,0},{2,3},{3,2},{4,5},{5,4},{6,7},{7,6},{8,9},{9,8},{10,11... | collective-permute-start | bytes 1622024 | tf_op jit(solution)/shard_map/ppermute | solution.py:73
  361.9 55.9 %collective-permute-start.54 = (bf16[2,2,64,4224]{3,2,0,1:T(8,128)(2,1)}, bf16[2,2,64,4224]{3,2,0,1:T(8,128)(2,1)}, u32[]{:S(2)}, u32[]{:S(2)}) collective-permute-start(bf16[2,2,64,4224]{3,2,0,1:T(8,128)(2,1)} %bitcast.426), channel_id=1, source_target_pairs={{0,2},{1,3},{2,0},{3,1},{4,6},{5,7},{6,4},{7,5},{8,10},{9,11},{10,... | collective-permute-start | bytes 6488072 | tf_op jit(solution)/shard_map/ppermute | solution.py:73
  362.1 68.5 %collective-permute-start.55 = (bf16[2,2,64,4224]{3,2,0,1:T(8,128)(2,1)}, bf16[2,2,64,4224]{3,2,0,1:T(8,128)(2,1)}, u32[]{:S(2)}, u32[]{:S(2)}) collective-permute-start(bf16[2,2,64,4224]{3,2,0,1:T(8,128)(2,1)} %bitcast.425), channel_id=1, source_target_pairs={{0,1},{1,0},{2,3},{3,2},{4,5},{5,4},{6,7},{7,6},{8,9},{9,8},{10,11... | collective-permute-start | bytes 6488072 | tf_op jit(solution)/shard_map/ppermute | solution.py:73
  463.3 39.3 %collective-permute-start.58 = (bf16[2,2,64,4224]{3,2,0,1:T(8,128)(2,1)S(1)}, bf16[2,2,64,4224]{3,2,0,1:T(8,128)(2,1)S(1)}, u32[]{:S(2)}, u32[]{:S(2)}) collective-permute-start(bf16[2,2,64,4224]{3,2,0,1:T(8,128)(2,1)S(1)} %bitcast.495), channel_id=1, source_target_pairs={{0,2},{1,3},{2,0},{3,1},{4,6},{5,7},{6,4},{7,5},{8,10},{9,11},{10,... | collective-permute-start | bytes 6488072 | tf_op jit(solution)/shard_map/ppermute | solution.py:73
  464.3 39.5 %collective-permute-start.59 = (bf16[2,2,64,4224]{3,2,0,1:T(8,128)(2,1)S(1)}, bf16[2,2,64,4224]{3,2,0,1:T(8,128)(2,1)S(1)}, u32[]{:S(2)}, u32[]{:S(2)}) collective-permute-start(bf16[2,2,64,4224]{3,2,0,1:T(8,128)(2,1)S(1)} %bitcast.496), channel_id=1, source_target_pairs={{0,1},{1,0},{2,3},{3,2},{4,5},{5,4},{6,7},{7,6},{8,9},{9,8},{10,11... | collective-permute-start | bytes 6488072 | tf_op jit(solution)/shard_map/ppermute | solution.py:73
  471.7 55.4 %collective-permute-start.62 = (bf16[128,4224]{1,0:T(8,128)(2,1)S(1)}, bf16[128,4224]{1,0:T(8,128)(2,1)}, u32[]{:S(2)}, u32[]{:S(2)}) collective-permute-start(bf16[128,4224]{1,0:T(8,128)(2,1)S(1)} %bitcast.501), channel_id=1, source_target_pairs={{0,4},{4,8},{8,12},{12,0},{1,5},{5,9},{9,13},{13,1},{2,6},{6,10},{... | collective-permute-start | bytes 3244040 | tf_op jit(solution)/shard_map/ppermute | solution.py:86
  587.2 28.7 %collective-permute-start.71 = (bf16[1,512,2048]{2,1,0:T(8,128)(2,1)}, bf16[1,512,2048]{2,1,0:T(8,128)(2,1)}, u32[]{:S(2)}, u32[]{:S(2)}) collective-permute-start(bf16[1,512,2048]{2,1,0:T(8,128)(2,1)} %bitcast.89), channel_id=1, source_target_pairs={{0,16},{16,0},{1,17},{17,1},{2,18},{18,2},{3,19},{19,3},{4,20},{20... | collective-permute-start | bytes 6291464 | tf_op jit(solution)/shard_map/ppermute | solution.py:73
  639.9 29.2 %collective-permute-start.74 = (bf16[128,2048]{1,0:T(8,128)(2,1)}, bf16[128,2048]{1,0:T(8,128)(2,1)}, u32[]{:S(2)}, u32[]{:S(2)}) collective-permute-start(bf16[128,2048]{1,0:T(8,128)(2,1)} %get-tuple-element.194), channel_id=1, source_target_pairs={{0,12},{4,0},{8,4},{12,8},{1,13},{5,1},{9,5},{13,9},{2,14},{6,2},{... | collective-permute-start | bytes 1572872 | tf_op jit(solution)/shard_map/ppermute | solution.py:86
  639.9 50.0 %collective-permute-start.75 = (bf16[128,2048]{1,0:T(8,128)(2,1)}, bf16[128,2048]{1,0:T(8,128)(2,1)}, u32[]{:S(2)}, u32[]{:S(2)}) collective-permute-start(bf16[128,2048]{1,0:T(8,128)(2,1)} %get-tuple-element.193), channel_id=1, source_target_pairs={{0,8},{4,12},{8,0},{12,4},{1,9},{5,13},{9,1},{13,5},{2,10},{6,14},... | collective-permute-start | bytes 1572872 | tf_op jit(solution)/shard_map/ppermute | solution.py:86
  644.1 45.8 %collective-permute-start.76 = (bf16[128,2048]{1,0:T(8,128)(2,1)}, bf16[128,2048]{1,0:T(8,128)(2,1)}, u32[]{:S(2)}, u32[]{:S(2)}) collective-permute-start(bf16[128,2048]{1,0:T(8,128)(2,1)} %get-tuple-element.192), channel_id=1, source_target_pairs={{0,4},{4,8},{8,12},{12,0},{1,5},{5,9},{9,13},{13,1},{2,6},{6,10},{... | collective-permute-start | bytes 1572872 | tf_op jit(solution)/shard_map/ppermute | solution.py:86
  708.8 25.1 %collective-permute-start.78 = (bf16[512,2048]{1,0:T(8,128)(2,1)}, bf16[512,2048]{1,0:T(8,128)(2,1)}, u32[]{:S(2)}, u32[]{:S(2)}) collective-permute-start(bf16[512,2048]{1,0:T(8,128)(2,1)} %convolution_convert_fusion.7), channel_id=1, source_target_pairs={{0,16},{16,0},{1,17},{17,1},{2,18},{18,2},{3,19},{19,3},{4,20},{20... | collective-permute-start | bytes 6291464 | tf_op jit(solution)/shard_map/ppermute | solution.py:73
  723.3 47.4 %collective-permute-start.86 = (bf16[1024,1536]{1,0:T(8,128)(2,1)}, bf16[1024,1536]{1,0:T(8,128)(2,1)S(1)}, u32[]{:S(2)}, u32[]{:S(2)}) collective-permute-start(bf16[1024,1536]{1,0:T(8,128)(2,1)} %fusion.24), channel_id=1, source_target_pairs={{0,16},{16,0},{1,17},{17,1},{2,18},{18,2},{3,19},{19,3},{4,20},{20... | collective-permute-start | bytes 9437192 | tf_op jit(solution)/shard_map/ppermute | solution.py:73
  729.5 44.9 %collective-permute-start.83 = (bf16[2,4,64,640]{3,2,1,0:T(8,128)(2,1)S(1)}, bf16[2,4,64,640]{3,2,1,0:T(8,128)(2,1)S(1)}, u32[]{:S(2)}, u32[]{:S(2)}) collective-permute-start(bf16[2,4,64,640]{3,2,1,0:T(8,128)(2,1)S(1)} %get-tuple-element.182), channel_id=1, source_target_pairs={{0,12},{4,0},{8,4},{12,8},{1,13},{5,1},{9,5},{13,9},{2,14},{6,2},{... | collective-permute-start | bytes 1966088 | tf_op jit(solution)/shard_map/ppermute | solution.py:86
  739.7 57.2 %collective-permute-start.84 = (bf16[2,4,64,640]{3,2,1,0:T(8,128)(2,1)S(1)}, bf16[2,4,64,640]{3,2,1,0:T(8,128)(2,1)}, u32[]{:S(2)}, u32[]{:S(2)}) collective-permute-start(bf16[2,4,64,640]{3,2,1,0:T(8,128)(2,1)S(1)} %get-tuple-element.183), channel_id=1, source_target_pairs={{0,8},{4,12},{8,0},{12,4},{1,9},{5,13},{9,1},{13,5},{2,10},{6,14},... | collective-permute-start | bytes 1966088 | tf_op jit(solution)/shard_map/ppermute | solution.py:86
  752.0 44.9 %collective-permute-start.85 = (bf16[2,4,64,640]{3,2,1,0:T(8,128)(2,1)S(1)}, bf16[2,4,64,640]{3,2,1,0:T(8,128)(2,1)S(1)}, u32[]{:S(2)}, u32[]{:S(2)}) collective-permute-start(bf16[2,4,64,640]{3,2,1,0:T(8,128)(2,1)S(1)} %get-tuple-element.181), channel_id=1, source_target_pairs={{0,4},{4,8},{8,12},{12,0},{1,5},{5,9},{9,13},{13,1},{2,6},{6,10},{... | collective-permute-start | bytes 1966088 | tf_op jit(solution)/shard_map/ppermute | solution.py:86
  765.7 49.3 %collective-permute-start.90 = (bf16[128,2048]{1,0:T(8,128)(2,1)}, bf16[128,2048]{1,0:T(8,128)(2,1)}, u32[]{:S(2)}, u32[]{:S(2)}) collective-permute-start(bf16[128,2048]{1,0:T(8,128)(2,1)} %fusion.92), channel_id=1, source_target_pairs={{0,0},{4,1},{8,2},{12,3},{20,4},{24,5},{28,6},{16,7},{9,8},{13,9},... | collective-permute-start | bytes 1572872 | tf_op jit(solution)/shard_map/ppermute | solution.py:544
  (209 other events, 2790.5 us)

commit v4 on v3

--- a/solution.py
+++ b/solution.py
@@ -336,7 +336,21 @@
     down_full = jnp.concatenate(list(dp_gather(down_weight[0])), axis=1)
 
     packed, small = tie(packed, small)
-    small = every_gather(small).reshape(n_all, -1)
+    small = every_gather(small)
+    qkv_w = jnp.zeros((n_dp, n_sq, n_cl, shard, pack), bf16)
+    rank = cl * n_dp + dp
+    qkv_pieces = [packed, shift(packed, 1)]
+    inputs_low = to_sequence(tokens).reshape(rows, width)
+    upstream_low = jnp.concatenate([cotangent, codes], axis=-1)
+    qkv_pieces[1], inputs_low = tie(qkv_pieces[1], inputs_low)
+    inputs = inputs_low.astype(f32)
+    inputs_all = spread(inputs_low)
+    for _ in range(2, n_sq - 1):
+        qkv_pieces.append(shift(qkv_pieces[-1], 1))
+    qkv_pieces[-1], inputs_all, o_weight, small = tie(
+        qkv_pieces[-1], inputs_all, o_weight, small
+    )
+    small = small.reshape(n_all, -1)
     router_t = small[:, :n_router].reshape(n_all, experts, shard)
     router_t = jnp.transpose(router_t, (1, 0, 2)).reshape(experts, width)
     gains = small[:, n_router:n_small].reshape(-1).astype(f32)
@@ -344,24 +358,13 @@
     ffn_gain = gains[width : 2 * width]
     q_gain = gains[2 * width : 2 * width + HD]
     k_gain = gains[2 * width + HD :]
-
-    qkv_w = jnp.zeros((n_dp, n_sq, n_cl, shard, pack), bf16)
-    rank = cl * n_dp + dp
-    qkv_pieces = [packed, shift(packed, 1)]
-    inputs_low = to_sequence(tokens).reshape(rows, width)
-    upstream_low = jnp.concatenate([cotangent, codes], axis=-1)
+    qkv_pieces.append(shift(qkv_pieces[-1], 1))
+    qkv_pieces[-1], gu_full, down_full, upstream_low = tie(
+        qkv_pieces[-1], gu_full, down_full, upstream_low
+    )
     upstream_low = to_sequence(upstream_low).reshape(rows, -1)
-    qkv_pieces[1], inputs_low, upstream_low = tie(qkv_pieces[1], inputs_low, upstream_low)
-    inputs = inputs_low.astype(f32)
-    inputs_all = spread(inputs_low)
-    for _ in range(2, n_sq - 1):
-        qkv_pieces.append(shift(qkv_pieces[-1], 1))
-    qkv_pieces[-1], inputs_all, gu_full, down_full, o_weight, upstream_low = tie(
-        qkv_pieces[-1], inputs_all, gu_full, down_full, o_weight, upstream_low
-    )
     upstream = upstream_low[:, :width].astype(f32)
     own_codes = upstream_low[:, width : width + experts].astype(f32)
-    qkv_pieces.append(shift(qkv_pieces[-1], 1))
     o_mine = lax.ppermute(o_weight, ("dp", "sq", "cl"), head_pairs())
     inputs_all = dp_rows(jnp.concatenate(inputs_all)).reshape(length, width).astype(f32)
 
@@ -446,16 +449,15 @@
     per = 2
     n_chunk = n_sq // per
     ins, actives, out_grads, gu_grads, backs = [], [], [], [], []
-    arrived = []
-    moving = hidden_wide
-    for t in range(n_sq):
-        arrived += spread(moving)
-        if t == 0:
-            moving = shift(moving, 1)
-        elif t + 1 < n_sq:
+    turns = list(range(1, n_sq)) + [0]
+    arrived = [None] * n_sq
+    moving, arrived[0] = tie(shift(hidden_wide, 1), spread(hidden_wide))
+    for t in range(1, n_sq):
+        arrived[t] = spread(moving)
+        if t + 1 < n_sq:
             moving = shift(moving, 1)
     for chunk in range(n_chunk):
-        pieces = arrived[chunk * per * 8 : (chunk + 1) * per * 8]
+        pieces = sum([arrived[t] for t in turns[chunk * per : (chunk + 1) * per]], [])
         expert_in, grad_slot, gate_lanes, chosen = pull_pieces(
             code_pick, pieces, 2 * per, capacity, width
         )
@@ -507,7 +509,7 @@
     down_parts = [dot_tn(activated, columns(out_grads, m)) for m in range(n_dp)]
     back_first, gu_parts, down_parts = tie(back_first, gu_parts, down_parts)
     backs = [v.reshape(rows, -1) for v in backs + list(fold_last(back_first))]
-    back = ring_scatter(backs).astype(bf16).astype(f32)
+    back = ring_scatter(backs[-1:] + backs[:-1]).astype(bf16).astype(f32)
     output = (middle + back[:, width : 2 * width]).astype(bf16)
 
     pair_own = back[:, 2 * width :]
@@ -538,12 +540,8 @@
         jnp.einsum("hqk,kd->qhd", score_grad, keys, preferred_element_type=f32) * score_scale
     )
     kv_sum = jnp.concatenate([key_part, value_part], axis=-1).reshape(n_dp, -1, 2 * HD)
+    kv_sum, o_got[:2] = tie(kv_sum, o_got[:2])
     kv_sum = dp_sum(kv_sum).reshape(length, 2 * HD)
-    query_grad, o_got = tie(query_grad, o_got)
-    o_got = o_parts[0].astype(f32) + sum(v.astype(f32) for v in o_got)
-    o_share = lax.ppermute(
-        o_got.astype(bf16), ("dp", "sq", "cl"), [(b, a) for a, b in head_pairs()]
-    )
     key_rot_grad = rotate_back(kv_sum[:, None, :HD], cosine, sine_table)
     k_gain_grad = jnp.sum(key_rot_grad * k_proj * k_scale, axis=(0, 1))
     k_gain_grad = jnp.where(dp == 0, k_gain_grad, 0.0)
@@ -556,22 +554,36 @@
     qkv_low = jnp.concatenate([q_low, kv_low], axis=-1)
     qkv_low, gu_parts, down_parts = tie(qkv_low, gu_parts, down_parts)
     gu_share, down_share = dp_fold(gu_parts), dp_fold(down_parts)
-    w_grad = dot_tn(normed_all, qkv_low).reshape(n_dp, n_sq, n_cl, shard, pack)
-    w_parts = [take(w_grad, (zi - t) % n_sq, 1) for t in range(n_sq)]
-    w_got = [shift(w_parts[t].astype(bf16), -t) for t in range(1, n_sq)]
+    w_grad = dot_tn(qkv_low, normed_all)
+    size = n_cl * shard
+
+    def w_part(t):
+        first = ((zi - t) % n_sq) * size
+        parts = [
+            lax.dynamic_slice_in_dim(w_grad, m * n_sq * size + first, size, 1)
+            for m in range(n_dp)
+        ]
+        return jnp.concatenate(parts)
+
+    w_grad, o_got[2:] = tie(w_grad, o_got[2:])
+    w_got = [shift(w_part(t).astype(bf16), -t) for t in range(1, n_sq)]
+    o_got = o_parts[0].astype(f32) + sum(v.astype(f32) for v in o_got)
+    o_share = lax.ppermute(
+        o_got.astype(bf16), ("dp", "sq", "cl"), [(b, a) for a, b in head_pairs()]
+    )
     normed_grad = [dot_nt(low_m, qkv_w) for low_m in qkv_low.reshape(n_dp, -1, pack)]
     normed_first = fold_first(dp_fold(normed_grad).reshape(1, 2, n_cl, rows // 2, width))
     normed_grad = fold_last(normed_first).reshape(rows, width)
     normed_grad, w_got, gu_share, down_share = tie(normed_grad, w_got, gu_share, down_share)
-    w_got = w_parts[0].astype(f32) + sum(v.astype(f32) for v in w_got)
+    w_got = w_part(0) + sum(v.astype(f32) for v in w_got)
     attn_gain_grad = jnp.sum(normed_grad * inputs * first_scale, axis=0)
     input_grad = middle_grad + norm_back(inputs, first_scale, attn_gain, normed_grad)
     input_grad = from_sequence(input_grad.astype(bf16).reshape(nl, bl, width))
 
     w_got, o_share = tie(w_got, o_share)
     o_share = o_share.astype(f32)
-    w_grad = w_got.astype(bf16)
-    w_grad = jnp.transpose(w_grad, (1, 0, 2, 3)).reshape(tp, shard, pack)
+    w_grad = w_got.astype(bf16).reshape(n_dp, pack, n_cl, shard)
+    w_grad = jnp.transpose(w_grad, (2, 0, 3, 1)).reshape(tp, shard, pack)
     w_grad = lax.all_to_all(w_grad, ("cl", "dp"), split_axis=0, concat_axis=0, tiled=True)
     w_grad = jnp.transpose(w_grad.reshape(n_cl, n_dp, shard, pack), (2, 0, 1, 3)).astype(f32)
     q_share = w_grad[..., :hw].reshape(shard, -1)

time: 848 us -> 799 us (0.942)
  waiting for transfers between devices: 352 us -> 334 us
  other arithmetic: 108 us -> 92.3 us
    ppermute x4, waiting for transfers between devices: 22.2 us -> 0.93 us  [to_sequence(): got.append(lax.ppermute(take(v, (m + zi) % nl), ('dp', 'sq'), pairs))]
    ppermute x18, waiting for transfers between devices: 140 us -> 122 us  [shift(): return lax.ppermute(v, 'sq', [(i, (i + by) % n) for i in range(n)])]
    ppermute x63, waiting for transfers between devices: 179 us -> 192 us  [flip(): return lax.ppermute(v, axis, [(i, i ^ bit) for i in range(n)])]
    all_to_all x1, waiting for transfers between devices: 0.01 us -> 10.7 us  [every_scatter(): lax.all_to_all(v, ('dp', 'sq', 'cl'), split_axis=0, concat_axis=0, tiled=...]
    unnamed x313 -> x295, local copies, waits for them, and re-layouts: 28.7 us -> 35.4 us
  transfers between devices with their start and end apart: 95 -> 95, of which waited for: 48 -> 51; matrix products, arithmetic and copies ran while one was open for 28% -> 29% of each run, Pallas kernels for 2% -> 2%
where the time goes in v4:
time: 799 us; the launch traced here: 787 us
  waiting for transfers between devices  334 us (42%)
  matrix products  128 us (16%)
  starting transfers between devices  125 us (16%)
  other arithmetic  92.3 us (12%)
  local copies, waits for them, and re-layouts  88.2 us (11%)
  Pallas kernels  15.6 us (2%)
    ppermute x63, waiting for transfers between devices, flip(): return lax.ppermute(v, axis, [(i, i ^ bit) for i in range(n)])  192 us
    ppermute x18, waiting for transfers between devices, shift(): return lax.ppermute(v, 'sq', [(i, (i + by) % n) for i in range(n)])  122 us
    ppermute x63, starting transfers between devices, flip(): return lax.ppermute(v, axis, [(i, i ^ bit) for i in range(n)])  68.4 us
    dot_general x7, matrix products, dot_tn(): lax.dot_general(a, b, (((0,), (0,)), ((), ())), preferred_element_type=f32)  39.7 us
    unnamed x295, local copies, waits for them, and re-layouts  35.4 us
    dot_general x8, matrix products, dot(): return jnp.dot(a, b, preferred_element_type=f32)  25.9 us
    dot_general x8, matrix products, dot_nt(): lax.dot_general(a, b, (((1,), (1,)), ((), ())), preferred_element_type=f32)  21.4 us
  transfers between devices with their start and end apart: 95, of which 51 were waited for; matrix products, arithmetic and copies ran while one was open for 29% of the time, Pallas kernels for 2%

profile of v4, /device:TPU:1, one launch (start us, length us, event | category | flops | bytes accessed | tf_op | source)
XLA Modules:
  0.0 787.0 jit_solution(16927134735337871385)
XLA Ops:
  35.4 7.8 collective-permute-done
  88.9 7.0 collective-permute-done.10
  116.4 10.9 %fusion.177 = (f32[4,1024]{1,0:T(4,128)S(1)}, f32[4,1024,1024]{1,2,0:T(8,128)}) fusion(pred[1024,1024]{0,1:T(8,128)(4,1)} %compare_and_fusion, bf16[1024,128,1]{0,1,2:T(8,128)(2,1)S(1)} %copy-done.55, bf16[1024,4,128]{0,2,1:T(8,128)(2,1)} %fusion.52), kind=kOutput, calls=%fused_computation.437 | convolution fusion | flops 1090520064 | bytes 19152896 | tf_op jit(solution)/shard_map/sub | solution.py:412
  132.4 7.1 fusion.58
  139.5 7.6 collective-permute-done.20
  148.3 12.5 %collective-permute-done.21 = bf16[128,2048]{1,0:T(8,128)(2,1)S(1)} collective-permute-done((bf16[128,2048]{1,0:T(8,128)(2,1)S(1)}, bf16[128,2048]{1,0:T(8,128)(2,1)S(1)}, u32[]{:S(2)}, u32[]{:S(2)}) %collective-permute-start.21) | collective-permute-done | bytes 524320 | tf_op jit(solution)/shard_map/ppermute | solution.py:86
  180.7 9.0 %collective-permute-done.23 = bf16[1,2,64,2048]{3,2,1,0:T(8,128)(2,1)S(1)} collective-permute-done((bf16[1,2,64,2048]{3,2,1,0:T(8,128)(2,1)S(1)}, bf16[1,2,64,2048]{3,2,1,0:T(8,128)(2,1)S(1)}, u32[]{:S(2)}, u32[]{:S(2)}) %collective-permute-start.23) | collective-permute-done | bytes 524320 | tf_op jit(solution)/shard_map/ppermute | solution.py:73
  208.7 10.3 %collective-permute-done.28.refs_9_ = bf16[64,4224]{1,0:T(8,128)(2,1)S(1)} collective-permute-done((bf16[64,4224]{1,0:T(8,128)(2,1)S(1)}, bf16[64,4224]{1,0:T(8,128)(2,1)S(1)}, u32[]{:S(2)}, u32[]{:S(2)}) %collective-permute-start.28) | collective-permute-done | bytes 540704 | tf_op jit(solution)/shard_map/ppermute | solution.py:73
  221.0 10.1 %collective-permute-done.29.refs_10_ = bf16[64,4224]{1,0:T(8,128)(2,1)S(1)} collective-permute-done((bf16[64,4224]{1,0:T(8,128)(2,1)S(1)}, bf16[64,4224]{1,0:T(8,128)(2,1)S(1)}, u32[]{:S(2)}, u32[]{:S(2)}) %collective-permute-start.29) | collective-permute-done | bytes 540704 | tf_op jit(solution)/shard_map/ppermute | solution.py:73
  231.1 11.6 %collective-permute-done.30.refs_11_ = bf16[64,4224]{1,0:T(8,128)(2,1)S(1)} collective-permute-done((bf16[64,4224]{1,0:T(8,128)(2,1)S(1)}, bf16[64,4224]{1,0:T(8,128)(2,1)S(1)}, u32[]{:S(2)}, u32[]{:S(2)}) %collective-permute-start.30) | collective-permute-done | bytes 540704 | tf_op jit(solution)/shard_map/ppermute | solution.py:73
  247.7 9.6 %collective-permute-done.34.refs_1_ = bf16[64,4224]{1,0:T(8,128)(2,1)} collective-permute-done((bf16[64,4224]{1,0:T(8,128)(2,1)S(1)}, bf16[64,4224]{1,0:T(8,128)(2,1)}, u32[]{:S(2)}, u32[]{:S(2)}) %collective-permute-start.34) | collective-permute-done | bytes 540704 | tf_op jit(solution)/shard_map/ppermute | solution.py:73
  258.2 12.0 %collective-permute-done.40 = bf16[128,4224]{1,0:T(8,128)(2,1)} collective-permute-done((bf16[128,4224]{1,0:T(8,128)(2,1)S(1)}, bf16[128,4224]{1,0:T(8,128)(2,1)}, u32[]{:S(2)}, u32[]{:S(2)}) %collective-permute-start.40) | collective-permute-done | bytes 1081376 | tf_op jit(solution)/shard_map/ppermute | solution.py:86
  284.6 8.3 %collective-permute-done.44.refs_13_ = bf16[64,4224]{1,0:T(8,128)(2,1)} collective-permute-done((bf16[64,4224]{1,0:T(8,128)(2,1)S(1)}, bf16[64,4224]{1,0:T(8,128)(2,1)}, u32[]{:S(2)}, u32[]{:S(2)}) %collective-permute-start.44) | collective-permute-done | bytes 540704 | tf_op jit(solution)/shard_map/ppermute | solution.py:73
  307.2 8.7 %collective-permute-done.43.refs_11_ = bf16[64,4224]{1,0:T(8,128)(2,1)S(1)} collective-permute-done((bf16[64,4224]{1,0:T(8,128)(2,1)}, bf16[64,4224]{1,0:T(8,128)(2,1)S(1)}, u32[]{:S(2)}, u32[]{:S(2)}) %collective-permute-start.43) | collective-permute-done | bytes 540704 | tf_op jit(solution)/shard_map/ppermute | solution.py:73
  319.6 7.8 pull.2
  328.5 7.3 fusion.180
  365.3 7.8 pull.3
  390.1 15.6 %collective-permute-done.54 = bf16[2,2,64,4224]{3,2,0,1:T(8,128)(2,1)} collective-permute-done((bf16[2,2,64,4224]{3,2,0,1:T(8,128)(2,1)}, bf16[2,2,64,4224]{3,2,0,1:T(8,128)(2,1)}, u32[]{:S(2)}, u32[]{:S(2)}) %collective-permute-start.54) | collective-permute-done | bytes 2162720 | tf_op jit(solution)/shard_map/ppermute | solution.py:73
  424.9 8.0 %collective-permute-done.56 = bf16[2,64,4224]{2,1,0:T(8,128)(2,1)S(1)} collective-permute-done((bf16[2,64,4224]{2,1,0:T(8,128)(2,1)S(1)}, bf16[2,64,4224]{2,1,0:T(8,128)(2,1)S(1)}, u32[]{:S(2)}, u32[]{:S(2)}) %collective-permute-start.56) | collective-permute-done | bytes 1081376 | tf_op jit(solution)/shard_map/ppermute | solution.py:73
  449.9 11.2 %fusion.24 = bf16[1024,1536]{1,0:T(8,128)(2,1)} fusion(bf16[640,1024]{1,0:T(8,128)(2,1)S(1)} %copy-done.48, bf16[640,1024]{1,0:T(8,128)(2,1)S(1)} %copy-done.46, bf16[640,1536]{1,0:T(8,128)(2,1)S(1)} %copy-done.44, bf16[640,768]{1,0:T(8,128)(2,1)S(1)} %copy-done.123, bf16[640,768]{1,0:T(8,128)(2,1)S(1)} %copy-done.121), kind=kOutput, calls=%fused_computation.68 | convolution fusion | flops 4043571200 | bytes 9699328 | tf_op jit(solution)/shard_map/dot_general | solution.py:64
  461.1 11.3 %fusion.20 = f32[1024,1536]{1,0:T(8,128)} fusion(bf16[640,1024]{1,0:T(8,128)(2,1)S(1)} %copy-done.47, bf16[640,1024]{1,0:T(8,128)(2,1)S(1)} %copy-done.45, bf16[640,1536]{1,0:T(8,128)(2,1)S(1)} %copy-done.44, bf16[640,768]{1,0:T(8,128)(2,1)S(1)} %copy-done.123, bf16[640,768]{1,0:T(8,128)(2,1)S(1)} %copy-done.121), kind=kOutput, calls=%fused_computation.64 | convolution fusion | flops 4043571200 | bytes 12845056 | tf_op jit(solution)/shard_map/dot_general | solution.py:64
  472.8 15.3 %collective-permute-done.58 = bf16[2,2,64,4224]{3,2,0,1:T(8,128)(2,1)S(1)} collective-permute-done((bf16[2,2,64,4224]{3,2,0,1:T(8,128)(2,1)S(1)}, bf16[2,2,64,4224]{3,2,0,1:T(8,128)(2,1)S(1)}, u32[]{:S(2)}, u32[]{:S(2)}) %collective-permute-start.58) | collective-permute-done | bytes 2162720 | tf_op jit(solution)/shard_map/ppermute | solution.py:73
  491.3 19.1 %collective-permute-done.60 = bf16[2,64,4224]{2,1,0:T(8,128)(2,1)S(1)} collective-permute-done((bf16[2,64,4224]{2,1,0:T(8,128)(2,1)S(1)}, bf16[2,64,4224]{2,1,0:T(8,128)(2,1)S(1)}, u32[]{:S(2)}, u32[]{:S(2)}) %collective-permute-start.60) | collective-permute-done | bytes 1081376 | tf_op jit(solution)/shard_map/ppermute | solution.py:73
  511.5 18.4 %collective-permute-done.64 = bf16[128,4224]{1,0:T(8,128)(2,1)S(1)} collective-permute-done((bf16[128,4224]{1,0:T(8,128)(2,1)S(1)}, bf16[128,4224]{1,0:T(8,128)(2,1)S(1)}, u32[]{:S(2)}, u32[]{:S(2)}) %collective-permute-start.64) | collective-permute-done | bytes 1081376 | tf_op jit(solution)/shard_map/ppermute | solution.py:86
  549.5 11.1 %collective-permute-start.71 = (bf16[1,512,2048]{2,1,0:T(8,128)(2,1)}, bf16[1,512,2048]{2,1,0:T(8,128)(2,1)}, u32[]{:S(2)}, u32[]{:S(2)}) collective-permute-start(bf16[1,512,2048]{2,1,0:T(8,128)(2,1)} %bitcast.89), channel_id=1, source_target_pairs={{0,16},{16,0},{1,17},{17,1},{2,18},{18,2},{3,19},{19,3},{4,20},{20... | collective-permute-start | bytes 6291464 | tf_op jit(solution)/shard_map/ppermute | solution.py:73
  589.2 7.1 fusion.1
  603.9 8.0 %fusion.3 = bf16[4,1024,1024]{1,2,0:T(8,128)(2,1)S(1)} fusion(f32[1024,1024,4]{1,0,2:T(8,128)} %get-tuple-element.307, f32[4,1024]{1,0:T(4,128)S(1)} %get-tuple-element.306, f32[4,1024,1024]{1,2,0:T(8,128)S(1)} %bitcast.435, f32[4,1024]{1,0:T(4,128)S(1)} %copy-done.101), kind=kLoop, calls=%fused_computation.5 | loop fusion | flops 16777216 | bytes 41975808 | tf_op jit(solution)/shard_map/convert_element_type | solution.py:534
  616.2 22.4 %collective-permute-done.75 = bf16[128,2048]{1,0:T(8,128)(2,1)} collective-permute-done((bf16[128,2048]{1,0:T(8,128)(2,1)}, bf16[128,2048]{1,0:T(8,128)(2,1)}, u32[]{:S(2)}, u32[]{:S(2)}) %collective-permute-start.75) | collective-permute-done | bytes 524320 | tf_op jit(solution)/shard_map/ppermute | solution.py:86
  685.5 8.3 %collective-permute-done.78 = bf16[1,2,64,2048]{3,2,1,0:T(8,128)(2,1)S(1)} collective-permute-done((bf16[1,2,64,2048]{3,2,1,0:T(8,128)(2,1)S(1)}, bf16[1,2,64,2048]{3,2,1,0:T(8,128)(2,1)S(1)}, u32[]{:S(2)}, u32[]{:S(2)}) %collective-permute-start.78) | collective-permute-done | bytes 524320 | tf_op jit(solution)/shard_map/ppermute | solution.py:73
  714.7 29.1 %collective-permute-done.84 = bf16[1280,256]{1,0:T(8,128)(2,1)S(1)} collective-permute-done((bf16[1280,256]{1,0:T(8,128)(2,1)S(1)}, bf16[1280,256]{1,0:T(8,128)(2,1)S(1)}, u32[]{:S(2)}, u32[]{:S(2)}) %collective-permute-start.84) | collective-permute-done | bytes 655392 | tf_op jit(solution)/shard_map/ppermute | solution.py:86
  748.8 7.3 all-to-all-start.3
  759.2 10.7 %all-to-all-done.3 = f32[32,10,128]{2,1,0:T(8,128)S(1)} async-done(((f32[32,10,128]{2,1,0:T(8,128)}), f32[32,10,128]{2,1,0:T(8,128)S(1)}, u32[]{:S(2)}, u32[]{:S(2)}) %all-to-all-start.3) | async-done | bytes 163872 | tf_op jit(solution)/shard_map/all_to_all | solution.py:104
  (712 shorter events, 425.4 us)
Async XLA Ops:
  16.1 66.2 %collective-permute-start.11 = (bf16[1,1024,1536]{2,1,0:T(8,128)(2,1)}, bf16[1,1024,1536]{2,1,0:T(8,128)(2,1)}, u32[]{:S(2)}, u32[]{:S(2)}) collective-permute-start(bf16[1,1024,1536]{2,1,0:T(8,128)(2,1)} %param.23), channel_id=1, source_target_pairs={{0,16},{16,0},{1,17},{17,1},{2,18},{18,2},{3,19},{19,3},{4,20},{20... | collective-permute-start | bytes 9437192 | tf_op jit(solution)/shard_map/ppermute | solution.py:73
  16.2 31.6 %collective-permute-start.12 = (bf16[1,768,1024]{2,1,0:T(8,128)(2,1)}, bf16[1,768,1024]{2,1,0:T(8,128)(2,1)}, u32[]{:S(2)}, u32[]{:S(2)}) collective-permute-start(bf16[1,768,1024]{2,1,0:T(8,128)(2,1)} %param.24), channel_id=1, source_target_pairs={{0,16},{16,0},{1,17},{17,1},{2,18},{18,2},{3,19},{19,3},{4,20},{20... | collective-permute-start | bytes 4718600 | tf_op jit(solution)/shard_map/ppermute | solution.py:73
  27.8 31.9 %all-to-all-start.1 = ((bf16[32,10,128]{2,1,0:T(8,128)(2,1)}), bf16[32,10,128]{2,1,0:T(8,128)(2,1)S(1)}, u32[]{:S(2)}, u32[]{:S(2)}) async-start(bf16[32,10,128]{2,1,0:T(8,128)(2,1)} %broadcast_in_dim.202), calls=%async_computation.1 | async-start | bytes 262144 | tf_op jit(solution)/shard_map/all_to_all | solution.py:100
  71.9 24.0 %collective-permute-start.15 = (bf16[1,512,2048]{2,1,0:T(8,128)(2,1)S(1)}, bf16[1,512,2048]{2,1,0:T(8,128)(2,1)S(1)}, u32[]{:S(2)}, u32[]{:S(2)}) collective-permute-start(bf16[1,512,2048]{2,1,0:T(8,128)(2,1)S(1)} %bitcast.428), channel_id=1, source_target_pairs={{0,16},{16,0},{1,17},{17,1},{2,18},{18,2},{3,19},{19,3},{4,20},{20... | collective-permute-start | bytes 6291464 | tf_op jit(solution)/shard_map/ppermute | solution.py:73
  77.6 38.6 %collective-permute-start.17 = (bf16[128,2048]{1,0:T(8,128)(2,1)}, bf16[128,2048]{1,0:T(8,128)(2,1)}, u32[]{:S(2)}, u32[]{:S(2)}) collective-permute-start(bf16[128,2048]{1,0:T(8,128)(2,1)} %param.20), channel_id=1, source_target_pairs={{0,0},{1,4},{2,8},{3,12},{4,20},{5,24},{6,28},{7,16},{8,9},{9,13},... | collective-permute-start | bytes 1572872 | tf_op jit(solution)/shard_map/ppermute | solution.py:368
  202.9 28.2 %collective-permute-start.27 = (bf16[128,4224]{1,0:T(8,128)(2,1)S(1)}, bf16[128,4224]{1,0:T(8,128)(2,1)S(1)}, u32[]{:S(2)}, u32[]{:S(2)}) collective-permute-start(bf16[128,4224]{1,0:T(8,128)(2,1)S(1)} %pad_maximum_fusion.15), channel_id=1, source_target_pairs={{0,4},{4,8},{8,12},{12,0},{1,5},{5,9},{9,13},{13,1},{2,6},{6,10},{... | collective-permute-start | bytes 3244040 | tf_op jit(solution)/shard_map/ppermute | solution.py:86
  219.1 23.6 %collective-permute-start.30 = (bf16[64,4224]{1,0:T(8,128)(2,1)S(1)}, bf16[64,4224]{1,0:T(8,128)(2,1)S(1)}, u32[]{:S(2)}, u32[]{:S(2)}) collective-permute-start(bf16[64,4224]{1,0:T(8,128)(2,1)S(1)} %collective-permute-done.28.refs_9_), channel_id=1, source_target_pairs={{0,2},{1,3},{2,0},{3,1},{4,6},{5,7},{6,4},{7,5},{8,10},{9,11},{10,... | collective-permute-start | bytes 1622024 | tf_op jit(solution)/shard_map/ppermute | solution.py:73
  244.3 25.9 %collective-permute-start.40 = (bf16[128,4224]{1,0:T(8,128)(2,1)S(1)}, bf16[128,4224]{1,0:T(8,128)(2,1)}, u32[]{:S(2)}, u32[]{:S(2)}) collective-permute-start(bf16[128,4224]{1,0:T(8,128)(2,1)S(1)} %collective-permute-done.27), channel_id=1, source_target_pairs={{0,4},{4,8},{8,12},{12,0},{1,5},{5,9},{9,13},{13,1},{2,6},{6,10},{... | collective-permute-start | bytes 3244040 | tf_op jit(solution)/shard_map/ppermute | solution.py:86
  245.8 26.0 %collective-permute-start.35 = (bf16[64,4224]{1,0:T(8,128)(2,1)S(1)}, bf16[64,4224]{1,0:T(8,128)(2,1)S(1)}, u32[]{:S(2)}, u32[]{:S(2)}) collective-permute-start(bf16[64,4224]{1,0:T(8,128)(2,1)S(1)} %get-tuple-element.254.refs_0_), channel_id=1, source_target_pairs={{0,2},{1,3},{2,0},{3,1},{4,6},{5,7},{6,4},{7,5},{8,10},{9,11},{10,... | collective-permute-start | bytes 1622024 | tf_op jit(solution)/shard_map/ppermute | solution.py:73
  247.0 25.9 %collective-permute-start.37 = (bf16[64,4224]{1,0:T(8,128)(2,1)S(1)}, bf16[64,4224]{1,0:T(8,128)(2,1)S(1)}, u32[]{:S(2)}, u32[]{:S(2)}) collective-permute-start(bf16[64,4224]{1,0:T(8,128)(2,1)S(1)} %get-tuple-element.253.refs_4_), channel_id=1, source_target_pairs={{0,2},{1,3},{2,0},{3,1},{4,6},{5,7},{6,4},{7,5},{8,10},{9,11},{10,... | collective-permute-start | bytes 1622024 | tf_op jit(solution)/shard_map/ppermute | solution.py:73
  247.3 27.4 %collective-permute-start.38 = (bf16[64,4224]{1,0:T(8,128)(2,1)S(1)}, bf16[64,4224]{1,0:T(8,128)(2,1)}, u32[]{:S(2)}, u32[]{:S(2)}) collective-permute-start(bf16[64,4224]{1,0:T(8,128)(2,1)S(1)} %get-tuple-element.253.refs_4_), channel_id=1, source_target_pairs={{0,1},{1,0},{2,3},{3,2},{4,5},{5,4},{6,7},{7,6},{8,9},{9,8},{10,11... | collective-permute-start | bytes 1622024 | tf_op jit(solution)/shard_map/ppermute | solution.py:73
  257.3 23.9 %collective-permute-start.36 = (bf16[64,4224]{1,0:T(8,128)(2,1)}, bf16[64,4224]{1,0:T(8,128)(2,1)}, u32[]{:S(2)}, u32[]{:S(2)}) collective-permute-start(bf16[64,4224]{1,0:T(8,128)(2,1)} %collective-permute-done.34.refs_1_), channel_id=1, source_target_pairs={{0,2},{1,3},{2,0},{3,1},{4,6},{5,7},{6,4},{7,5},{8,10},{9,11},{10,... | collective-permute-start | bytes 1622024 | tf_op jit(solution)/shard_map/ppermute | solution.py:73
  270.2 25.5 %collective-permute-start.47 = (bf16[128,4224]{1,0:T(8,128)(2,1)}, bf16[128,4224]{1,0:T(8,128)(2,1)}, u32[]{:S(2)}, u32[]{:S(2)}) collective-permute-start(bf16[128,4224]{1,0:T(8,128)(2,1)} %collective-permute-done.40), channel_id=1, source_target_pairs={{0,4},{4,8},{8,12},{12,0},{1,5},{5,9},{9,13},{13,1},{2,6},{6,10},{... | collective-permute-start | bytes 3244040 | tf_op jit(solution)/shard_map/ppermute | solution.py:86
  298.1 52.2 %collective-permute-start.48 = (bf16[64,4224]{1,0:T(8,128)(2,1)S(1)}, bf16[64,4224]{1,0:T(8,128)(2,1)S(1)}, u32[]{:S(2)}, u32[]{:S(2)}) collective-permute-start(bf16[64,4224]{1,0:T(8,128)(2,1)S(1)} %get-tuple-element.250.refs_0_), channel_id=1, source_target_pairs={{0,1},{1,0},{2,3},{3,2},{4,5},{5,4},{6,7},{7,6},{8,9},{9,8},{10,11... | collective-permute-start | bytes 1622024 | tf_op jit(solution)/shard_map/ppermute | solution.py:73
  304.3 59.0 %collective-permute-start.49 = (bf16[64,4224]{1,0:T(8,128)(2,1)S(1)}, bf16[64,4224]{1,0:T(8,128)(2,1)S(1)}, u32[]{:S(2)}, u32[]{:S(2)}) collective-permute-start(bf16[64,4224]{1,0:T(8,128)(2,1)S(1)} %get-tuple-element.250.refs_0_), channel_id=1, source_target_pairs={{0,2},{1,3},{2,0},{3,1},{4,6},{5,7},{6,4},{7,5},{8,10},{9,11},{10,... | collective-permute-start | bytes 1622024 | tf_op jit(solution)/shard_map/ppermute | solution.py:73
  306.6 44.4 %collective-permute-start.51 = (bf16[64,4224]{1,0:T(8,128)(2,1)S(1)}, bf16[64,4224]{1,0:T(8,128)(2,1)}, u32[]{:S(2)}, u32[]{:S(2)}) collective-permute-start(bf16[64,4224]{1,0:T(8,128)(2,1)S(1)} %get-tuple-element.249.refs_4_), channel_id=1, source_target_pairs={{0,2},{1,3},{2,0},{3,1},{4,6},{5,7},{6,4},{7,5},{8,10},{9,11},{10,... | collective-permute-start | bytes 1622024 | tf_op jit(solution)/shard_map/ppermute | solution.py:73
  315.9 47.8 %collective-permute-start.52 = (bf16[64,4224]{1,0:T(8,128)(2,1)S(1)}, bf16[64,4224]{1,0:T(8,128)(2,1)}, u32[]{:S(2)}, u32[]{:S(2)}) collective-permute-start(bf16[64,4224]{1,0:T(8,128)(2,1)S(1)} %get-tuple-element.249.refs_4_), channel_id=1, source_target_pairs={{0,1},{1,0},{2,3},{3,2},{4,5},{5,4},{6,7},{7,6},{8,9},{9,8},{10,11... | collective-permute-start | bytes 1622024 | tf_op jit(solution)/shard_map/ppermute | solution.py:73
  356.4 49.4 %collective-permute-start.54 = (bf16[2,2,64,4224]{3,2,0,1:T(8,128)(2,1)}, bf16[2,2,64,4224]{3,2,0,1:T(8,128)(2,1)}, u32[]{:S(2)}, u32[]{:S(2)}) collective-permute-start(bf16[2,2,64,4224]{3,2,0,1:T(8,128)(2,1)} %bitcast.412), channel_id=1, source_target_pairs={{0,2},{1,3},{2,0},{3,1},{4,6},{5,7},{6,4},{7,5},{8,10},{9,11},{10,... | collective-permute-start | bytes 6488072 | tf_op jit(solution)/shard_map/ppermute | solution.py:73
  363.3 43.5 %collective-permute-start.55 = (bf16[2,2,64,4224]{3,2,0,1:T(8,128)(2,1)}, bf16[2,2,64,4224]{3,2,0,1:T(8,128)(2,1)}, u32[]{:S(2)}, u32[]{:S(2)}) collective-permute-start(bf16[2,2,64,4224]{3,2,0,1:T(8,128)(2,1)} %bitcast.411), channel_id=1, source_target_pairs={{0,1},{1,0},{2,3},{3,2},{4,5},{5,4},{6,7},{7,6},{8,9},{9,8},{10,11... | collective-permute-start | bytes 6488072 | tf_op jit(solution)/shard_map/ppermute | solution.py:73
  446.9 41.2 %collective-permute-start.58 = (bf16[2,2,64,4224]{3,2,0,1:T(8,128)(2,1)S(1)}, bf16[2,2,64,4224]{3,2,0,1:T(8,128)(2,1)S(1)}, u32[]{:S(2)}, u32[]{:S(2)}) collective-permute-start(bf16[2,2,64,4224]{3,2,0,1:T(8,128)(2,1)S(1)} %bitcast.482), channel_id=1, source_target_pairs={{0,2},{1,3},{2,0},{3,1},{4,6},{5,7},{6,4},{7,5},{8,10},{9,11},{10,... | collective-permute-start | bytes 6488072 | tf_op jit(solution)/shard_map/ppermute | solution.py:73
  447.1 41.0 %collective-permute-start.59 = (bf16[2,2,64,4224]{3,2,0,1:T(8,128)(2,1)S(1)}, bf16[2,2,64,4224]{3,2,0,1:T(8,128)(2,1)S(1)}, u32[]{:S(2)}, u32[]{:S(2)}) collective-permute-start(bf16[2,2,64,4224]{3,2,0,1:T(8,128)(2,1)S(1)} %bitcast.483), channel_id=1, source_target_pairs={{0,1},{1,0},{2,3},{3,2},{4,5},{5,4},{6,7},{7,6},{8,9},{9,8},{10,11... | collective-permute-start | bytes 6488072 | tf_op jit(solution)/shard_map/ppermute | solution.py:73
  447.9 24.5 %collective-permute-start.62 = (bf16[128,4224]{1,0:T(8,128)(2,1)S(1)}, bf16[128,4224]{1,0:T(8,128)(2,1)S(1)}, u32[]{:S(2)}, u32[]{:S(2)}) collective-permute-start(bf16[128,4224]{1,0:T(8,128)(2,1)S(1)} %bitcast.488), channel_id=1, source_target_pairs={{0,4},{4,8},{8,12},{12,0},{1,5},{5,9},{9,13},{13,1},{2,6},{6,10},{... | collective-permute-start | bytes 3244040 | tf_op jit(solution)/shard_map/ppermute | solution.py:86
  472.6 38.7 %collective-permute-start.63 = (bf16[128,4224]{1,0:T(8,128)(2,1)S(1)}, bf16[128,4224]{1,0:T(8,128)(2,1)S(1)}, u32[]{:S(2)}, u32[]{:S(2)}) collective-permute-start(bf16[128,4224]{1,0:T(8,128)(2,1)S(1)} %fusion.48), channel_id=1, source_target_pairs={{0,4},{4,8},{8,12},{12,0},{1,5},{5,9},{9,13},{13,1},{2,6},{6,10},{... | collective-permute-start | bytes 3244040 | tf_op jit(solution)/shard_map/ppermute | solution.py:86
  549.5 26.8 %collective-permute-start.71 = (bf16[1,512,2048]{2,1,0:T(8,128)(2,1)}, bf16[1,512,2048]{2,1,0:T(8,128)(2,1)}, u32[]{:S(2)}, u32[]{:S(2)}) collective-permute-start(bf16[1,512,2048]{2,1,0:T(8,128)(2,1)} %bitcast.89), channel_id=1, source_target_pairs={{0,16},{16,0},{1,17},{17,1},{2,18},{18,2},{3,19},{19,3},{4,20},{20... | collective-permute-start | bytes 6291464 | tf_op jit(solution)/shard_map/ppermute | solution.py:73
  599.6 38.9 %collective-permute-start.75 = (bf16[128,2048]{1,0:T(8,128)(2,1)}, bf16[128,2048]{1,0:T(8,128)(2,1)}, u32[]{:S(2)}, u32[]{:S(2)}) collective-permute-start(bf16[128,2048]{1,0:T(8,128)(2,1)} %get-tuple-element.218), channel_id=1, source_target_pairs={{0,8},{4,12},{8,0},{12,4},{1,9},{5,13},{9,1},{13,5},{2,10},{6,14},... | collective-permute-start | bytes 1572872 | tf_op jit(solution)/shard_map/ppermute | solution.py:86
  671.6 43.1 %collective-permute-start.83 = (bf16[1280,256]{1,0:T(8,128)(2,1)S(1)}, bf16[1280,256]{1,0:T(8,128)(2,1)S(1)}, u32[]{:S(2)}, u32[]{:S(2)}) collective-permute-start(bf16[1280,256]{1,0:T(8,128)(2,1)S(1)} %pad_maximum_fusion.19), channel_id=1, source_target_pairs={{0,12},{4,0},{8,4},{12,8},{1,13},{5,1},{9,5},{13,9},{2,14},{6,2},{... | collective-permute-start | bytes 1966088 | tf_op jit(solution)/shard_map/ppermute | solution.py:86
  675.2 35.8 %collective-permute-start.86 = (bf16[1024,1536]{1,0:T(8,128)(2,1)S(1)}, bf16[1024,1536]{1,0:T(8,128)(2,1)S(1)}, u32[]{:S(2)}, u32[]{:S(2)}) collective-permute-start(bf16[1024,1536]{1,0:T(8,128)(2,1)S(1)} %copy-done.115), channel_id=1, source_target_pairs={{0,16},{16,0},{1,17},{17,1},{2,18},{18,2},{3,19},{19,3},{4,20},{20... | collective-permute-start | bytes 9437192 | tf_op jit(solution)/shard_map/ppermute | solution.py:73
  683.3 60.5 %collective-permute-start.84 = (bf16[1280,256]{1,0:T(8,128)(2,1)S(1)}, bf16[1280,256]{1,0:T(8,128)(2,1)S(1)}, u32[]{:S(2)}, u32[]{:S(2)}) collective-permute-start(bf16[1280,256]{1,0:T(8,128)(2,1)S(1)} %pad_maximum_fusion.20), channel_id=1, source_target_pairs={{0,8},{4,12},{8,0},{12,4},{1,9},{5,13},{9,1},{13,5},{2,10},{6,14},... | collective-permute-start | bytes 1966088 | tf_op jit(solution)/shard_map/ppermute | solution.py:86
  693.8 50.0 %collective-permute-start.85 = (bf16[1280,256]{1,0:T(8,128)(2,1)S(1)}, bf16[1280,256]{1,0:T(8,128)(2,1)S(1)}, u32[]{:S(2)}, u32[]{:S(2)}) collective-permute-start(bf16[1280,256]{1,0:T(8,128)(2,1)S(1)} %pad_maximum_fusion.21), channel_id=1, source_target_pairs={{0,4},{4,8},{8,12},{12,0},{1,5},{5,9},{9,13},{13,1},{2,6},{6,10},{... | collective-permute-start | bytes 1966088 | tf_op jit(solution)/shard_map/ppermute | solution.py:86
  707.0 50.8 %collective-permute-start.90 = (bf16[128,2048]{1,0:T(8,128)(2,1)}, bf16[128,2048]{1,0:T(8,128)(2,1)}, u32[]{:S(2)}, u32[]{:S(2)}) collective-permute-start(bf16[128,2048]{1,0:T(8,128)(2,1)} %fusion.90), channel_id=1, source_target_pairs={{0,0},{4,1},{8,2},{12,3},{20,4},{24,5},{28,6},{16,7},{9,8},{13,9},... | collective-permute-start | bytes 1572872 | tf_op jit(solution)/shard_map/ppermute | solution.py:571
  744.9 31.1 %collective-permute-start.88 = (bf16[64,2048]{1,0:T(8,128)(2,1)S(1)}, bf16[64,2048]{1,0:T(8,128)(2,1)S(1)}, u32[]{:S(2)}, u32[]{:S(2)}) collective-permute-start(bf16[64,2048]{1,0:T(8,128)(2,1)S(1)} %get-tuple-element.262), channel_id=1, source_target_pairs={{0,0},{4,4},{16,8},{20,12},{8,16},{12,20},{24,24},{28,28},{1,1},{5... | collective-permute-start | bytes 786440 | tf_op jit(solution)/shard_map/ppermute | solution.py:181
  747.8 28.3 %collective-permute-start.89 = (bf16[64,2048]{1,0:T(8,128)(2,1)S(1)}, bf16[64,2048]{1,0:T(8,128)(2,1)S(1)}, u32[]{:S(2)}, u32[]{:S(2)}) collective-permute-start(bf16[64,2048]{1,0:T(8,128)(2,1)S(1)} %get-tuple-element.261), channel_id=1, source_target_pairs={{4,0},{0,4},{20,8},{16,12},{12,16},{8,20},{28,24},{24,28},{5,1},{1... | collective-permute-start | bytes 786440 | tf_op jit(solution)/shard_map/ppermute | solution.py:181
  (200 other events, 2627.3 us)

commit v5 on v4

--- a/solution.py
+++ b/solution.py
@@ -540,7 +540,7 @@
         jnp.einsum("hqk,kd->qhd", score_grad, keys, preferred_element_type=f32) * score_scale
     )
     kv_sum = jnp.concatenate([key_part, value_part], axis=-1).reshape(n_dp, -1, 2 * HD)
-    kv_sum, o_got[:2] = tie(kv_sum, o_got[:2])
+    kv_sum, o_got[:1] = tie(kv_sum, o_got[:1])
     kv_sum = dp_sum(kv_sum).reshape(length, 2 * HD)
     key_rot_grad = rotate_back(kv_sum[:, None, :HD], cosine, sine_table)
     k_gain_grad = jnp.sum(key_rot_grad * k_proj * k_scale, axis=(0, 1))
@@ -565,21 +565,31 @@
         ]
         return jnp.concatenate(parts)
 
-    w_grad, o_got[2:] = tie(w_grad, o_got[2:])
     w_got = [shift(w_part(t).astype(bf16), -t) for t in range(1, n_sq)]
+    normed_grad = [dot_nt(low_m, qkv_w) for low_m in qkv_low.reshape(n_dp, -1, pack)]
+    normed_grad, o_got[1:] = tie(normed_grad, o_got[1:])
     o_got = o_parts[0].astype(f32) + sum(v.astype(f32) for v in o_got)
     o_share = lax.ppermute(
         o_got.astype(bf16), ("dp", "sq", "cl"), [(b, a) for a, b in head_pairs()]
     )
-    normed_grad = [dot_nt(low_m, qkv_w) for low_m in qkv_low.reshape(n_dp, -1, pack)]
     normed_first = fold_first(dp_fold(normed_grad).reshape(1, 2, n_cl, rows // 2, width))
     normed_grad = fold_last(normed_first).reshape(rows, width)
-    normed_grad, w_got, gu_share, down_share = tie(normed_grad, w_got, gu_share, down_share)
-    w_got = w_part(0) + sum(v.astype(f32) for v in w_got)
+    normed_grad, w_got[:1], gu_share, down_share = tie(
+        normed_grad, w_got[:1], gu_share, down_share
+    )
     attn_gain_grad = jnp.sum(normed_grad * inputs * first_scale, axis=0)
     input_grad = middle_grad + norm_back(inputs, first_scale, attn_gain, normed_grad)
     input_grad = from_sequence(input_grad.astype(bf16).reshape(nl, bl, width))
 
+    gain_grads = jnp.concatenate([attn_gain_grad, ffn_gain_grad, q_gain_grad, k_gain_grad])
+    router_grad = jnp.transpose(router_grad.reshape(experts, n_all, shard), (1, 0, 2))
+    small_grad = jnp.concatenate(
+        [router_grad.reshape(n_all, n_router), gain_grads.reshape(n_all, -1)], axis=-1
+    )
+    small_grad = jnp.pad(small_grad, ((0, 0), (0, -n_small % 128))).reshape(n_all, -1, 128)
+    small_grad = every_scatter(small_grad).reshape(-1)
+    w_got, small_grad = tie(w_got, small_grad)
+    w_got = w_part(0) + sum(v.astype(f32) for v in w_got)
     w_got, o_share = tie(w_got, o_share)
     o_share = o_share.astype(f32)
     w_grad = w_got.astype(bf16).reshape(n_dp, pack, n_cl, shard)
@@ -591,13 +601,6 @@
     k_share = kv_share[..., :HD].reshape(shard, -1)
     v_share = kv_share[..., HD:].reshape(shard, -1)
 
-    gain_grads = jnp.concatenate([attn_gain_grad, ffn_gain_grad, q_gain_grad, k_gain_grad])
-    router_grad = jnp.transpose(router_grad.reshape(experts, n_all, shard), (1, 0, 2))
-    small_grad = jnp.concatenate(
-        [router_grad.reshape(n_all, n_router), gain_grads.reshape(n_all, -1)], axis=-1
-    )
-    small_grad = jnp.pad(small_grad, ((0, 0), (0, -n_small % 128))).reshape(n_all, -1, 128)
-    small_grad = every_scatter(small_grad).reshape(-1)
     router_share = small_grad[:n_router].reshape(experts, shard).T
     gains_share = small_grad[n_router:n_small]
     return (

time: 799 us -> 790 us (0.989)
  waiting for transfers between devices: 334 us -> 318 us
    ppermute x18, waiting for transfers between devices: 122 us -> 83.7 us  [shift(): return lax.ppermute(v, 'sq', [(i, (i + by) % n) for i in range(n)])]
    all_to_all x1, waiting for transfers between devices: 10.7 us -> 36.1 us  [every_scatter(): lax.all_to_all(v, ('dp', 'sq', 'cl'), split_axis=0, concat_axis=0, tiled=...]
    unnamed x295 -> x293, local copies, waits for them, and re-layouts: 35.4 us -> 37.6 us
  transfers between devices with their start and end apart: 95 -> 95, of which waited for: 51 -> 49; matrix products, arithmetic and copies ran while one was open for 29% -> 30% of each run, Pallas kernels for 2% -> 2%
where the time goes in v5:
time: 790 us; the launch traced here: 780 us
  waiting for transfers between devices  318 us (40%)
  matrix products  128 us (16%)
  starting transfers between devices  127 us (16%)
  other arithmetic  95.7 us (12%)
  local copies, waits for them, and re-layouts  91.4 us (12%)
  Pallas kernels  15.6 us (2%)
    ppermute x63, waiting for transfers between devices, flip(): return lax.ppermute(v, axis, [(i, i ^ bit) for i in range(n)])  189 us
    ppermute x18, waiting for transfers between devices, shift(): return lax.ppermute(v, 'sq', [(i, (i + by) % n) for i in range(n)])  83.7 us
    ppermute x63, starting transfers between devices, flip(): return lax.ppermute(v, axis, [(i, i ^ bit) for i in range(n)])  70.8 us
    dot_general x7, matrix products, dot_tn(): lax.dot_general(a, b, (((0,), (0,)), ((), ())), preferred_element_type=f32)  39.7 us
    unnamed x293, local copies, waits for them, and re-layouts  37.6 us
    all_to_all x1, waiting for transfers between devices, every_scatter(): lax.all_to_all(v, ('dp', 'sq', 'cl'), split_axis=0, concat_axis=0, tiled=...  36.1 us
    dot_general x8, matrix products, dot(): return jnp.dot(a, b, preferred_element_type=f32)  25.9 us
    dot_general x8, matrix products, dot_nt(): lax.dot_general(a, b, (((1,), (1,)), ((), ())), preferred_element_type=f32)  21.4 us
  transfers between devices with their start and end apart: 95, of which 49 were waited for; matrix products, arithmetic and copies ran while one was open for 30% of the time, Pallas kernels for 2%

profile of v5, /device:TPU:1, one launch (start us, length us, event | category | flops | bytes accessed | tf_op | source)
XLA Modules:
  0.0 779.7 jit_solution(10937174634861652563)
XLA Ops:
  27.8 6.0 all-to-all-start.1
  35.4 7.7 collective-permute-done
  88.7 7.2 collective-permute-done.10
  116.7 10.9 %fusion.176 = (f32[4,1024]{1,0:T(4,128)S(1)}, f32[4,1024,1024]{1,2,0:T(8,128)}) fusion(pred[1024,1024]{0,1:T(8,128)(4,1)} %compare_and_fusion, bf16[1024,128,1]{0,1,2:T(8,128)(2,1)S(1)} %copy-done.55, bf16[1024,4,128]{0,2,1:T(8,128)(2,1)} %fusion.52), kind=kOutput, calls=%fused_computation.437 | convolution fusion | flops 1090520064 | bytes 19152896 | tf_op jit(solution)/shard_map/sub | solution.py:412
  132.8 7.1 fusion.58
  139.9 7.6 collective-permute-done.20
  148.6 12.5 %collective-permute-done.21 = bf16[128,2048]{1,0:T(8,128)(2,1)S(1)} collective-permute-done((bf16[128,2048]{1,0:T(8,128)(2,1)S(1)}, bf16[128,2048]{1,0:T(8,128)(2,1)S(1)}, u32[]{:S(2)}, u32[]{:S(2)}) %collective-permute-start.21) | collective-permute-done | bytes 524320 | tf_op jit(solution)/shard_map/ppermute | solution.py:86
  181.1 9.0 %collective-permute-done.23 = bf16[1,2,64,2048]{3,2,1,0:T(8,128)(2,1)S(1)} collective-permute-done((bf16[1,2,64,2048]{3,2,1,0:T(8,128)(2,1)S(1)}, bf16[1,2,64,2048]{3,2,1,0:T(8,128)(2,1)S(1)}, u32[]{:S(2)}, u32[]{:S(2)}) %collective-permute-start.23) | collective-permute-done | bytes 524320 | tf_op jit(solution)/shard_map/ppermute | solution.py:73
  209.1 10.3 %collective-permute-done.28.refs_9_ = bf16[64,4224]{1,0:T(8,128)(2,1)S(1)} collective-permute-done((bf16[64,4224]{1,0:T(8,128)(2,1)S(1)}, bf16[64,4224]{1,0:T(8,128)(2,1)S(1)}, u32[]{:S(2)}, u32[]{:S(2)}) %collective-permute-start.28) | collective-permute-done | bytes 540704 | tf_op jit(solution)/shard_map/ppermute | solution.py:73
  221.3 10.1 %collective-permute-done.29.refs_10_ = bf16[64,4224]{1,0:T(8,128)(2,1)S(1)} collective-permute-done((bf16[64,4224]{1,0:T(8,128)(2,1)S(1)}, bf16[64,4224]{1,0:T(8,128)(2,1)S(1)}, u32[]{:S(2)}, u32[]{:S(2)}) %collective-permute-start.29) | collective-permute-done | bytes 540704 | tf_op jit(solution)/shard_map/ppermute | solution.py:73
  231.4 11.6 %collective-permute-done.30.refs_11_ = bf16[64,4224]{1,0:T(8,128)(2,1)S(1)} collective-permute-done((bf16[64,4224]{1,0:T(8,128)(2,1)S(1)}, bf16[64,4224]{1,0:T(8,128)(2,1)S(1)}, u32[]{:S(2)}, u32[]{:S(2)}) %collective-permute-start.30) | collective-permute-done | bytes 540704 | tf_op jit(solution)/shard_map/ppermute | solution.py:73
  248.0 9.6 %collective-permute-done.34.refs_1_ = bf16[64,4224]{1,0:T(8,128)(2,1)} collective-permute-done((bf16[64,4224]{1,0:T(8,128)(2,1)S(1)}, bf16[64,4224]{1,0:T(8,128)(2,1)}, u32[]{:S(2)}, u32[]{:S(2)}) %collective-permute-start.34) | collective-permute-done | bytes 540704 | tf_op jit(solution)/shard_map/ppermute | solution.py:73
  258.5 12.0 %collective-permute-done.40 = bf16[128,4224]{1,0:T(8,128)(2,1)} collective-permute-done((bf16[128,4224]{1,0:T(8,128)(2,1)S(1)}, bf16[128,4224]{1,0:T(8,128)(2,1)}, u32[]{:S(2)}, u32[]{:S(2)}) %collective-permute-start.40) | collective-permute-done | bytes 1081376 | tf_op jit(solution)/shard_map/ppermute | solution.py:86
  284.8 8.3 %collective-permute-done.44.refs_13_ = bf16[64,4224]{1,0:T(8,128)(2,1)} collective-permute-done((bf16[64,4224]{1,0:T(8,128)(2,1)S(1)}, bf16[64,4224]{1,0:T(8,128)(2,1)}, u32[]{:S(2)}, u32[]{:S(2)}) %collective-permute-start.44) | collective-permute-done | bytes 540704 | tf_op jit(solution)/shard_map/ppermute | solution.py:73
  307.5 8.7 %collective-permute-done.43.refs_11_ = bf16[64,4224]{1,0:T(8,128)(2,1)S(1)} collective-permute-done((bf16[64,4224]{1,0:T(8,128)(2,1)}, bf16[64,4224]{1,0:T(8,128)(2,1)S(1)}, u32[]{:S(2)}, u32[]{:S(2)}) %collective-permute-start.43) | collective-permute-done | bytes 540704 | tf_op jit(solution)/shard_map/ppermute | solution.py:73
  319.9 7.8 pull.2
  328.8 7.3 fusion.179
  365.5 7.8 pull.3
  390.4 15.6 %collective-permute-done.54 = bf16[2,2,64,4224]{3,2,0,1:T(8,128)(2,1)} collective-permute-done((bf16[2,2,64,4224]{3,2,0,1:T(8,128)(2,1)}, bf16[2,2,64,4224]{3,2,0,1:T(8,128)(2,1)}, u32[]{:S(2)}, u32[]{:S(2)}) %collective-permute-start.54) | collective-permute-done | bytes 2162720 | tf_op jit(solution)/shard_map/ppermute | solution.py:73
  425.1 8.0 %collective-permute-done.56 = bf16[2,64,4224]{2,1,0:T(8,128)(2,1)S(1)} collective-permute-done((bf16[2,64,4224]{2,1,0:T(8,128)(2,1)S(1)}, bf16[2,64,4224]{2,1,0:T(8,128)(2,1)S(1)}, u32[]{:S(2)}, u32[]{:S(2)}) %collective-permute-start.56) | collective-permute-done | bytes 1081376 | tf_op jit(solution)/shard_map/ppermute | solution.py:73
  450.2 11.2 %fusion.24 = bf16[1024,1536]{1,0:T(8,128)(2,1)} fusion(bf16[640,1024]{1,0:T(8,128)(2,1)S(1)} %copy-done.48, bf16[640,1024]{1,0:T(8,128)(2,1)S(1)} %copy-done.46, bf16[640,1536]{1,0:T(8,128)(2,1)S(1)} %copy-done.44, bf16[640,768]{1,0:T(8,128)(2,1)S(1)} %copy-done.122, bf16[640,768]{1,0:T(8,128)(2,1)S(1)} %copy-done.120), kind=kOutput, calls=%fused_computation.67 | convolution fusion | flops 4043571200 | bytes 9699328 | tf_op jit(solution)/shard_map/dot_general | solution.py:64
  461.4 11.3 %fusion.20 = f32[1024,1536]{1,0:T(8,128)} fusion(bf16[640,1024]{1,0:T(8,128)(2,1)S(1)} %copy-done.47, bf16[640,1024]{1,0:T(8,128)(2,1)S(1)} %copy-done.45, bf16[640,1536]{1,0:T(8,128)(2,1)S(1)} %copy-done.44, bf16[640,768]{1,0:T(8,128)(2,1)S(1)} %copy-done.122, bf16[640,768]{1,0:T(8,128)(2,1)S(1)} %copy-done.120), kind=kOutput, calls=%fused_computation.63 | convolution fusion | flops 4043571200 | bytes 12845056 | tf_op jit(solution)/shard_map/dot_general | solution.py:64
  473.0 15.3 %collective-permute-done.58 = bf16[2,2,64,4224]{3,2,0,1:T(8,128)(2,1)S(1)} collective-permute-done((bf16[2,2,64,4224]{3,2,0,1:T(8,128)(2,1)S(1)}, bf16[2,2,64,4224]{3,2,0,1:T(8,128)(2,1)S(1)}, u32[]{:S(2)}, u32[]{:S(2)}) %collective-permute-start.58) | collective-permute-done | bytes 2162720 | tf_op jit(solution)/shard_map/ppermute | solution.py:73
  491.6 19.1 %collective-permute-done.60 = bf16[2,64,4224]{2,1,0:T(8,128)(2,1)S(1)} collective-permute-done((bf16[2,64,4224]{2,1,0:T(8,128)(2,1)S(1)}, bf16[2,64,4224]{2,1,0:T(8,128)(2,1)S(1)}, u32[]{:S(2)}, u32[]{:S(2)}) %collective-permute-start.60) | collective-permute-done | bytes 1081376 | tf_op jit(solution)/shard_map/ppermute | solution.py:73
  511.8 18.4 %collective-permute-done.64 = bf16[128,4224]{1,0:T(8,128)(2,1)S(1)} collective-permute-done((bf16[128,4224]{1,0:T(8,128)(2,1)S(1)}, bf16[128,4224]{1,0:T(8,128)(2,1)S(1)}, u32[]{:S(2)}, u32[]{:S(2)}) %collective-permute-start.64) | collective-permute-done | bytes 1081376 | tf_op jit(solution)/shard_map/ppermute | solution.py:86
  549.7 11.1 %collective-permute-start.71 = (bf16[1,512,2048]{2,1,0:T(8,128)(2,1)}, bf16[1,512,2048]{2,1,0:T(8,128)(2,1)}, u32[]{:S(2)}, u32[]{:S(2)}) collective-permute-start(bf16[1,512,2048]{2,1,0:T(8,128)(2,1)} %bitcast.89), channel_id=1, source_target_pairs={{0,16},{16,0},{1,17},{17,1},{2,18},{18,2},{3,19},{19,3},{4,20},{20... | collective-permute-start | bytes 6291464 | tf_op jit(solution)/shard_map/ppermute | solution.py:73
  589.5 7.1 fusion.1
  599.9 8.0 %fusion.3 = bf16[4,1024,1024]{1,2,0:T(8,128)(2,1)S(1)} fusion(f32[1024,1024,4]{1,0,2:T(8,128)} %get-tuple-element.313, f32[4,1024]{1,0:T(4,128)S(1)} %get-tuple-element.312, f32[4,1024,1024]{1,2,0:T(8,128)S(1)} %bitcast.437, f32[4,1024]{1,0:T(4,128)S(1)} %copy-done.99), kind=kLoop, calls=%fused_computation.5 | loop fusion | flops 16777216 | bytes 41975808 | tf_op jit(solution)/shard_map/convert_element_type | solution.py:534
  615.5 6.1 fusion.6
  648.7 12.7 %collective-permute-done.76 = bf16[128,2048]{1,0:T(8,128)(2,1)S(1)} collective-permute-done((bf16[128,2048]{1,0:T(8,128)(2,1)}, bf16[128,2048]{1,0:T(8,128)(2,1)S(1)}, u32[]{:S(2)}, u32[]{:S(2)}) %collective-permute-start.76) | collective-permute-done | bytes 524320 | tf_op jit(solution)/shard_map/ppermute | solution.py:86
  700.1 7.9 %collective-permute-start.90 = (bf16[128,2048]{1,0:T(8,128)(2,1)}, bf16[128,2048]{1,0:T(8,128)(2,1)}, u32[]{:S(2)}, u32[]{:S(2)}) collective-permute-start(bf16[128,2048]{1,0:T(8,128)(2,1)} %fusion.90), channel_id=1, source_target_pairs={{0,0},{4,1},{8,2},{12,3},{20,4},{24,5},{28,6},{16,7},{9,8},{13,9},... | collective-permute-start | bytes 1572872 | tf_op jit(solution)/shard_map/ppermute | solution.py:572
  722.7 36.1 %all-to-all-done.2 = f32[32,10,128]{2,1,0:T(8,128)S(1)} async-done(((f32[32,10,128]{2,1,0:T(8,128)}), f32[32,10,128]{2,1,0:T(8,128)S(1)}, u32[]{:S(2)}, u32[]{:S(2)}) %all-to-all-start.2) | async-done | bytes 163872 | tf_op jit(solution)/shard_map/all_to_all | solution.py:104
  (711 shorter events, 426.8 us)
Async XLA Ops:
  16.1 66.0 %collective-permute-start.11 = (bf16[1,1024,1536]{2,1,0:T(8,128)(2,1)}, bf16[1,1024,1536]{2,1,0:T(8,128)(2,1)}, u32[]{:S(2)}, u32[]{:S(2)}) collective-permute-start(bf16[1,1024,1536]{2,1,0:T(8,128)(2,1)} %param.23), channel_id=1, source_target_pairs={{0,16},{16,0},{1,17},{17,1},{2,18},{18,2},{3,19},{19,3},{4,20},{20... | collective-permute-start | bytes 9437192 | tf_op jit(solution)/shard_map/ppermute | solution.py:73
  16.2 31.6 %collective-permute-start.12 = (bf16[1,768,1024]{2,1,0:T(8,128)(2,1)}, bf16[1,768,1024]{2,1,0:T(8,128)(2,1)}, u32[]{:S(2)}, u32[]{:S(2)}) collective-permute-start(bf16[1,768,1024]{2,1,0:T(8,128)(2,1)} %param.24), channel_id=1, source_target_pairs={{0,16},{16,0},{1,17},{17,1},{2,18},{18,2},{3,19},{19,3},{4,20},{20... | collective-permute-start | bytes 4718600 | tf_op jit(solution)/shard_map/ppermute | solution.py:73
  27.8 31.9 %all-to-all-start.1 = ((bf16[32,10,128]{2,1,0:T(8,128)(2,1)}), bf16[32,10,128]{2,1,0:T(8,128)(2,1)S(1)}, u32[]{:S(2)}, u32[]{:S(2)}) async-start(bf16[32,10,128]{2,1,0:T(8,128)(2,1)} %broadcast_in_dim.202), calls=%async_computation.1 | async-start | bytes 262144 | tf_op jit(solution)/shard_map/all_to_all | solution.py:100
  71.9 24.0 %collective-permute-start.15 = (bf16[1,512,2048]{2,1,0:T(8,128)(2,1)S(1)}, bf16[1,512,2048]{2,1,0:T(8,128)(2,1)S(1)}, u32[]{:S(2)}, u32[]{:S(2)}) collective-permute-start(bf16[1,512,2048]{2,1,0:T(8,128)(2,1)S(1)} %bitcast.430), channel_id=1, source_target_pairs={{0,16},{16,0},{1,17},{17,1},{2,18},{18,2},{3,19},{19,3},{4,20},{20... | collective-permute-start | bytes 6291464 | tf_op jit(solution)/shard_map/ppermute | solution.py:73
  77.6 38.6 %collective-permute-start.17 = (bf16[128,2048]{1,0:T(8,128)(2,1)}, bf16[128,2048]{1,0:T(8,128)(2,1)}, u32[]{:S(2)}, u32[]{:S(2)}) collective-permute-start(bf16[128,2048]{1,0:T(8,128)(2,1)} %param.20), channel_id=1, source_target_pairs={{0,0},{1,4},{2,8},{3,12},{4,20},{5,24},{6,28},{7,16},{8,9},{9,13},... | collective-permute-start | bytes 1572872 | tf_op jit(solution)/shard_map/ppermute | solution.py:368
  203.3 28.1 %collective-permute-start.27 = (bf16[128,4224]{1,0:T(8,128)(2,1)S(1)}, bf16[128,4224]{1,0:T(8,128)(2,1)S(1)}, u32[]{:S(2)}, u32[]{:S(2)}) collective-permute-start(bf16[128,4224]{1,0:T(8,128)(2,1)S(1)} %pad_maximum_fusion.15), channel_id=1, source_target_pairs={{0,4},{4,8},{8,12},{12,0},{1,5},{5,9},{9,13},{13,1},{2,6},{6,10},{... | collective-permute-start | bytes 3244040 | tf_op jit(solution)/shard_map/ppermute | solution.py:86
  244.7 25.9 %collective-permute-start.40 = (bf16[128,4224]{1,0:T(8,128)(2,1)S(1)}, bf16[128,4224]{1,0:T(8,128)(2,1)}, u32[]{:S(2)}, u32[]{:S(2)}) collective-permute-start(bf16[128,4224]{1,0:T(8,128)(2,1)S(1)} %collective-permute-done.27), channel_id=1, source_target_pairs={{0,4},{4,8},{8,12},{12,0},{1,5},{5,9},{9,13},{13,1},{2,6},{6,10},{... | collective-permute-start | bytes 3244040 | tf_op jit(solution)/shard_map/ppermute | solution.py:86
  246.2 25.9 %collective-permute-start.35 = (bf16[64,4224]{1,0:T(8,128)(2,1)S(1)}, bf16[64,4224]{1,0:T(8,128)(2,1)S(1)}, u32[]{:S(2)}, u32[]{:S(2)}) collective-permute-start(bf16[64,4224]{1,0:T(8,128)(2,1)S(1)} %get-tuple-element.260.refs_0_), channel_id=1, source_target_pairs={{0,2},{1,3},{2,0},{3,1},{4,6},{5,7},{6,4},{7,5},{8,10},{9,11},{10,... | collective-permute-start | bytes 1622024 | tf_op jit(solution)/shard_map/ppermute | solution.py:73
  247.3 25.9 %collective-permute-start.37 = (bf16[64,4224]{1,0:T(8,128)(2,1)S(1)}, bf16[64,4224]{1,0:T(8,128)(2,1)S(1)}, u32[]{:S(2)}, u32[]{:S(2)}) collective-permute-start(bf16[64,4224]{1,0:T(8,128)(2,1)S(1)} %get-tuple-element.259.refs_4_), channel_id=1, source_target_pairs={{0,2},{1,3},{2,0},{3,1},{4,6},{5,7},{6,4},{7,5},{8,10},{9,11},{10,... | collective-permute-start | bytes 1622024 | tf_op jit(solution)/shard_map/ppermute | solution.py:73
  247.6 27.3 %collective-permute-start.38 = (bf16[64,4224]{1,0:T(8,128)(2,1)S(1)}, bf16[64,4224]{1,0:T(8,128)(2,1)}, u32[]{:S(2)}, u32[]{:S(2)}) collective-permute-start(bf16[64,4224]{1,0:T(8,128)(2,1)S(1)} %get-tuple-element.259.refs_4_), channel_id=1, source_target_pairs={{0,1},{1,0},{2,3},{3,2},{4,5},{5,4},{6,7},{7,6},{8,9},{9,8},{10,11... | collective-permute-start | bytes 1622024 | tf_op jit(solution)/shard_map/ppermute | solution.py:73
  270.6 25.4 %collective-permute-start.47 = (bf16[128,4224]{1,0:T(8,128)(2,1)}, bf16[128,4224]{1,0:T(8,128)(2,1)}, u32[]{:S(2)}, u32[]{:S(2)}) collective-permute-start(bf16[128,4224]{1,0:T(8,128)(2,1)} %collective-permute-done.40), channel_id=1, source_target_pairs={{0,4},{4,8},{8,12},{12,0},{1,5},{5,9},{9,13},{13,1},{2,6},{6,10},{... | collective-permute-start | bytes 3244040 | tf_op jit(solution)/shard_map/ppermute | solution.py:86
  298.4 52.1 %collective-permute-start.48 = (bf16[64,4224]{1,0:T(8,128)(2,1)S(1)}, bf16[64,4224]{1,0:T(8,128)(2,1)S(1)}, u32[]{:S(2)}, u32[]{:S(2)}) collective-permute-start(bf16[64,4224]{1,0:T(8,128)(2,1)S(1)} %get-tuple-element.256.refs_0_), channel_id=1, source_target_pairs={{0,1},{1,0},{2,3},{3,2},{4,5},{5,4},{6,7},{7,6},{8,9},{9,8},{10,11... | collective-permute-start | bytes 1622024 | tf_op jit(solution)/shard_map/ppermute | solution.py:73
  304.6 58.9 %collective-permute-start.49 = (bf16[64,4224]{1,0:T(8,128)(2,1)S(1)}, bf16[64,4224]{1,0:T(8,128)(2,1)S(1)}, u32[]{:S(2)}, u32[]{:S(2)}) collective-permute-start(bf16[64,4224]{1,0:T(8,128)(2,1)S(1)} %get-tuple-element.256.refs_0_), channel_id=1, source_target_pairs={{0,2},{1,3},{2,0},{3,1},{4,6},{5,7},{6,4},{7,5},{8,10},{9,11},{10,... | collective-permute-start | bytes 1622024 | tf_op jit(solution)/shard_map/ppermute | solution.py:73
  306.9 44.3 %collective-permute-start.51 = (bf16[64,4224]{1,0:T(8,128)(2,1)S(1)}, bf16[64,4224]{1,0:T(8,128)(2,1)}, u32[]{:S(2)}, u32[]{:S(2)}) collective-permute-start(bf16[64,4224]{1,0:T(8,128)(2,1)S(1)} %get-tuple-element.255.refs_4_), channel_id=1, source_target_pairs={{0,2},{1,3},{2,0},{3,1},{4,6},{5,7},{6,4},{7,5},{8,10},{9,11},{10,... | collective-permute-start | bytes 1622024 | tf_op jit(solution)/shard_map/ppermute | solution.py:73
  316.2 47.7 %collective-permute-start.52 = (bf16[64,4224]{1,0:T(8,128)(2,1)S(1)}, bf16[64,4224]{1,0:T(8,128)(2,1)}, u32[]{:S(2)}, u32[]{:S(2)}) collective-permute-start(bf16[64,4224]{1,0:T(8,128)(2,1)S(1)} %get-tuple-element.255.refs_4_), channel_id=1, source_target_pairs={{0,1},{1,0},{2,3},{3,2},{4,5},{5,4},{6,7},{7,6},{8,9},{9,8},{10,11... | collective-permute-start | bytes 1622024 | tf_op jit(solution)/shard_map/ppermute | solution.py:73
  356.7 49.4 %collective-permute-start.54 = (bf16[2,2,64,4224]{3,2,0,1:T(8,128)(2,1)}, bf16[2,2,64,4224]{3,2,0,1:T(8,128)(2,1)}, u32[]{:S(2)}, u32[]{:S(2)}) collective-permute-start(bf16[2,2,64,4224]{3,2,0,1:T(8,128)(2,1)} %bitcast.412), channel_id=1, source_target_pairs={{0,2},{1,3},{2,0},{3,1},{4,6},{5,7},{6,4},{7,5},{8,10},{9,11},{10,... | collective-permute-start | bytes 6488072 | tf_op jit(solution)/shard_map/ppermute | solution.py:73
  363.5 43.5 %collective-permute-start.55 = (bf16[2,2,64,4224]{3,2,0,1:T(8,128)(2,1)}, bf16[2,2,64,4224]{3,2,0,1:T(8,128)(2,1)}, u32[]{:S(2)}, u32[]{:S(2)}) collective-permute-start(bf16[2,2,64,4224]{3,2,0,1:T(8,128)(2,1)} %bitcast.411), channel_id=1, source_target_pairs={{0,1},{1,0},{2,3},{3,2},{4,5},{5,4},{6,7},{7,6},{8,9},{9,8},{10,11... | collective-permute-start | bytes 6488072 | tf_op jit(solution)/shard_map/ppermute | solution.py:73
  447.1 41.2 %collective-permute-start.58 = (bf16[2,2,64,4224]{3,2,0,1:T(8,128)(2,1)S(1)}, bf16[2,2,64,4224]{3,2,0,1:T(8,128)(2,1)S(1)}, u32[]{:S(2)}, u32[]{:S(2)}) collective-permute-start(bf16[2,2,64,4224]{3,2,0,1:T(8,128)(2,1)S(1)} %bitcast.482), channel_id=1, source_target_pairs={{0,2},{1,3},{2,0},{3,1},{4,6},{5,7},{6,4},{7,5},{8,10},{9,11},{10,... | collective-permute-start | bytes 6488072 | tf_op jit(solution)/shard_map/ppermute | solution.py:73
  447.4 41.0 %collective-permute-start.59 = (bf16[2,2,64,4224]{3,2,0,1:T(8,128)(2,1)S(1)}, bf16[2,2,64,4224]{3,2,0,1:T(8,128)(2,1)S(1)}, u32[]{:S(2)}, u32[]{:S(2)}) collective-permute-start(bf16[2,2,64,4224]{3,2,0,1:T(8,128)(2,1)S(1)} %bitcast.483), channel_id=1, source_target_pairs={{0,1},{1,0},{2,3},{3,2},{4,5},{5,4},{6,7},{7,6},{8,9},{9,8},{10,11... | collective-permute-start | bytes 6488072 | tf_op jit(solution)/shard_map/ppermute | solution.py:73
  448.1 24.5 %collective-permute-start.62 = (bf16[128,4224]{1,0:T(8,128)(2,1)S(1)}, bf16[128,4224]{1,0:T(8,128)(2,1)S(1)}, u32[]{:S(2)}, u32[]{:S(2)}) collective-permute-start(bf16[128,4224]{1,0:T(8,128)(2,1)S(1)} %bitcast.488), channel_id=1, source_target_pairs={{0,4},{4,8},{8,12},{12,0},{1,5},{5,9},{9,13},{13,1},{2,6},{6,10},{... | collective-permute-start | bytes 3244040 | tf_op jit(solution)/shard_map/ppermute | solution.py:86
  472.8 38.7 %collective-permute-start.63 = (bf16[128,4224]{1,0:T(8,128)(2,1)S(1)}, bf16[128,4224]{1,0:T(8,128)(2,1)S(1)}, u32[]{:S(2)}, u32[]{:S(2)}) collective-permute-start(bf16[128,4224]{1,0:T(8,128)(2,1)S(1)} %fusion.48), channel_id=1, source_target_pairs={{0,4},{4,8},{8,12},{12,0},{1,5},{5,9},{9,13},{13,1},{2,6},{6,10},{... | collective-permute-start | bytes 3244040 | tf_op jit(solution)/shard_map/ppermute | solution.py:86
  549.7 26.8 %collective-permute-start.71 = (bf16[1,512,2048]{2,1,0:T(8,128)(2,1)}, bf16[1,512,2048]{2,1,0:T(8,128)(2,1)}, u32[]{:S(2)}, u32[]{:S(2)}) collective-permute-start(bf16[1,512,2048]{2,1,0:T(8,128)(2,1)} %bitcast.89), channel_id=1, source_target_pairs={{0,16},{16,0},{1,17},{17,1},{2,18},{18,2},{3,19},{19,3},{4,20},{20... | collective-permute-start | bytes 6291464 | tf_op jit(solution)/shard_map/ppermute | solution.py:73
  624.3 37.1 %collective-permute-start.76 = (bf16[128,2048]{1,0:T(8,128)(2,1)}, bf16[128,2048]{1,0:T(8,128)(2,1)S(1)}, u32[]{:S(2)}, u32[]{:S(2)}) collective-permute-start(bf16[128,2048]{1,0:T(8,128)(2,1)} %get-tuple-element.226), channel_id=1, source_target_pairs={{0,8},{4,12},{8,0},{12,4},{1,9},{5,13},{9,1},{13,5},{2,10},{6,14},... | collective-permute-start | bytes 1572872 | tf_op jit(solution)/shard_map/ppermute | solution.py:86
  626.5 34.9 %collective-permute-start.77 = (bf16[128,2048]{1,0:T(8,128)(2,1)}, bf16[128,2048]{1,0:T(8,128)(2,1)S(1)}, u32[]{:S(2)}, u32[]{:S(2)}) collective-permute-start(bf16[128,2048]{1,0:T(8,128)(2,1)} %get-tuple-element.225), channel_id=1, source_target_pairs={{0,4},{4,8},{8,12},{12,0},{1,5},{5,9},{9,13},{13,1},{2,6},{6,10},{... | collective-permute-start | bytes 1572872 | tf_op jit(solution)/shard_map/ppermute | solution.py:86
  665.5 46.3 %collective-permute-start.83 = (bf16[1280,256]{1,0:T(8,128)(2,1)S(1)}, bf16[1280,256]{1,0:T(8,128)(2,1)S(1)}, u32[]{:S(2)}, u32[]{:S(2)}) collective-permute-start(bf16[1280,256]{1,0:T(8,128)(2,1)S(1)} %pad_maximum_fusion.19), channel_id=1, source_target_pairs={{0,12},{4,0},{8,4},{12,8},{1,13},{5,1},{9,5},{13,9},{2,14},{6,2},{... | collective-permute-start | bytes 1966088 | tf_op jit(solution)/shard_map/ppermute | solution.py:86
  667.1 41.1 %collective-permute-start.84 = (bf16[1024,1536]{1,0:T(8,128)(2,1)S(1)}, bf16[1024,1536]{1,0:T(8,128)(2,1)S(1)}, u32[]{:S(2)}, u32[]{:S(2)}) collective-permute-start(bf16[1024,1536]{1,0:T(8,128)(2,1)S(1)} %copy-done.113), channel_id=1, source_target_pairs={{0,16},{16,0},{1,17},{17,1},{2,18},{18,2},{3,19},{19,3},{4,20},{20... | collective-permute-start | bytes 9437192 | tf_op jit(solution)/shard_map/ppermute | solution.py:73
  676.6 82.3 %collective-permute-start.88 = (bf16[1280,256]{1,0:T(8,128)(2,1)}, bf16[1280,256]{1,0:T(8,128)(2,1)}, u32[]{:S(2)}, u32[]{:S(2)}) collective-permute-start(bf16[1280,256]{1,0:T(8,128)(2,1)} %pad_maximum_fusion.20), channel_id=1, source_target_pairs={{0,8},{4,12},{8,0},{12,4},{1,9},{5,13},{9,1},{13,5},{2,10},{6,14},... | collective-permute-start | bytes 1966088 | tf_op jit(solution)/shard_map/ppermute | solution.py:86
  686.3 72.6 %collective-permute-start.89 = (bf16[1280,256]{1,0:T(8,128)(2,1)}, bf16[1280,256]{1,0:T(8,128)(2,1)}, u32[]{:S(2)}, u32[]{:S(2)}) collective-permute-start(bf16[1280,256]{1,0:T(8,128)(2,1)} %pad_maximum_fusion.21), channel_id=1, source_target_pairs={{0,4},{4,8},{8,12},{12,0},{1,5},{5,9},{9,13},{13,1},{2,6},{6,10},{... | collective-permute-start | bytes 1966088 | tf_op jit(solution)/shard_map/ppermute | solution.py:86
  700.1 61.0 %collective-permute-start.90 = (bf16[128,2048]{1,0:T(8,128)(2,1)}, bf16[128,2048]{1,0:T(8,128)(2,1)}, u32[]{:S(2)}, u32[]{:S(2)}) collective-permute-start(bf16[128,2048]{1,0:T(8,128)(2,1)} %fusion.90), channel_id=1, source_target_pairs={{0,0},{4,1},{8,2},{12,3},{20,4},{24,5},{28,6},{16,7},{9,8},{13,9},... | collective-permute-start | bytes 1572872 | tf_op jit(solution)/shard_map/ppermute | solution.py:572
  713.9 45.0 %all-to-all-start.2 = ((f32[32,10,128]{2,1,0:T(8,128)}), f32[32,10,128]{2,1,0:T(8,128)S(1)}, u32[]{:S(2)}, u32[]{:S(2)}) async-start(f32[32,10,128]{2,1,0:T(8,128)} %reshape.834), calls=%async_computation.2 | async-start | bytes 524288 | tf_op jit(solution)/shard_map/all_to_all | solution.py:104
  717.0 49.6 %collective-permute-start.86 = (bf16[64,2048]{1,0:T(8,128)(2,1)S(1)}, bf16[64,2048]{1,0:T(8,128)(2,1)S(1)}, u32[]{:S(2)}, u32[]{:S(2)}) collective-permute-start(bf16[64,2048]{1,0:T(8,128)(2,1)S(1)} %get-tuple-element.268), channel_id=1, source_target_pairs={{0,0},{4,4},{16,8},{20,12},{8,16},{12,20},{24,24},{28,28},{1,1},{5... | collective-permute-start | bytes 786440 | tf_op jit(solution)/shard_map/ppermute | solution.py:181
  721.5 45.0 %collective-permute-start.87 = (bf16[64,2048]{1,0:T(8,128)(2,1)S(1)}, bf16[64,2048]{1,0:T(8,128)(2,1)S(1)}, u32[]{:S(2)}, u32[]{:S(2)}) collective-permute-start(bf16[64,2048]{1,0:T(8,128)(2,1)S(1)} %get-tuple-element.267), channel_id=1, source_target_pairs={{4,0},{0,4},{20,8},{16,12},{12,16},{8,20},{28,24},{24,28},{5,1},{1... | collective-permute-start | bytes 786440 | tf_op jit(solution)/shard_map/ppermute | solution.py:181
  (199 other events, 2577.6 us)

commit v6 on v5

--- a/solution.py
+++ b/solution.py
@@ -389,6 +389,7 @@
 
     first_scale = rms_scale(inputs)
     normed_all = (inputs_all * rms_scale(inputs_all) * attn_gain).astype(bf16)
+    (normed_all,) = tie(normed_all)
     proj = dot(normed_all, qkv_w)
     q_proj = proj[:, :hw].reshape(length, heads, HD)
     kv_proj = dp_columns(proj[:, hw:].reshape(n_dp, -1, kvw)).reshape(n_dp, length, kvw)

time: 790 us -> 784 us (level)
  other arithmetic: 95.7 us -> 85 us
    unnamed x293 -> x291, local copies, waits for them, and re-layouts: 37.6 us -> 38.9 us
  transfers between devices with their start and end apart: 95 -> 95, of which waited for: 49 -> 49; matrix products, arithmetic and copies ran while one was open for 30% -> 28% of each run, Pallas kernels for 2% -> 2%
where the time goes in v6:
time: 784 us; the launch traced here: 774 us
  waiting for transfers between devices  324 us (41%)
  matrix products  126 us (16%)
  starting transfers between devices  124 us (16%)
  local copies, waits for them, and re-layouts  94.7 us (12%)
  other arithmetic  85 us (11%)
  Pallas kernels  15.6 us (2%)
    ppermute x63, waiting for transfers between devices, flip(): return lax.ppermute(v, axis, [(i, i ^ bit) for i in range(n)])  188 us
    ppermute x18, waiting for transfers between devices, shift(): return lax.ppermute(v, 'sq', [(i, (i + by) % n) for i in range(n)])  85.2 us
    ppermute x63, starting transfers between devices, flip(): return lax.ppermute(v, axis, [(i, i ^ bit) for i in range(n)])  67.8 us
    unnamed x291, local copies, waits for them, and re-layouts  38.9 us
    dot_general x7, matrix products, dot_tn(): lax.dot_general(a, b, (((0,), (0,)), ((), ())), preferred_element_type=f32)  38.6 us
    all_to_all x1, waiting for transfers between devices, every_scatter(): lax.all_to_all(v, ('dp', 'sq', 'cl'), split_axis=0, concat_axis=0, tiled=...  35.3 us
    dot_general x8, matrix products, dot(): return jnp.dot(a, b, preferred_element_type=f32)  24.2 us
    dot_general x8, matrix products, dot_nt(): lax.dot_general(a, b, (((1,), (1,)), ((), ())), preferred_element_type=f32)  21.4 us
  transfers between devices with their start and end apart: 95, of which 49 were waited for; matrix products, arithmetic and copies ran while one was open for 28% of the time, Pallas kernels for 2%

profile of v6, /device:TPU:1, one launch (start us, length us, event | category | flops | bytes accessed | tf_op | source)
XLA Modules:
  0.0 774.3 jit_solution(16718474024016875967)
XLA Ops:
  27.8 6.0 all-to-all-start.1
  35.4 7.8 %collective-permute-done = bf16[2,4,64,640]{3,2,0,1:T(8,128)(2,1)} collective-permute-done((bf16[2,4,64,640]{3,2,0,1:T(8,128)(2,1)}, bf16[2,4,64,640]{3,2,0,1:T(8,128)(2,1)}, u32[]{:S(2)}, u32[]{:S(2)}) %collective-permute-start) | collective-permute-done | bytes 655392 | tf_op jit(solution)/shard_map/ppermute | solution.py:86
  88.8 7.0 collective-permute-done.10
  114.7 10.9 %fusion.175 = (f32[4,1024]{1,0:T(4,128)S(1)}, f32[4,1024,1024]{1,2,0:T(8,128)}) fusion(pred[1024,1024]{0,1:T(8,128)(4,1)} %compare_and_fusion, bf16[1024,128,1]{0,1,2:T(8,128)(2,1)S(1)} %copy-done.54, bf16[1024,4,128]{0,2,1:T(8,128)(2,1)} %fusion.52), kind=kOutput, calls=%fused_computation.435 | convolution fusion | flops 1090520064 | bytes 19152896 | tf_op jit(solution)/shard_map/sub | solution.py:413
  131.3 7.1 fusion.58
  138.4 8.6 %collective-permute-done.20 = bf16[128,2048]{1,0:T(8,128)(2,1)S(1)} collective-permute-done((bf16[128,2048]{1,0:T(8,128)(2,1)}, bf16[128,2048]{1,0:T(8,128)(2,1)S(1)}, u32[]{:S(2)}, u32[]{:S(2)}) %collective-permute-start.20) | collective-permute-done | bytes 524320 | tf_op jit(solution)/shard_map/ppermute | solution.py:86
  148.1 13.7 %collective-permute-done.21 = bf16[128,2048]{1,0:T(8,128)(2,1)S(1)} collective-permute-done((bf16[128,2048]{1,0:T(8,128)(2,1)S(1)}, bf16[128,2048]{1,0:T(8,128)(2,1)S(1)}, u32[]{:S(2)}, u32[]{:S(2)}) %collective-permute-start.21) | collective-permute-done | bytes 524320 | tf_op jit(solution)/shard_map/ppermute | solution.py:86
  180.6 7.5 collective-permute-done.23
  207.1 10.3 %collective-permute-done.28.refs_9_ = bf16[64,4224]{1,0:T(8,128)(2,1)S(1)} collective-permute-done((bf16[64,4224]{1,0:T(8,128)(2,1)S(1)}, bf16[64,4224]{1,0:T(8,128)(2,1)S(1)}, u32[]{:S(2)}, u32[]{:S(2)}) %collective-permute-start.28) | collective-permute-done | bytes 540704 | tf_op jit(solution)/shard_map/ppermute | solution.py:73
  219.3 10.1 %collective-permute-done.29.refs_10_ = bf16[64,4224]{1,0:T(8,128)(2,1)S(1)} collective-permute-done((bf16[64,4224]{1,0:T(8,128)(2,1)S(1)}, bf16[64,4224]{1,0:T(8,128)(2,1)S(1)}, u32[]{:S(2)}, u32[]{:S(2)}) %collective-permute-start.29) | collective-permute-done | bytes 540704 | tf_op jit(solution)/shard_map/ppermute | solution.py:73
  229.4 11.6 %collective-permute-done.30.refs_11_ = bf16[64,4224]{1,0:T(8,128)(2,1)S(1)} collective-permute-done((bf16[64,4224]{1,0:T(8,128)(2,1)S(1)}, bf16[64,4224]{1,0:T(8,128)(2,1)S(1)}, u32[]{:S(2)}, u32[]{:S(2)}) %collective-permute-start.30) | collective-permute-done | bytes 540704 | tf_op jit(solution)/shard_map/ppermute | solution.py:73
  246.0 9.6 %collective-permute-done.34.refs_1_ = bf16[64,4224]{1,0:T(8,128)(2,1)} collective-permute-done((bf16[64,4224]{1,0:T(8,128)(2,1)S(1)}, bf16[64,4224]{1,0:T(8,128)(2,1)}, u32[]{:S(2)}, u32[]{:S(2)}) %collective-permute-start.34) | collective-permute-done | bytes 540704 | tf_op jit(solution)/shard_map/ppermute | solution.py:73
  256.5 12.0 %collective-permute-done.40 = bf16[128,4224]{1,0:T(8,128)(2,1)} collective-permute-done((bf16[128,4224]{1,0:T(8,128)(2,1)S(1)}, bf16[128,4224]{1,0:T(8,128)(2,1)}, u32[]{:S(2)}, u32[]{:S(2)}) %collective-permute-start.40) | collective-permute-done | bytes 1081376 | tf_op jit(solution)/shard_map/ppermute | solution.py:86
  282.9 8.3 %collective-permute-done.44.refs_13_ = bf16[64,4224]{1,0:T(8,128)(2,1)} collective-permute-done((bf16[64,4224]{1,0:T(8,128)(2,1)S(1)}, bf16[64,4224]{1,0:T(8,128)(2,1)}, u32[]{:S(2)}, u32[]{:S(2)}) %collective-permute-start.44) | collective-permute-done | bytes 540704 | tf_op jit(solution)/shard_map/ppermute | solution.py:73
  305.5 8.7 %collective-permute-done.43.refs_11_ = bf16[64,4224]{1,0:T(8,128)(2,1)S(1)} collective-permute-done((bf16[64,4224]{1,0:T(8,128)(2,1)}, bf16[64,4224]{1,0:T(8,128)(2,1)S(1)}, u32[]{:S(2)}, u32[]{:S(2)}) %collective-permute-start.43) | collective-permute-done | bytes 540704 | tf_op jit(solution)/shard_map/ppermute | solution.py:73
  317.9 7.8 %pull.2 = (bf16[640,2048]{1,0:T(8,128)(2,1)}, bf16[640,2048]{1,0:T(8,128)(2,1)}, bf16[640,128]{1,0:T(8,128)(2,1)}, bf16[4,160,256]{2,1,0:T(8,128)(2,1)}) custom-call(bf16[8,128]{1,0:T(8,128)(2,1)} %broadcast_in_dim.224.pick, bf16[64,4224]{1,0:T(8,128)(2,1)} %copy-done.37, bf16[64,4224]{1,0:T(8,128)(2,1)} %collective-permute-done.34.refs_1_, ...), custom_call_target="tpu_custom_call" | custom-call | tf_op jit(solution)/shard_map/pull/pallas_call | solution.py:268
  326.8 7.3 fusion.178
  363.6 7.8 %pull.3 = (bf16[640,2048]{1,0:T(8,128)(2,1)}, bf16[640,2048]{1,0:T(8,128)(2,1)}, bf16[640,128]{1,0:T(8,128)(2,1)}, bf16[4,160,256]{2,1,0:T(8,128)(2,1)}) custom-call(bf16[8,128]{1,0:T(8,128)(2,1)} %broadcast_in_dim.224.pick, bf16[64,4224]{1,0:T(8,128)(2,1)} %copy-done.39, bf16[64,4224]{1,0:T(8,128)(2,1)} %copy-done.67, bf16[64,4224]{1,0:T(8,128)(2,1)} %copy-done.68, ...), custom_call_target="tpu_custom_call" | custom-call | tf_op jit(solution)/shard_map/pull/pallas_call | solution.py:268
  388.5 15.6 %collective-permute-done.54 = bf16[2,2,64,4224]{3,2,0,1:T(8,128)(2,1)} collective-permute-done((bf16[2,2,64,4224]{3,2,0,1:T(8,128)(2,1)}, bf16[2,2,64,4224]{3,2,0,1:T(8,128)(2,1)}, u32[]{:S(2)}, u32[]{:S(2)}) %collective-permute-start.54) | collective-permute-done | bytes 2162720 | tf_op jit(solution)/shard_map/ppermute | solution.py:73
  423.2 8.0 %collective-permute-done.56 = bf16[2,64,4224]{2,1,0:T(8,128)(2,1)S(1)} collective-permute-done((bf16[2,64,4224]{2,1,0:T(8,128)(2,1)S(1)}, bf16[2,64,4224]{2,1,0:T(8,128)(2,1)S(1)}, u32[]{:S(2)}, u32[]{:S(2)}) %collective-permute-start.56) | collective-permute-done | bytes 1081376 | tf_op jit(solution)/shard_map/ppermute | solution.py:73
  448.2 11.0 %fusion.24 = bf16[1024,1536]{1,0:T(8,128)(2,1)} fusion(bf16[640,1024]{1,0:T(8,128)(2,1)S(1)} %copy-done.47, bf16[640,1024]{1,0:T(8,128)(2,1)S(1)} %copy-done.45, bf16[640,1536]{1,0:T(8,128)(2,1)S(1)} %copy-done.43, bf16[640,768]{1,0:T(8,128)(2,1)S(1)} %copy-done.121, bf16[640,768]{1,0:T(8,128)(2,1)S(1)} %copy-done.119), kind=kOutput, calls=%fused_computation.66 | convolution fusion | flops 4043571200 | bytes 9699328 | tf_op jit(solution)/shard_map/dot_general | solution.py:64
  459.2 11.3 %fusion.20 = f32[1024,1536]{1,0:T(8,128)} fusion(bf16[640,1024]{1,0:T(8,128)(2,1)S(1)} %copy-done.46, bf16[640,1024]{1,0:T(8,128)(2,1)S(1)} %copy-done.44, bf16[640,1536]{1,0:T(8,128)(2,1)S(1)} %copy-done.43, bf16[640,768]{1,0:T(8,128)(2,1)S(1)} %copy-done.121, bf16[640,768]{1,0:T(8,128)(2,1)S(1)} %copy-done.119), kind=kOutput, calls=%fused_computation.62 | convolution fusion | flops 4043571200 | bytes 12845056 | tf_op jit(solution)/shard_map/dot_general | solution.py:64
  471.1 15.2 %collective-permute-done.58 = bf16[2,2,64,4224]{3,2,0,1:T(8,128)(2,1)S(1)} collective-permute-done((bf16[2,2,64,4224]{3,2,0,1:T(8,128)(2,1)S(1)}, bf16[2,2,64,4224]{3,2,0,1:T(8,128)(2,1)S(1)}, u32[]{:S(2)}, u32[]{:S(2)}) %collective-permute-start.58) | collective-permute-done | bytes 2162720 | tf_op jit(solution)/shard_map/ppermute | solution.py:73
  489.6 19.1 %collective-permute-done.60 = bf16[2,64,4224]{2,1,0:T(8,128)(2,1)S(1)} collective-permute-done((bf16[2,64,4224]{2,1,0:T(8,128)(2,1)S(1)}, bf16[2,64,4224]{2,1,0:T(8,128)(2,1)S(1)}, u32[]{:S(2)}, u32[]{:S(2)}) %collective-permute-start.60) | collective-permute-done | bytes 1081376 | tf_op jit(solution)/shard_map/ppermute | solution.py:73
  509.8 18.3 %collective-permute-done.64 = bf16[128,4224]{1,0:T(8,128)(2,1)S(1)} collective-permute-done((bf16[128,4224]{1,0:T(8,128)(2,1)S(1)}, bf16[128,4224]{1,0:T(8,128)(2,1)S(1)}, u32[]{:S(2)}, u32[]{:S(2)}) %collective-permute-start.64) | collective-permute-done | bytes 1081376 | tf_op jit(solution)/shard_map/ppermute | solution.py:86
  547.7 11.1 %collective-permute-start.71 = (bf16[1,512,2048]{2,1,0:T(8,128)(2,1)}, bf16[1,512,2048]{2,1,0:T(8,128)(2,1)}, u32[]{:S(2)}, u32[]{:S(2)}) collective-permute-start(bf16[1,512,2048]{2,1,0:T(8,128)(2,1)} %bitcast.89), channel_id=1, source_target_pairs={{0,16},{16,0},{1,17},{17,1},{2,18},{18,2},{3,19},{19,3},{4,20},{20... | collective-permute-start | bytes 6291464 | tf_op jit(solution)/shard_map/ppermute | solution.py:73
  562.2 10.2 %collective-permute-done.72 = bf16[64,2048]{1,0:T(8,128)(2,1)S(1)} collective-permute-done((bf16[64,2048]{1,0:T(8,128)(2,1)S(1)}, bf16[64,2048]{1,0:T(8,128)(2,1)S(1)}, u32[]{:S(2)}, u32[]{:S(2)}) %collective-permute-start.72) | collective-permute-done | bytes 262176 | tf_op jit(solution)/shard_map/ppermute | solution.py:181
  587.4 8.3 %fusion.1 = (f32[4,1024]{1,0:T(4,128)S(1)}, f32[1024,1024,4]{1,0,2:T(8,128)}) fusion(f32[4,1024,1024]{1,2,0:T(8,128)S(1)} %bitcast.432, f32[4,1024]{1,0:T(4,128)S(1)} %copy-done.98, bf16[1024,4,128]{0,2,1:T(8,128)(2,1)} %bitcast.509, bf16[1024,128]{0,1:T(8,128)(2,1)S(1)} %copy-done.90), kind=kOutput, calls=%fused_computation.3 | convolution fusion | flops 1086320640 | bytes 34897920 | tf_op jit(solution)/shard_map/qhd,kd->hqk/dot_general | solution.py:533
  599.0 8.0 %fusion.3 = bf16[4,1024,1024]{1,2,0:T(8,128)(2,1)S(1)} fusion(f32[1024,1024,4]{1,0,2:T(8,128)} %get-tuple-element.311, f32[4,1024]{1,0:T(4,128)S(1)} %get-tuple-element.310, f32[4,1024,1024]{1,2,0:T(8,128)S(1)} %bitcast.432, f32[4,1024]{1,0:T(4,128)S(1)} %copy-done.98), kind=kLoop, calls=%fused_computation.5 | loop fusion | flops 16777216 | bytes 41975808 | tf_op jit(solution)/shard_map/convert_element_type | solution.py:535
  644.6 11.6 %collective-permute-done.76 = bf16[128,2048]{1,0:T(8,128)(2,1)S(1)} collective-permute-done((bf16[128,2048]{1,0:T(8,128)(2,1)}, bf16[128,2048]{1,0:T(8,128)(2,1)S(1)}, u32[]{:S(2)}, u32[]{:S(2)}) %collective-permute-start.76) | collective-permute-done | bytes 524320 | tf_op jit(solution)/shard_map/ppermute | solution.py:86
  694.8 7.8 %collective-permute-start.90 = (bf16[128,2048]{1,0:T(8,128)(2,1)}, bf16[128,2048]{1,0:T(8,128)(2,1)}, u32[]{:S(2)}, u32[]{:S(2)}) collective-permute-start(bf16[128,2048]{1,0:T(8,128)(2,1)} %fusion.90), channel_id=1, source_target_pairs={{0,0},{4,1},{8,2},{12,3},{20,4},{24,5},{28,6},{16,7},{9,8},{13,9},... | collective-permute-start | bytes 1572872 | tf_op jit(solution)/shard_map/ppermute | solution.py:573
  718.3 35.3 %all-to-all-done.2 = f32[32,10,128]{2,1,0:T(8,128)S(1)} async-done(((f32[32,10,128]{2,1,0:T(8,128)}), f32[32,10,128]{2,1,0:T(8,128)S(1)}, u32[]{:S(2)}, u32[]{:S(2)}) %all-to-all-start.2) | async-done | bytes 163872 | tf_op jit(solution)/shard_map/all_to_all | solution.py:104
  (708 shorter events, 417.9 us)
Async XLA Ops:
  16.1 66.2 %collective-permute-start.11 = (bf16[1,1024,1536]{2,1,0:T(8,128)(2,1)}, bf16[1,1024,1536]{2,1,0:T(8,128)(2,1)}, u32[]{:S(2)}, u32[]{:S(2)}) collective-permute-start(bf16[1,1024,1536]{2,1,0:T(8,128)(2,1)} %param.23), channel_id=1, source_target_pairs={{0,16},{16,0},{1,17},{17,1},{2,18},{18,2},{3,19},{19,3},{4,20},{20... | collective-permute-start | bytes 9437192 | tf_op jit(solution)/shard_map/ppermute | solution.py:73
  16.2 31.6 %collective-permute-start.12 = (bf16[1,768,1024]{2,1,0:T(8,128)(2,1)}, bf16[1,768,1024]{2,1,0:T(8,128)(2,1)}, u32[]{:S(2)}, u32[]{:S(2)}) collective-permute-start(bf16[1,768,1024]{2,1,0:T(8,128)(2,1)} %param.24), channel_id=1, source_target_pairs={{0,16},{16,0},{1,17},{17,1},{2,18},{18,2},{3,19},{19,3},{4,20},{20... | collective-permute-start | bytes 4718600 | tf_op jit(solution)/shard_map/ppermute | solution.py:73
  27.8 31.9 %all-to-all-start.1 = ((bf16[32,10,128]{2,1,0:T(8,128)(2,1)}), bf16[32,10,128]{2,1,0:T(8,128)(2,1)S(1)}, u32[]{:S(2)}, u32[]{:S(2)}) async-start(bf16[32,10,128]{2,1,0:T(8,128)(2,1)} %broadcast_in_dim.202), calls=%async_computation.1 | async-start | bytes 262144 | tf_op jit(solution)/shard_map/all_to_all | solution.py:100
  71.9 24.0 %collective-permute-start.15 = (bf16[1,512,2048]{2,1,0:T(8,128)(2,1)S(1)}, bf16[1,512,2048]{2,1,0:T(8,128)(2,1)S(1)}, u32[]{:S(2)}, u32[]{:S(2)}) collective-permute-start(bf16[1,512,2048]{2,1,0:T(8,128)(2,1)S(1)} %bitcast.437), channel_id=1, source_target_pairs={{0,16},{16,0},{1,17},{17,1},{2,18},{18,2},{3,19},{19,3},{4,20},{20... | collective-permute-start | bytes 6291464 | tf_op jit(solution)/shard_map/ppermute | solution.py:73
  77.6 36.9 %collective-permute-start.17 = (bf16[128,2048]{1,0:T(8,128)(2,1)}, bf16[128,2048]{1,0:T(8,128)(2,1)}, u32[]{:S(2)}, u32[]{:S(2)}) collective-permute-start(bf16[128,2048]{1,0:T(8,128)(2,1)} %param.20), channel_id=1, source_target_pairs={{0,0},{1,4},{2,8},{3,12},{4,20},{5,24},{6,28},{7,16},{8,9},{9,13},... | collective-permute-start | bytes 1572872 | tf_op jit(solution)/shard_map/ppermute | solution.py:368
  201.2 28.2 %collective-permute-start.27 = (bf16[128,4224]{1,0:T(8,128)(2,1)S(1)}, bf16[128,4224]{1,0:T(8,128)(2,1)S(1)}, u32[]{:S(2)}, u32[]{:S(2)}) collective-permute-start(bf16[128,4224]{1,0:T(8,128)(2,1)S(1)} %pad_maximum_fusion.15), channel_id=1, source_target_pairs={{0,4},{4,8},{8,12},{12,0},{1,5},{5,9},{9,13},{13,1},{2,6},{6,10},{... | collective-permute-start | bytes 3244040 | tf_op jit(solution)/shard_map/ppermute | solution.py:86
  242.6 25.9 %collective-permute-start.40 = (bf16[128,4224]{1,0:T(8,128)(2,1)S(1)}, bf16[128,4224]{1,0:T(8,128)(2,1)}, u32[]{:S(2)}, u32[]{:S(2)}) collective-permute-start(bf16[128,4224]{1,0:T(8,128)(2,1)S(1)} %collective-permute-done.27), channel_id=1, source_target_pairs={{0,4},{4,8},{8,12},{12,0},{1,5},{5,9},{9,13},{13,1},{2,6},{6,10},{... | collective-permute-start | bytes 3244040 | tf_op jit(solution)/shard_map/ppermute | solution.py:86
  244.1 26.0 %collective-permute-start.35 = (bf16[64,4224]{1,0:T(8,128)(2,1)S(1)}, bf16[64,4224]{1,0:T(8,128)(2,1)S(1)}, u32[]{:S(2)}, u32[]{:S(2)}) collective-permute-start(bf16[64,4224]{1,0:T(8,128)(2,1)S(1)} %get-tuple-element.260.refs_0_), channel_id=1, source_target_pairs={{0,2},{1,3},{2,0},{3,1},{4,6},{5,7},{6,4},{7,5},{8,10},{9,11},{10,... | collective-permute-start | bytes 1622024 | tf_op jit(solution)/shard_map/ppermute | solution.py:73
  245.3 25.9 %collective-permute-start.37 = (bf16[64,4224]{1,0:T(8,128)(2,1)S(1)}, bf16[64,4224]{1,0:T(8,128)(2,1)S(1)}, u32[]{:S(2)}, u32[]{:S(2)}) collective-permute-start(bf16[64,4224]{1,0:T(8,128)(2,1)S(1)} %get-tuple-element.259.refs_4_), channel_id=1, source_target_pairs={{0,2},{1,3},{2,0},{3,1},{4,6},{5,7},{6,4},{7,5},{8,10},{9,11},{10,... | collective-permute-start | bytes 1622024 | tf_op jit(solution)/shard_map/ppermute | solution.py:73
  245.6 27.3 %collective-permute-start.38 = (bf16[64,4224]{1,0:T(8,128)(2,1)S(1)}, bf16[64,4224]{1,0:T(8,128)(2,1)}, u32[]{:S(2)}, u32[]{:S(2)}) collective-permute-start(bf16[64,4224]{1,0:T(8,128)(2,1)S(1)} %get-tuple-element.259.refs_4_), channel_id=1, source_target_pairs={{0,1},{1,0},{2,3},{3,2},{4,5},{5,4},{6,7},{7,6},{8,9},{9,8},{10,11... | collective-permute-start | bytes 1622024 | tf_op jit(solution)/shard_map/ppermute | solution.py:73
  268.5 25.4 %collective-permute-start.47 = (bf16[128,4224]{1,0:T(8,128)(2,1)}, bf16[128,4224]{1,0:T(8,128)(2,1)}, u32[]{:S(2)}, u32[]{:S(2)}) collective-permute-start(bf16[128,4224]{1,0:T(8,128)(2,1)} %collective-permute-done.40), channel_id=1, source_target_pairs={{0,4},{4,8},{8,12},{12,0},{1,5},{5,9},{9,13},{13,1},{2,6},{6,10},{... | collective-permute-start | bytes 3244040 | tf_op jit(solution)/shard_map/ppermute | solution.py:86
  296.4 52.2 %collective-permute-start.48 = (bf16[64,4224]{1,0:T(8,128)(2,1)S(1)}, bf16[64,4224]{1,0:T(8,128)(2,1)S(1)}, u32[]{:S(2)}, u32[]{:S(2)}) collective-permute-start(bf16[64,4224]{1,0:T(8,128)(2,1)S(1)} %get-tuple-element.256.refs_0_), channel_id=1, source_target_pairs={{0,1},{1,0},{2,3},{3,2},{4,5},{5,4},{6,7},{7,6},{8,9},{9,8},{10,11... | collective-permute-start | bytes 1622024 | tf_op jit(solution)/shard_map/ppermute | solution.py:73
  302.6 59.0 %collective-permute-start.49 = (bf16[64,4224]{1,0:T(8,128)(2,1)S(1)}, bf16[64,4224]{1,0:T(8,128)(2,1)S(1)}, u32[]{:S(2)}, u32[]{:S(2)}) collective-permute-start(bf16[64,4224]{1,0:T(8,128)(2,1)S(1)} %get-tuple-element.256.refs_0_), channel_id=1, source_target_pairs={{0,2},{1,3},{2,0},{3,1},{4,6},{5,7},{6,4},{7,5},{8,10},{9,11},{10,... | collective-permute-start | bytes 1622024 | tf_op jit(solution)/shard_map/ppermute | solution.py:73
  304.9 44.4 %collective-permute-start.51 = (bf16[64,4224]{1,0:T(8,128)(2,1)S(1)}, bf16[64,4224]{1,0:T(8,128)(2,1)}, u32[]{:S(2)}, u32[]{:S(2)}) collective-permute-start(bf16[64,4224]{1,0:T(8,128)(2,1)S(1)} %get-tuple-element.255.refs_4_), channel_id=1, source_target_pairs={{0,2},{1,3},{2,0},{3,1},{4,6},{5,7},{6,4},{7,5},{8,10},{9,11},{10,... | collective-permute-start | bytes 1622024 | tf_op jit(solution)/shard_map/ppermute | solution.py:73
  314.2 47.8 %collective-permute-start.52 = (bf16[64,4224]{1,0:T(8,128)(2,1)S(1)}, bf16[64,4224]{1,0:T(8,128)(2,1)}, u32[]{:S(2)}, u32[]{:S(2)}) collective-permute-start(bf16[64,4224]{1,0:T(8,128)(2,1)S(1)} %get-tuple-element.255.refs_4_), channel_id=1, source_target_pairs={{0,1},{1,0},{2,3},{3,2},{4,5},{5,4},{6,7},{7,6},{8,9},{9,8},{10,11... | collective-permute-start | bytes 1622024 | tf_op jit(solution)/shard_map/ppermute | solution.py:73
  354.7 49.3 %collective-permute-start.54 = (bf16[2,2,64,4224]{3,2,0,1:T(8,128)(2,1)}, bf16[2,2,64,4224]{3,2,0,1:T(8,128)(2,1)}, u32[]{:S(2)}, u32[]{:S(2)}) collective-permute-start(bf16[2,2,64,4224]{3,2,0,1:T(8,128)(2,1)} %bitcast.411), channel_id=1, source_target_pairs={{0,2},{1,3},{2,0},{3,1},{4,6},{5,7},{6,4},{7,5},{8,10},{9,11},{10,... | collective-permute-start | bytes 6488072 | tf_op jit(solution)/shard_map/ppermute | solution.py:73
  361.6 43.6 %collective-permute-start.55 = (bf16[2,2,64,4224]{3,2,0,1:T(8,128)(2,1)}, bf16[2,2,64,4224]{3,2,0,1:T(8,128)(2,1)}, u32[]{:S(2)}, u32[]{:S(2)}) collective-permute-start(bf16[2,2,64,4224]{3,2,0,1:T(8,128)(2,1)} %bitcast.410), channel_id=1, source_target_pairs={{0,1},{1,0},{2,3},{3,2},{4,5},{5,4},{6,7},{7,6},{8,9},{9,8},{10,11... | collective-permute-start | bytes 6488072 | tf_op jit(solution)/shard_map/ppermute | solution.py:73
  445.2 41.2 %collective-permute-start.58 = (bf16[2,2,64,4224]{3,2,0,1:T(8,128)(2,1)S(1)}, bf16[2,2,64,4224]{3,2,0,1:T(8,128)(2,1)S(1)}, u32[]{:S(2)}, u32[]{:S(2)}) collective-permute-start(bf16[2,2,64,4224]{3,2,0,1:T(8,128)(2,1)S(1)} %bitcast.479), channel_id=1, source_target_pairs={{0,2},{1,3},{2,0},{3,1},{4,6},{5,7},{6,4},{7,5},{8,10},{9,11},{10,... | collective-permute-start | bytes 6488072 | tf_op jit(solution)/shard_map/ppermute | solution.py:73
  445.4 41.0 %collective-permute-start.59 = (bf16[2,2,64,4224]{3,2,0,1:T(8,128)(2,1)S(1)}, bf16[2,2,64,4224]{3,2,0,1:T(8,128)(2,1)S(1)}, u32[]{:S(2)}, u32[]{:S(2)}) collective-permute-start(bf16[2,2,64,4224]{3,2,0,1:T(8,128)(2,1)S(1)} %bitcast.480), channel_id=1, source_target_pairs={{0,1},{1,0},{2,3},{3,2},{4,5},{5,4},{6,7},{7,6},{8,9},{9,8},{10,11... | collective-permute-start | bytes 6488072 | tf_op jit(solution)/shard_map/ppermute | solution.py:73
  446.2 24.3 %collective-permute-start.62 = (bf16[128,4224]{1,0:T(8,128)(2,1)S(1)}, bf16[128,4224]{1,0:T(8,128)(2,1)S(1)}, u32[]{:S(2)}, u32[]{:S(2)}) collective-permute-start(bf16[128,4224]{1,0:T(8,128)(2,1)S(1)} %bitcast.484), channel_id=1, source_target_pairs={{0,4},{4,8},{8,12},{12,0},{1,5},{5,9},{9,13},{13,1},{2,6},{6,10},{... | collective-permute-start | bytes 3244040 | tf_op jit(solution)/shard_map/ppermute | solution.py:86
  470.7 38.8 %collective-permute-start.63 = (bf16[128,4224]{1,0:T(8,128)(2,1)S(1)}, bf16[128,4224]{1,0:T(8,128)(2,1)S(1)}, u32[]{:S(2)}, u32[]{:S(2)}) collective-permute-start(bf16[128,4224]{1,0:T(8,128)(2,1)S(1)} %fusion.48), channel_id=1, source_target_pairs={{0,4},{4,8},{8,12},{12,0},{1,5},{5,9},{9,13},{13,1},{2,6},{6,10},{... | collective-permute-start | bytes 3244040 | tf_op jit(solution)/shard_map/ppermute | solution.py:86
  547.7 25.8 %collective-permute-start.71 = (bf16[1,512,2048]{2,1,0:T(8,128)(2,1)}, bf16[1,512,2048]{2,1,0:T(8,128)(2,1)}, u32[]{:S(2)}, u32[]{:S(2)}) collective-permute-start(bf16[1,512,2048]{2,1,0:T(8,128)(2,1)} %bitcast.89), channel_id=1, source_target_pairs={{0,16},{16,0},{1,17},{17,1},{2,18},{18,2},{3,19},{19,3},{4,20},{20... | collective-permute-start | bytes 6291464 | tf_op jit(solution)/shard_map/ppermute | solution.py:73
  619.1 37.0 %collective-permute-start.76 = (bf16[128,2048]{1,0:T(8,128)(2,1)}, bf16[128,2048]{1,0:T(8,128)(2,1)S(1)}, u32[]{:S(2)}, u32[]{:S(2)}) collective-permute-start(bf16[128,2048]{1,0:T(8,128)(2,1)} %get-tuple-element.226), channel_id=1, source_target_pairs={{0,8},{4,12},{8,0},{12,4},{1,9},{5,13},{9,1},{13,5},{2,10},{6,14},... | collective-permute-start | bytes 1572872 | tf_op jit(solution)/shard_map/ppermute | solution.py:86
  621.2 34.9 %collective-permute-start.77 = (bf16[128,2048]{1,0:T(8,128)(2,1)}, bf16[128,2048]{1,0:T(8,128)(2,1)S(1)}, u32[]{:S(2)}, u32[]{:S(2)}) collective-permute-start(bf16[128,2048]{1,0:T(8,128)(2,1)} %get-tuple-element.225), channel_id=1, source_target_pairs={{0,4},{4,8},{8,12},{12,0},{1,5},{5,9},{9,13},{13,1},{2,6},{6,10},{... | collective-permute-start | bytes 1572872 | tf_op jit(solution)/shard_map/ppermute | solution.py:86
  660.3 46.2 %collective-permute-start.83 = (bf16[1280,256]{1,0:T(8,128)(2,1)S(1)}, bf16[1280,256]{1,0:T(8,128)(2,1)S(1)}, u32[]{:S(2)}, u32[]{:S(2)}) collective-permute-start(bf16[1280,256]{1,0:T(8,128)(2,1)S(1)} %pad_maximum_fusion.19), channel_id=1, source_target_pairs={{0,12},{4,0},{8,4},{12,8},{1,13},{5,1},{9,5},{13,9},{2,14},{6,2},{... | collective-permute-start | bytes 1966088 | tf_op jit(solution)/shard_map/ppermute | solution.py:86
  661.8 41.0 %collective-permute-start.84 = (bf16[1024,1536]{1,0:T(8,128)(2,1)S(1)}, bf16[1024,1536]{1,0:T(8,128)(2,1)S(1)}, u32[]{:S(2)}, u32[]{:S(2)}) collective-permute-start(bf16[1024,1536]{1,0:T(8,128)(2,1)S(1)} %copy-done.111), channel_id=1, source_target_pairs={{0,16},{16,0},{1,17},{17,1},{2,18},{18,2},{3,19},{19,3},{4,20},{20... | collective-permute-start | bytes 9437192 | tf_op jit(solution)/shard_map/ppermute | solution.py:73
  671.1 82.5 %collective-permute-start.88 = (bf16[1280,256]{1,0:T(8,128)(2,1)}, bf16[1280,256]{1,0:T(8,128)(2,1)}, u32[]{:S(2)}, u32[]{:S(2)}) collective-permute-start(bf16[1280,256]{1,0:T(8,128)(2,1)} %pad_maximum_fusion.20), channel_id=1, source_target_pairs={{0,8},{4,12},{8,0},{12,4},{1,9},{5,13},{9,1},{13,5},{2,10},{6,14},... | collective-permute-start | bytes 1966088 | tf_op jit(solution)/shard_map/ppermute | solution.py:86
  681.0 72.6 %collective-permute-start.89 = (bf16[1280,256]{1,0:T(8,128)(2,1)}, bf16[1280,256]{1,0:T(8,128)(2,1)}, u32[]{:S(2)}, u32[]{:S(2)}) collective-permute-start(bf16[1280,256]{1,0:T(8,128)(2,1)} %pad_maximum_fusion.21), channel_id=1, source_target_pairs={{0,4},{4,8},{8,12},{12,0},{1,5},{5,9},{9,13},{13,1},{2,6},{6,10},{... | collective-permute-start | bytes 1966088 | tf_op jit(solution)/shard_map/ppermute | solution.py:86
  694.8 60.8 %collective-permute-start.90 = (bf16[128,2048]{1,0:T(8,128)(2,1)}, bf16[128,2048]{1,0:T(8,128)(2,1)}, u32[]{:S(2)}, u32[]{:S(2)}) collective-permute-start(bf16[128,2048]{1,0:T(8,128)(2,1)} %fusion.90), channel_id=1, source_target_pairs={{0,0},{4,1},{8,2},{12,3},{20,4},{24,5},{28,6},{16,7},{9,8},{13,9},... | collective-permute-start | bytes 1572872 | tf_op jit(solution)/shard_map/ppermute | solution.py:573
  709.4 44.2 %all-to-all-start.2 = ((f32[32,10,128]{2,1,0:T(8,128)}), f32[32,10,128]{2,1,0:T(8,128)S(1)}, u32[]{:S(2)}, u32[]{:S(2)}) async-start(f32[32,10,128]{2,1,0:T(8,128)} %reshape.787), calls=%async_computation.2 | async-start | bytes 524288 | tf_op jit(solution)/shard_map/all_to_all | solution.py:104
  712.6 48.6 %collective-permute-start.86 = (bf16[64,2048]{1,0:T(8,128)(2,1)S(1)}, bf16[64,2048]{1,0:T(8,128)(2,1)S(1)}, u32[]{:S(2)}, u32[]{:S(2)}) collective-permute-start(bf16[64,2048]{1,0:T(8,128)(2,1)S(1)} %get-tuple-element.268), channel_id=1, source_target_pairs={{0,0},{4,4},{16,8},{20,12},{8,16},{12,20},{24,24},{28,28},{1,1},{5... | collective-permute-start | bytes 786440 | tf_op jit(solution)/shard_map/ppermute | solution.py:181
  717.1 44.0 %collective-permute-start.87 = (bf16[64,2048]{1,0:T(8,128)(2,1)S(1)}, bf16[64,2048]{1,0:T(8,128)(2,1)S(1)}, u32[]{:S(2)}, u32[]{:S(2)}) collective-permute-start(bf16[64,2048]{1,0:T(8,128)(2,1)S(1)} %get-tuple-element.267), channel_id=1, source_target_pairs={{4,0},{0,4},{20,8},{16,12},{12,16},{8,20},{28,24},{24,28},{5,1},{1... | collective-permute-start | bytes 786440 | tf_op jit(solution)/shard_map/ppermute | solution.py:181
  (198 other events, 2489.6 us)
